TPU v7x, 512 devices: a whole 4x8x8 slice. The times are simulated.
512 devices in a mesh: ch: 16 (over x_lo, y), row: 32 (over z, x_hi, core).
Axes of the slice: x: 4 (x_hi: 2, x_lo: 2; x = x_hi * 2 + x_lo), y: 8, z: 8, core: 2. Of those that a mesh axis runs over, the one named last changes fastest.
Arguments:
- latent: bfloat16 [512, 32, 1280], P('row', None, 'ch'), may hold values from -50 to 50
- timestep: int32 [16], replicated, may hold values from 0 to 999
- norm_gain_a: float32 [1280], P('ch'), may hold values from 0.1 to 1.9
- conv_weight_a: bfloat16 [1280, 3, 3, 1280], P('ch'), may hold values from -0.0546875 to 0.0546875
- time_weight: bfloat16 [320, 1280], P(None, 'ch'), may hold values from -0.3125 to 0.3125
- norm_gain_b: float32 [1280], P('ch'), may hold values from 0.1 to 1.9
- conv_weight_b: bfloat16 [1280, 3, 3, 1280], P('ch'), may hold values from -0.0546875 to 0.0546875
- norm_gain_c: float32 [1280], P('ch'), may hold values from 0.1 to 1.9
- w_query: bfloat16 [1024, 1280], P('ch'), may hold values from -4 to 4
- w_key: bfloat16 [1024, 1280], P('ch'), may hold values from -4 to 4
- w_value: bfloat16 [1024, 1280], P('ch'), may hold values from -0.3125 to 0.3125
- w_out: bfloat16 [1280, 1024], P('ch'), may hold values from -0.1875 to 0.1875
Outputs:
- result: bfloat16 [512, 32, 1280], P('row', None, 'ch')
All inputs are finite; a program needn't handle non-finite values.
Results may differ from a plain program's by a relative error of at most 0.017.
Values may be sent and summed in bfloat16 or wider, within the bound.
No kernel may reach another device: no remote copies, remote signals or barrier semaphores. Data moves between devices by JAX's collectives and lax.ppermute only.
A program may use at most 64 MiB of HBM per device.

v0:
```python
import math

import jax
import jax.numpy as jnp
from jax import lax
from jax.sharding import PartitionSpec as P

C = 1280
GROUPS = 32
HEAD_DIM = 64
TDIM = 320
H = 32


eps_value = 1e-06


def swapped(value, axis, stride):
    mask = 2**stride
    pairs = [(source, source ^ mask) for source in range(lax.axis_size(axis))]
    return lax.ppermute(value, axis, pairs)


def copy_for_each(array, axis):
    peers = lax.axis_size(axis)
    return lax.all_to_all(
        jnp.broadcast_to(array[None], (peers, *array.shape)), axis, 0, 0, tiled=True
    )


def in_order(pieces, dim):
    lengths = list(pieces.shape[1:])
    lengths[dim] *= pieces.shape[0]
    return jnp.moveaxis(pieces, 0, dim).reshape(lengths)


def collect(array, axis, dim):
    pieces = copy_for_each(array, axis)
    return in_order(pieces, dim)


def right_product(left, weight):
    return lax.dot_general(
        left, weight, (((1,), (1,)), ((), ())), preferred_element_type=jnp.float32
    )


def conv_taps(padded, weight):
    outcome = lax.conv_general_dilated(
        padded[None],
        weight,
        (1, 1),
        "VALID",
        dimension_numbers=("NHWC", "OHWI", "NHWC"),
        preferred_element_type=jnp.float32,
    )
    return outcome[0]


def pad_columns(field):
    return jnp.pad(field, ((0, 0), (1, 1), (0, 0)))


def body(
    latent,
    timestep,
    norm_gain_a,
    conv_weight_a,
    time_weight,
    norm_gain_b,
    conv_weight_b,
    norm_gain_c,
    w_query,
    w_key,
    w_value,
    w_out,
):
    rows, width, local_ch = latent.shape
    span = H // rows
    place = lax.axis_index("row")
    within = place % span
    image_id = place // span
    group_width = C // GROUPS
    local_groups = local_ch // group_width
    members = float(H * width * group_width)
    tokens = rows * width

    def group_norm(value, gain):
        flat = value.reshape(tokens, local_groups, group_width)
        stats = jnp.stack([jnp.sum(flat, axis=(0, 2)), jnp.sum(flat * flat, axis=(0, 2))])
        stats = stats + swapped(stats, "row", 0)
        mean = stats[0] / members
        spread = stats[1] / members - mean * mean
        scaled = (flat - mean[None, :, None]) * lax.rsqrt(spread + eps_value)[None, :, None]
        return scaled.reshape(rows, width, local_ch) * gain

    upper_half = within == 0

    def facing_row(field):
        return jnp.where(upper_half, field[-1:], field[:1])

    def attach_rim(field, partner):
        empty_row = jnp.zeros_like(partner)
        above = jnp.where(upper_half, empty_row, partner)
        below = jnp.where(upper_half, partner, empty_row)
        return jnp.concatenate([above, field, below], axis=0)

    def convolve(active, weight):
        full = collect(active, "ch", 2)
        partner = swapped(facing_row(full), "row", 0)
        rimmed = attach_rim(full, partner)
        result_conv = conv_taps(pad_columns(rimmed), weight)
        return result_conv

    image_ids = jnp.arange(timestep.shape[0])
    step_value = jnp.sum(jnp.where(image_ids == image_id, timestep, 0)).astype(jnp.float32)
    half = TDIM // 2
    freqs = jnp.exp(-math.log(10000.0) * jnp.arange(half, dtype=jnp.float32) / half)
    angles = step_value * freqs
    sinus = jnp.concatenate([jnp.cos(angles), jnp.sin(angles)])[None, :].astype(jnp.bfloat16)
    time_add = jax.nn.silu(jnp.dot(sinus, time_weight, preferred_element_type=jnp.float32))
    source = latent.astype(jnp.float32)
    active_a = jax.nn.silu(group_norm(source, norm_gain_a)).astype(jnp.bfloat16)
    hidden_a = convolve(active_a, conv_weight_a) + time_add[None]
    active_b = jax.nn.silu(group_norm(hidden_a, norm_gain_b)).astype(jnp.bfloat16)
    hidden_b = source + convolve(active_b, conv_weight_b)
    normed = group_norm(hidden_b, norm_gain_c).astype(jnp.bfloat16).reshape(tokens, local_ch)
    inner = w_query.shape[0]
    projections = jnp.concatenate([w_query, w_key, w_value], axis=0)
    weight_cols = projections
    mixed = right_product(collect(normed, "ch", 1), weight_cols)
    query = mixed[:, :inner].astype(jnp.bfloat16)
    keyed = mixed[:, inner : 2 * inner].astype(jnp.bfloat16)
    valued = mixed[:, 2 * inner :].astype(jnp.bfloat16)
    key_value = jnp.stack([keyed, valued])
    key_value = jnp.concatenate([key_value, swapped(key_value, "row", 0)], axis=1)
    local_heads = inner // HEAD_DIM
    query_heads = query.reshape(tokens, local_heads, HEAD_DIM)
    key_heads = key_value[0].reshape(-1, local_heads, HEAD_DIM)
    value_heads = key_value[1].reshape(-1, local_heads, HEAD_DIM)
    scores = jnp.einsum(
        "qhd,khd->hqk", query_heads, key_heads, preferred_element_type=jnp.float32
    ) * (1.0 / math.sqrt(HEAD_DIM))
    highest = jnp.max(scores, axis=-1, keepdims=True)
    raised = jnp.exp(scores - highest)
    weights = (raised / jnp.sum(raised, axis=-1, keepdims=True)).astype(jnp.bfloat16)
    heads_out = jnp.einsum("hqk,khd->qhd", weights, value_heads, preferred_element_type=jnp.float32)
    heads_out = heads_out.astype(jnp.bfloat16).reshape(tokens, inner)
    weight_cols = w_out
    projected = right_product(collect(heads_out, "ch", 1), weight_cols)
    total = hidden_b.reshape(tokens, local_ch) + projected
    return total.reshape(rows, width, local_ch).astype(jnp.bfloat16)


def solution(mesh):
    return jax.shard_map(
        body,
        mesh=mesh,
        in_specs=(
            P("row", None, "ch"),
            P(),
            P("ch"),
            P("ch", None, None, None),
            P(None, "ch"),
            P("ch"),
            P("ch", None, None, None),
            P("ch"),
            P("ch", None),
            P("ch", None),
            P("ch", None),
            P("ch", None),
        ),
        out_specs=P("row", None, "ch"),
        check_vma=False,
    )
```

profile of v0, /device:TPU:1, one launch (start us, length us, event | category | flops | bytes accessed | tf_op | source)
XLA Modules:
  0.0 245.2 jit_solution(4317104241846614965)
XLA Ops:
  0.0 1.1 convert_reduce_fusion
  1.5 8.7 %collective-permute-start = (f32[2,2]{1,0:T(2,128)S(1)}, f32[2,2]{1,0:T(2,128)S(1)}, u32[]{:S(2)}, u32[]{:S(2)}) collective-permute-start(f32[2,2]{1,0:T(2,128)S(1)} %pad_maximum_fusion.2), channel_id=1, source_target_pairs={{0,1},{1,0},{2,3},{3,2},{4,5},{5,4},{6,7},{7,6},{8,9},{9,8},{10,11... | collective-permute-start | bytes 56 | tf_op jit(solution)/shard_map/ppermute | solution.py:21
  10.3 0.8 collective-permute-done
  11.4 1.0 fusion.47
  12.5 1.7 broadcast_in_dim.22
  14.2 4.6 %all-to-all-start = ((bf16[16,16,32,80]{3,2,1,0:T(8,128)(2,1)}), bf16[16,16,32,80]{3,2,1,0:T(8,128)(2,1)}, u32[]{:S(2)}, u32[]{:S(2)}) async-start(bf16[16,16,32,80]{3,2,1,0:T(8,128)(2,1)} %broadcast_in_dim.22), calls=%async_computation | async-start | bytes 4194304 | tf_op jit(solution)/shard_map/all_to_all | solution.py:26
  20.2 46.8 %all-to-all-done = bf16[16,16,32,80]{3,2,1,0:T(8,128)(2,1)} async-done(((bf16[16,16,32,80]{3,2,1,0:T(8,128)(2,1)}), bf16[16,16,32,80]{3,2,1,0:T(8,128)(2,1)}, u32[]{:S(2)}, u32[]{:S(2)}) %all-to-all-start) | async-done | bytes 1310752 | tf_op jit(solution)/shard_map/all_to_all | solution.py:26
  67.1 1.0 slice_select_fusion.1
  68.3 3.1 %collective-permute-start.1 = (bf16[1,32,1280]{2,1,0:T(8,128)(2,1)S(1)}, bf16[1,32,1280]{2,1,0:T(8,128)(2,1)S(1)}, u32[]{:S(2)}, u32[]{:S(2)}) collective-permute-start(bf16[1,32,1280]{2,1,0:T(8,128)(2,1)S(1)} %select_n.71), channel_id=1, source_target_pairs={{0,1},{1,0},{2,3},{3,2},{4,5},{5,4},{6,7},{7,6},{8,9},{9,8},{10,11... | collective-permute-start | bytes 245768 | tf_op jit(solution)/shard_map/ppermute | solution.py:21
  71.6 4.3 %copy.73 = bf16[16,32,16,80]{3,2,1,0:T(8,128)(2,1)} copy(bf16[16,32,16,80]{3,1,0,2:T(8,128)(2,1)} %bitcast.4) | data formatting | bytes 2621440 | tf_op jit(solution)/shard_map/transpose | solution.py:34
  75.8 3.7 %reshape.209 = bf16[16,32,1280]{2,1,0:T(8,128)(2,1)S(1)} reshape(bf16[16,32,16,80]{3,2,1,0:T(8,128)(2,1)} %copy.73) | data formatting | bytes 2621440 | tf_op jit(solution)/shard_map/reshape | solution.py:34
  81.5 4.0 %select_reduce_fusion.1 = (f32[80]{0:T(128)S(1)}, f32[80]{0:T(128)S(1)}, f32[16,8,5,80]{3,1,2,0:T(8,128)S(1)}) fusion(pred[8,5]{0,1:T(8,128)(4,1)S(1)} %copy-done.11, f32[80]{0:T(128)S(1)} %divide_multiply_fusion, bf16[80,3,3,1280]{3,0,2,1:T(8,128)(2,1)S(1)} %copy-done, bf16[18,1,7,2,1280]{4,2,3,0,1:T(8,128)(2,1)S(1)} %slice.73, ...), kind=kOutput, calls=%fused_computation.51 | convolution fusion | flops 1187747584 | bytes 4537320 | tf_op jit(solution)/shard_map/conv_general_dilated | solution.py:49
  85.9 1.9 collective-permute-start.2
  87.8 1.1 collective-permute-done.2
  89.9 54.1 %all_to_all.20 = bf16[16,16,32,80]{3,2,1,0:T(8,128)(2,1)S(1)} all-to-all(bf16[16,16,32,80]{3,2,1,0:T(8,128)(2,1)S(1)} %broadcast_in_dim.26), channel_id=1, replica_groups=mesh['ch'=16,'row'=32] {'ch'}, dimensions={0} | all-to-all | bytes 2621440 | tf_op jit(solution)/shard_map/all_to_all | solution.py:26
  144.0 1.3 copy-done.1
  145.6 4.7 %collective-permute-start.3 = (bf16[1,32,1280]{2,1,0:T(8,128)(2,1)S(1)}, bf16[1,32,1280]{2,1,0:T(8,128)(2,1)S(1)}, u32[]{:S(2)}, u32[]{:S(2)}) collective-permute-start(bf16[1,32,1280]{2,1,0:T(8,128)(2,1)S(1)} %select_n.77), channel_id=1, source_target_pairs={{0,1},{1,0},{2,3},{3,2},{4,5},{5,4},{6,7},{7,6},{8,9},{9,8},{10,11... | collective-permute-start | bytes 245768 | tf_op jit(solution)/shard_map/ppermute | solution.py:21
  150.3 4.2 %copy.80 = bf16[16,32,16,80]{3,2,1,0:T(8,128)(2,1)} copy(bf16[16,32,16,80]{3,1,0,2:T(8,128)(2,1)} %bitcast.116) | data formatting | bytes 2621440 | tf_op jit(solution)/shard_map/transpose | solution.py:34
  154.5 3.7 %reshape.210 = bf16[16,32,1280]{2,1,0:T(8,128)(2,1)S(1)} reshape(bf16[16,32,16,80]{3,2,1,0:T(8,128)(2,1)} %copy.80) | data formatting | bytes 2621440 | tf_op jit(solution)/shard_map/reshape | solution.py:34
  160.0 1.0 copy-done.5
  161.0 4.0 %fusion.23 = f32[16,8,5,80]{3,1,2,0:T(8,128)S(1)} fusion(bf16[80,3,3,1280]{3,0,2,1:T(8,128)(2,1)S(1)} %copy-done.5, bf16[18,1,7,2,1280]{4,2,3,0,1:T(8,128)(2,1)S(1)} %slice.77, bf16[18,1,8,5,1280]{4,2,3,0,1:T(8,128)(2,1)S(1)} %copy.83, pred[8,5]{0,1:T(8,128)(4,1)S(1)} %copy-done.11), kind=kOutput, calls=%fused_computation.32 | convolution fusion | flops 1187440640 | bytes 4536360 | tf_op jit(solution)/shard_map/conv_general_dilated | solution.py:49
  165.6 1.9 collective-permute-start.4
  167.5 1.1 collective-permute-done.4
  169.4 35.8 %all_to_all.21 = bf16[16,512,80]{1,2,0:T(8,128)(2,1)S(1)} all-to-all(bf16[16,512,80]{1,2,0:T(8,128)(2,1)S(1)} %broadcast_in_dim.29), channel_id=1, replica_groups=mesh['ch'=16,'row'=32] {'ch'}, dimensions={0} | all-to-all | bytes 2621440 | tf_op jit(solution)/shard_map/all_to_all | solution.py:26
  205.6 3.9 %collective-permute-start.5 = (bf16[2,512,64]{1,2,0:T(8,128)(2,1)S(1)}, bf16[2,512,64]{1,2,0:T(8,128)(2,1)S(1)}, u32[]{:S(2)}, u32[]{:S(2)}) collective-permute-start(bf16[2,512,64]{1,2,0:T(8,128)(2,1)S(1)} %pad_maximum_fusion.1), channel_id=1, source_target_pairs={{0,1},{1,0},{2,3},{3,2},{4,5},{5,4},{6,7},{7,6},{8,9},{9,8},{10,11... | collective-permute-start | bytes 393224 | tf_op jit(solution)/shard_map/ppermute | solution.py:21
  209.5 1.0 collective-permute-done.5
  211.5 0.7 fusion.33
  212.2 1.1 broadcast_in_dim.60
  213.3 4.4 %all-to-all-start.3 = ((bf16[16,512,64]{1,2,0:T(8,128)(2,1)}), bf16[16,512,64]{1,2,0:T(8,128)(2,1)S(1)}, u32[]{:S(2)}, u32[]{:S(2)}) async-start(bf16[16,512,64]{1,2,0:T(8,128)(2,1)} %broadcast_in_dim.60), calls=%async_computation.3 | async-start | bytes 2097152 | tf_op jit(solution)/shard_map/all_to_all | solution.py:26
  217.9 25.3 %all-to-all-done.3 = bf16[16,512,64]{1,2,0:T(8,128)(2,1)S(1)} async-done(((bf16[16,512,64]{1,2,0:T(8,128)(2,1)}), bf16[16,512,64]{1,2,0:T(8,128)(2,1)S(1)}, u32[]{:S(2)}, u32[]{:S(2)}) %all-to-all-start.3) | async-done | bytes 1048608 | tf_op jit(solution)/shard_map/all_to_all | solution.py:26
  243.2 1.2 fusion.32
  244.4 0.8 copy.89
  (102 shorter events, 10.0 us)
Async XLA Ops:
  0.0 81.3 %copy-start = (bf16[80,3,3,1280]{3,0,2,1:T(8,128)(2,1)S(1)}, bf16[80,3,3,1280]{3,0,2,1:T(8,128)(2,1)}, u32[]{:S(2)}) copy-start(bf16[80,3,3,1280]{3,0,2,1:T(8,128)(2,1)} %param.15) | copy-start | bytes 5529604
  1.5 9.5 %collective-permute-start = (f32[2,2]{1,0:T(2,128)S(1)}, f32[2,2]{1,0:T(2,128)S(1)}, u32[]{:S(2)}, u32[]{:S(2)}) collective-permute-start(f32[2,2]{1,0:T(2,128)S(1)} %pad_maximum_fusion.2), channel_id=1, source_target_pairs={{0,1},{1,0},{2,3},{3,2},{4,5},{5,4},{6,7},{7,6},{8,9},{9,8},{10,11... | collective-permute-start | bytes 56 | tf_op jit(solution)/shard_map/ppermute | solution.py:21
  14.2 4.6 %copy-start.10 = (s32[16]{0:T(128)S(1)}, s32[16]{0:T(128)}, u32[]{:S(2)}) copy-start(s32[16]{0:T(128)} %param.13) | copy-start | bytes 196
  14.2 57.2 %copy-start.9 = (bf16[320,80]{0,1:T(8,128)(2,1)S(1)}, bf16[320,80]{0,1:T(8,128)(2,1)}, u32[]{:S(2)}) copy-start(bf16[320,80]{0,1:T(8,128)(2,1)} %param.16) | copy-start | bytes 153604
  14.2 52.9 %all-to-all-start = ((bf16[16,16,32,80]{3,2,1,0:T(8,128)(2,1)}), bf16[16,16,32,80]{3,2,1,0:T(8,128)(2,1)}, u32[]{:S(2)}, u32[]{:S(2)}) async-start(bf16[16,16,32,80]{3,2,1,0:T(8,128)(2,1)} %broadcast_in_dim.22), calls=%async_computation | async-start | bytes 4194304 | tf_op jit(solution)/shard_map/all_to_all | solution.py:26
  68.3 11.3 %collective-permute-start.1 = (bf16[1,32,1280]{2,1,0:T(8,128)(2,1)S(1)}, bf16[1,32,1280]{2,1,0:T(8,128)(2,1)S(1)}, u32[]{:S(2)}, u32[]{:S(2)}) collective-permute-start(bf16[1,32,1280]{2,1,0:T(8,128)(2,1)S(1)} %select_n.71), channel_id=1, source_target_pairs={{0,1},{1,0},{2,3},{3,2},{4,5},{5,4},{6,7},{7,6},{8,9},{9,8},{10,11... | collective-permute-start | bytes 245768 | tf_op jit(solution)/shard_map/ppermute | solution.py:21
  80.8 0.7 copy-start.11
  81.5 7.8 %copy-start.3 = (f32[80]{0:T(128)S(1)}, f32[80]{0:T(128)}, u32[]{:S(2)}) copy-start(f32[80]{0:T(128)} %param.17) | copy-start | bytes 964
  85.9 3.1 %collective-permute-start.2 = (f32[2,2]{1,0:T(2,128)S(1)}, f32[2,2]{1,0:T(2,128)S(1)}, u32[]{:S(2)}, u32[]{:S(2)}) collective-permute-start(f32[2,2]{1,0:T(2,128)S(1)} %pad_maximum_fusion.4), channel_id=1, source_target_pairs={{0,1},{1,0},{2,3},{3,2},{4,5},{5,4},{6,7},{7,6},{8,9},{9,8},{10,11... | collective-permute-start | bytes 56 | tf_op jit(solution)/shard_map/ppermute | solution.py:21
  144.0 1.4 copy-start.1
  145.6 12.7 %collective-permute-start.3 = (bf16[1,32,1280]{2,1,0:T(8,128)(2,1)S(1)}, bf16[1,32,1280]{2,1,0:T(8,128)(2,1)S(1)}, u32[]{:S(2)}, u32[]{:S(2)}) collective-permute-start(bf16[1,32,1280]{2,1,0:T(8,128)(2,1)S(1)} %select_n.77), channel_id=1, source_target_pairs={{0,1},{1,0},{2,3},{3,2},{4,5},{5,4},{6,7},{7,6},{8,9},{9,8},{10,11... | collective-permute-start | bytes 245768 | tf_op jit(solution)/shard_map/ppermute | solution.py:21
  159.5 1.5 copy-start.5
  161.0 4.1 %copy-start.2 = (bf16[16,32,80]{2,1,0:T(8,128)(2,1)S(1)}, bf16[16,32,80]{2,1,0:T(8,128)(2,1)}, u32[]{:S(2)}) copy-start(bf16[16,32,80]{2,1,0:T(8,128)(2,1)} %param.12) | copy-start | bytes 245764
  161.0 8.0 %copy-start.4 = (f32[80]{0:T(128)S(1)}, f32[80]{0:T(128)}, u32[]{:S(2)}) copy-start(f32[80]{0:T(128)} %param.19) | copy-start | bytes 964
  165.6 3.1 %collective-permute-start.4 = (f32[2,2]{1,0:T(2,128)S(1)}, f32[2,2]{1,0:T(2,128)S(1)}, u32[]{:S(2)}, u32[]{:S(2)}) collective-permute-start(f32[2,2]{1,0:T(2,128)S(1)} %pad_maximum_fusion.5), channel_id=1, source_target_pairs={{0,1},{1,0},{2,3},{3,2},{4,5},{5,4},{6,7},{7,6},{8,9},{9,8},{10,11... | collective-permute-start | bytes 56 | tf_op jit(solution)/shard_map/ppermute | solution.py:21
  169.1 36.1 %copy-start.6 = (bf16[64,1280]{1,0:T(8,128)(2,1)S(1)}, bf16[64,1280]{1,0:T(8,128)(2,1)}, u32[]{:S(2)}) copy-start(bf16[64,1280]{1,0:T(8,128)(2,1)} %param.22) | copy-start | bytes 491524
  169.1 36.0 %copy-start.7 = (bf16[64,1280]{1,0:T(8,128)(2,1)S(1)}, bf16[64,1280]{1,0:T(8,128)(2,1)}, u32[]{:S(2)}) copy-start(bf16[64,1280]{1,0:T(8,128)(2,1)} %param.21) | copy-start | bytes 491524
  169.1 36.0 %copy-start.8 = (bf16[64,1280]{1,0:T(8,128)(2,1)S(1)}, bf16[64,1280]{1,0:T(8,128)(2,1)}, u32[]{:S(2)}) copy-start(bf16[64,1280]{1,0:T(8,128)(2,1)} %param.20) | copy-start | bytes 491524
  205.6 4.8 %collective-permute-start.5 = (bf16[2,512,64]{1,2,0:T(8,128)(2,1)S(1)}, bf16[2,512,64]{1,2,0:T(8,128)(2,1)S(1)}, u32[]{:S(2)}, u32[]{:S(2)}) collective-permute-start(bf16[2,512,64]{1,2,0:T(8,128)(2,1)S(1)} %pad_maximum_fusion.1), channel_id=1, source_target_pairs={{0,1},{1,0},{2,3},{3,2},{4,5},{5,4},{6,7},{7,6},{8,9},{9,8},{10,11... | collective-permute-start | bytes 393224 | tf_op jit(solution)/shard_map/ppermute | solution.py:21
  213.3 29.9 %all-to-all-start.3 = ((bf16[16,512,64]{1,2,0:T(8,128)(2,1)}), bf16[16,512,64]{1,2,0:T(8,128)(2,1)S(1)}, u32[]{:S(2)}, u32[]{:S(2)}) async-start(bf16[16,512,64]{1,2,0:T(8,128)(2,1)} %broadcast_in_dim.60), calls=%async_computation.3 | async-start | bytes 2097152 | tf_op jit(solution)/shard_map/all_to_all | solution.py:26
where the time goes:
time: 247 us; the launch traced here: 245 us
  blocking collectives  89.8 us (36%)
  waiting for transfers between devices  76.1 us (31%)
  starting transfers between devices  33.2 us (13%)
  local copies, waits for them, and re-layouts  27 us (11%)
  matrix products  11 us (4%)
  other arithmetic  6.89 us (3%)
    all_to_all x2, blocking collectives, copy_for_each(): lax.all_to_all(jnp.broadcast_to(array[None], (peers, *array.shape)), axis...  89.8 us
    all_to_all x2, waiting for transfers between devices, copy_for_each(): lax.all_to_all(jnp.broadcast_to(array[None], (peers, *array.shape)), axis...  72.1 us
    ppermute x6, starting transfers between devices, swapped(): return lax.ppermute(value, axis, pairs)  24.3 us
    all_to_all x2, starting transfers between devices, copy_for_each(): lax.all_to_all(jnp.broadcast_to(array[None], (peers, *array.shape)), axis...  8.93 us
    transpose x2, local copies, waits for them, and re-layouts, in_order(): return jnp.moveaxis(pieces, 0, dim).reshape(lengths)  8.5 us
    conv_general_dilated x2, matrix products, conv_taps(): lax.conv_general_dilated(padded[None], weight, (1, 1), 'VALID', dimension...  7.99 us
    reshape x2, local copies, waits for them, and re-layouts, in_order(): return jnp.moveaxis(pieces, 0, dim).reshape(lengths)  7.45 us
  transfers between devices with their start and end apart: 8, of which 6 were waited for; matrix products, arithmetic and copies ran while one was open for 7% of the time, Pallas kernels for 0%

commit v1 on v0

v1 whole, which is shorter than its diff:
```python
import functools
import math

import jax
import jax.numpy as jnp
from jax import lax
from jax.experimental import pallas as pl
from jax.experimental.pallas import tpu as pltpu
from jax.sharding import PartitionSpec as P

C = 1280
GROUPS = 32
HEAD_DIM = 64
TDIM = 320
H = 32
W = 32
WIDE = C // GROUPS
MEMBERS = float(H * W * WIDE)
EPS = 1e-06
F32 = jnp.float32
BF16 = jnp.bfloat16

VM = pl.BlockSpec(memory_space=pltpu.VMEM)
SM = pl.BlockSpec(memory_space=pltpu.SMEM)


def call(kernel, outs, specs, scratch=()):
    return pl.pallas_call(
        kernel,
        out_shape=[jax.ShapeDtypeStruct(s, d) for s, d in outs],
        in_specs=specs,
        out_specs=[VM] * len(outs),
        scratch_shapes=list(scratch),
    )


def swapped(value):
    pairs = [(source, source ^ 1) for source in range(lax.axis_size("row"))]
    return lax.ppermute(value, "row", pairs)


def collect(block):
    peers = lax.axis_size("ch")
    pieces = jnp.broadcast_to(block[None], (peers, *block.shape))
    pieces = lax.all_to_all(pieces, "ch", 0, 0, tiled=True)
    return pieces.reshape(peers * block.shape[0], block.shape[1])


def lanes(shape):
    return lax.broadcasted_iota(jnp.int32, shape, 1)


def silu(u):
    return u / (1.0 + jnp.exp(-u))


def normalised(value, total, squares, gain):
    pieces = []
    for first in range(0, value.shape[0], WIDE):
        rows = slice(first, first + WIDE)
        mean = jnp.sum(total[rows], axis=0, keepdims=True) / MEMBERS
        spread = jnp.sum(squares[rows], axis=0, keepdims=True) / MEMBERS - mean * mean
        scale = lax.rsqrt(spread + EPS) * gain[rows]
        pieces.append((value[rows] - mean) * scale)
    return jnp.concatenate(pieces, axis=0)


def enter_kernel(latent_ref, turned_ref, sums_ref):
    value = latent_ref[...].astype(F32).T
    turned_ref[...] = value
    lane = lanes(sums_ref.shape)
    total = jnp.sum(value, axis=1, keepdims=True)
    squares = jnp.sum(value * value, axis=1, keepdims=True)
    sums_ref[...] = jnp.where(lane == 0, total, jnp.where(lane == 1, squares, 0.0))


def first_kernel(turned_ref, own_ref, peer_ref, gain_ref, active_ref):
    sums = own_ref[...] + peer_ref[...]
    value = normalised(turned_ref[...], sums[:, 0:1], sums[:, 1:2], gain_ref[...])
    active_ref[...] = silu(value).astype(BF16)


def conv_kernel(place_ref, weight_ref, full_ref, base_ref, part_ref, note_ref):
    count, tokens = part_ref.shape
    upper = place_ref[0] == 0
    token = lanes((count, tokens))
    column = token % W
    full = full_ref[...]
    combined = []
    for dy in range(3):
        rows = weight_ref[dy * 3 * count : (dy + 1) * 3 * count, :]
        taps = jnp.dot(rows, full, preferred_element_type=F32)
        left = pltpu.roll(taps[:count], 1, 1)
        right = pltpu.roll(taps[2 * count :], tokens - 1, 1)
        combined.append(
            taps[count : 2 * count]
            + jnp.where(column == 0, 0.0, left)
            + jnp.where(column == W - 1, 0.0, right)
        )
    above, middle, below = combined
    part = (
        base_ref[...]
        + middle
        + jnp.where(token < W, 0.0, pltpu.roll(above, W, 1))
        + jnp.where(token >= tokens - W, 0.0, pltpu.roll(below, tokens - W, 1))
    )
    part_ref[...] = part
    first = jnp.where(upper, 0, W)
    whole = jnp.logical_and(token >= first, token < first + tokens - W)
    kept = jnp.where(whole, part, 0.0)
    total = jnp.sum(kept, axis=1, keepdims=True)
    squares = jnp.sum(kept * kept, axis=1, keepdims=True)
    last = slice(tokens - 128, tokens)
    edge = jnp.where(upper, pltpu.roll(part[:, last], W, 1), part[:, :128])
    push = jnp.where(upper, pltpu.roll(above[:, last], 2 * W, 1), pltpu.roll(below[:, :128], W, 1))
    lane = lanes((count, 128))
    note = jnp.where(lane < W, edge, jnp.where(lane < 2 * W, push, 0.0))
    note_ref[...] = jnp.where(lane == 2 * W, total, jnp.where(lane == 2 * W + 1, squares, note))


def finish_kernel(place_ref, part_ref, own_ref, peer_ref, gain_ref, *outs, act):
    count, tokens = part_ref.shape
    upper = place_ref[0] == 0
    own, peer = own_ref[...], peer_ref[...]
    lane = lanes((count, 128))
    top = jnp.where(lane < jnp.where(upper, 0, W), pltpu.roll(peer, 128 - W, 1), 0.0)
    low = jnp.where(lane >= jnp.where(upper, 128 - W, 128), pltpu.roll(peer, 2 * W, 1), 0.0)
    part = part_ref[...]
    value = jnp.concatenate(
        [part[:, :128] + top, part[:, 128 : tokens - 128], part[:, tokens - 128 :] + low], axis=1
    )
    other = jnp.where(lane < W, peer + pltpu.roll(own, 128 - W, 1), 0.0)
    total = (
        jnp.sum(value, axis=1, keepdims=True)
        + jnp.sum(other, axis=1, keepdims=True)
        + peer[:, 2 * W : 2 * W + 1]
    )
    squares = (
        jnp.sum(value * value, axis=1, keepdims=True)
        + jnp.sum(other * other, axis=1, keepdims=True)
        + peer[:, 2 * W + 1 : 2 * W + 2]
    )
    result = normalised(value, total, squares, gain_ref[...])
    if act:
        outs[0][...] = silu(result).astype(BF16)
    else:
        outs[0][...] = result.astype(BF16)
        outs[1][...] = value


def project_kernel(query_ref, key_ref, value_ref, full_ref, q_ref, kv_ref, stack_ref):
    inner = query_ref.shape[0]
    stack_ref[:inner] = query_ref[...]
    stack_ref[inner : 2 * inner] = key_ref[...]
    stack_ref[2 * inner :] = value_ref[...]
    mixed = jnp.dot(stack_ref[...], full_ref[...], preferred_element_type=F32).astype(BF16)
    q_ref[...] = mixed[:inner]
    kv_ref[...] = mixed[inner:]


def attend_kernel(q_ref, own_ref, peer_ref, out_ref):
    inner = q_ref.shape[0]
    keys = jnp.concatenate([own_ref[:inner], peer_ref[:inner]], axis=1)
    values = jnp.concatenate([own_ref[inner:], peer_ref[inner:]], axis=1)
    scores = lax.dot_general(
        keys, q_ref[...], (((0,), (0,)), ((), ())), preferred_element_type=F32
    ) * (1.0 / math.sqrt(HEAD_DIM))
    raised = jnp.exp(scores - jnp.max(scores, axis=0, keepdims=True))
    weights = (raised * (1.0 / jnp.sum(raised, axis=0, keepdims=True))).astype(BF16)
    out_ref[...] = jnp.dot(values, weights, preferred_element_type=F32).astype(BF16)


def leave_kernel(weight_ref, full_ref, hidden_ref, result_ref):
    total = hidden_ref[...] + jnp.dot(weight_ref[...], full_ref[...], preferred_element_type=F32)
    result_ref[...] = total.T.astype(BF16)


def body(
    latent,
    timestep,
    norm_gain_a,
    conv_weight_a,
    time_weight,
    norm_gain_b,
    conv_weight_b,
    norm_gain_c,
    w_query,
    w_key,
    w_value,
    w_out,
):
    rows, width, count = latent.shape
    tokens = rows * width
    span = H // rows
    place = lax.axis_index("row")
    within = (place % span).astype(jnp.int32).reshape(1)
    image_id = place // span
    inner = w_query.shape[0]

    def tall(weight):
        return jnp.transpose(weight, (1, 2, 0, 3)).reshape(9 * count, C)

    def column(gain):
        return gain.reshape(count, 1)

    step_value = jnp.sum(jnp.where(jnp.arange(timestep.shape[0]) == image_id, timestep, 0)).astype(F32)
    half = TDIM // 2
    freqs = jnp.exp(-math.log(10000.0) * jnp.arange(half, dtype=F32) / half)
    angles = step_value * freqs
    sinus = jnp.concatenate([jnp.cos(angles), jnp.sin(angles)])[None, :].astype(BF16)
    time_add = jax.nn.silu(jnp.dot(sinus, time_weight, preferred_element_type=F32)).reshape(count, 1)

    field = ((count, tokens), F32)
    note = ((count, 128), F32)
    active = ((count, tokens), BF16)

    turned, sums = call(enter_kernel, [field, note], [VM])(latent.reshape(tokens, count))
    (active_a,) = call(first_kernel, [active], [VM] * 4)(turned, sums, swapped(sums), column(norm_gain_a))

    conv = call(conv_kernel, [field, note], [SM, VM, VM, VM])
    part, own = conv(within, tall(conv_weight_a), collect(active_a), time_add)
    (active_b,) = call(functools.partial(finish_kernel, act=True), [active], [SM] + [VM] * 4)(
        within, part, own, swapped(own), column(norm_gain_b)
    )
    part, own = conv(within, tall(conv_weight_b), collect(active_b), turned)
    normed, hidden_b = call(functools.partial(finish_kernel, act=False), [active, field], [SM] + [VM] * 4)(
        within, part, own, swapped(own), column(norm_gain_c)
    )
    query, key_value = call(
        project_kernel,
        [((inner, tokens), BF16), ((2 * inner, tokens), BF16)],
        [VM] * 4,
        [pltpu.VMEM((3 * inner, C), BF16)],
    )(w_query, w_key, w_value, collect(normed))
    (heads_out,) = call(attend_kernel, [((inner, tokens), BF16)], [VM] * 3)(
        query, key_value, swapped(key_value)
    )
    (result,) = call(leave_kernel, [((tokens, count), BF16)], [VM] * 3)(w_out, collect(heads_out), hidden_b)
    return result.reshape(rows, width, count)


def solution(mesh):
    return jax.shard_map(
        body,
        mesh=mesh,
        in_specs=(
            P("row", None, "ch"),
            P(),
            P("ch"),
            P("ch", None, None, None),
            P(None, "ch"),
            P("ch"),
            P("ch", None, None, None),
            P("ch"),
            P("ch", None),
            P("ch", None),
            P("ch", None),
            P("ch", None),
        ),
        out_specs=P("row", None, "ch"),
        check_vma=False,
    )
```

time: 247 us -> 196 us (0.79)
  waiting for transfers between devices: 76.1 us -> 32.7 us
  Pallas kernels: 0 us -> 23.2 us
  local copies, waits for them, and re-layouts: 27 us -> 12.2 us
  blocking collectives: 89.8 us -> 101 us
  matrix products: 11 us -> 0.13 us
  starting transfers between devices: 33.2 us -> 23.1 us
  other arithmetic: 6.89 us -> 0.76 us
    all_to_all x2 -> x1, waiting for transfers between devices: 72.1 us -> 30.8 us  [collect(): pieces = lax.all_to_all(pieces, 'ch', 0, 0, tiled=True)]
    pallas_call x0 -> x9, Pallas kernels: none -> 23.2 us  [the longest x1 3.97 us: body(): part, own = conv(within, tall(conv_weight_a), collect(active_a), time_add)]
    all_to_all x2 -> x3, blocking collectives: 89.8 us -> 101 us  [collect(): pieces = lax.all_to_all(pieces, 'ch', 0, 0, tiled=True)]
    transpose x2 -> x0, local copies, waits for them, and re-layouts: 8.5 us -> none  [in_order(): return jnp.moveaxis(pieces, 0, dim).reshape(lengths)]
    conv_general_dilated x2 -> x0, matrix products: 7.99 us -> none  [conv_taps(): lax.conv_general_dilated(padded[None], weight, (1, 1), 'VALID', dimension...]
    all_to_all x2 -> x1, starting transfers between devices: 8.93 us -> 3.83 us  [collect(): pieces = lax.all_to_all(pieces, 'ch', 0, 0, tiled=True)]
    ppermute x6 -> x4, starting transfers between devices: 24.3 us -> 19.3 us  [swapped(): return lax.ppermute(value, 'row', pairs)]
    reshape x3 -> x4, local copies, waits for them, and re-layouts: 7.57 us -> 3.53 us  [the longest x3 2.79 us: column(): return gain.reshape(count, 1)]
  transfers between devices with their start and end apart: 8 -> 5, of which waited for: 6 -> 4; matrix products, arithmetic and copies ran while one was open for 7% -> 2% of each run, Pallas kernels for 0% -> 0%
where the time goes in v1:
time: 196 us; the launch traced here: 194 us
  blocking collectives  101 us (52%)
  waiting for transfers between devices  32.7 us (17%)
  Pallas kernels  23.2 us (12%)
  starting transfers between devices  23.1 us (12%)
  local copies, waits for them, and re-layouts  12.2 us (6%)
    all_to_all x3, blocking collectives, collect(): pieces = lax.all_to_all(pieces, 'ch', 0, 0, tiled=True)  101 us
    all_to_all x1, waiting for transfers between devices, collect(): pieces = lax.all_to_all(pieces, 'ch', 0, 0, tiled=True)  30.8 us
    ppermute x4, starting transfers between devices, swapped(): return lax.ppermute(value, 'row', pairs)  19.3 us
    broadcast_in_dim x4, local copies, waits for them, and re-layouts, collect(): pieces = jnp.broadcast_to(block[None], (peers, *block.shape))  5.05 us
    pallas_call x1, Pallas kernels, body(): part, own = conv(within, tall(conv_weight_a), collect(active_a), time_add)  3.97 us
    pallas_call x1, Pallas kernels, body(): part, own = conv(within, tall(conv_weight_b), collect(active_b), turned)  3.97 us
  transfers between devices with their start and end apart: 5, of which 4 were waited for; matrix products, arithmetic and copies ran while one was open for 2% of the time, Pallas kernels for 0%

profile of v1, /device:TPU:1, one launch (start us, length us, event | category | flops | bytes accessed | tf_op | source)
XLA Modules:
  0.0 193.6 jit_solution(10466340328928576390)
XLA Ops:
  0.0 1.7 shard_map.118
  1.7 8.7 %collective-permute-start = (f32[80,128]{1,0:T(8,128)}, f32[80,128]{1,0:T(8,128)S(1)}, u32[]{:S(2)}, u32[]{:S(2)}) collective-permute-start(f32[80,128]{1,0:T(8,128)} %get-tuple-element.16.own_ref), channel_id=1, source_target_pairs={{0,1},{1,0},{2,3},{3,2},{4,5},{5,4},{6,7},{7,6},{8,9},{9,8},{10,11... | collective-permute-start | bytes 122888 | tf_op jit(solution)/shard_map/ppermute | solution.py:39
  10.5 1.4 copy.13.gain_ref
  12.5 1.8 shard_map.119
  14.3 2.1 %broadcast_in_dim.12 = bf16[16,80,512]{2,1,0:T(8,128)(2,1)} broadcast(bf16[80,512]{1,0:T(8,128)(2,1)} %shard_map.119), dimensions={1,2} | broadcast | bytes 1392640 | tf_op jit(solution)/shard_map/broadcast_in_dim | solution.py:44
  16.4 3.8 %all-to-all-start = ((bf16[16,80,512]{2,1,0:T(8,128)(2,1)}), bf16[16,80,512]{2,1,0:T(8,128)(2,1)S(1)}, u32[]{:S(2)}, u32[]{:S(2)}) async-start(bf16[16,80,512]{2,1,0:T(8,128)(2,1)} %broadcast_in_dim.12), calls=%async_computation | async-start | bytes 2621440 | tf_op jit(solution)/shard_map/all_to_all | solution.py:45
  20.2 0.6 fusion
  21.8 0.7 copy.14.base_ref
  22.5 30.8 %all-to-all-done = bf16[16,80,512]{2,1,0:T(8,128)(2,1)S(1)} async-done(((bf16[16,80,512]{2,1,0:T(8,128)(2,1)}), bf16[16,80,512]{2,1,0:T(8,128)(2,1)S(1)}, u32[]{:S(2)}, u32[]{:S(2)}) %all-to-all-start) | async-done | bytes 1310752 | tf_op jit(solution)/shard_map/all_to_all | solution.py:45
  53.4 1.1 copy-done.1
  54.5 4.0 %shard_map.120 = (f32[80,512]{1,0:T(8,128)}, f32[80,128]{1,0:T(8,128)}) custom-call(s32[1]{0:T(128)} %bitcast.place_ref, bf16[720,1280]{1,0:T(8,128)(2,1)} %bitcast.30, bf16[1280,512]{1,0:T(8,128)(2,1)} %bitcast.26, f32[80,1]{1,0:T(8,128)} %copy.14.base_ref), custom_call_target="tpu_custom_call" | custom-call | tf_op jit(solution)/shard_map/pallas_call | solution.py:221
  58.5 2.9 %collective-permute-start.1 = (f32[80,128]{1,0:T(8,128)}, f32[80,128]{1,0:T(8,128)S(1)}, u32[]{:S(2)}, u32[]{:S(2)}) collective-permute-start(f32[80,128]{1,0:T(8,128)} %get-tuple-element.18.own_ref), channel_id=1, source_target_pairs={{0,1},{1,0},{2,3},{3,2},{4,5},{5,4},{6,7},{7,6},{8,9},{9,8},{10,11... | collective-permute-start | bytes 122888 | tf_op jit(solution)/shard_map/ppermute | solution.py:39
  61.3 0.7 copy.15.gain_ref
  62.4 0.6 copy-done.4
  63.0 2.0 %shard_map.121 = bf16[80,512]{1,0:T(8,128)(2,1)} custom-call(s32[1]{0:T(128)} %bitcast.place_ref, f32[80,512]{1,0:T(8,128)} %get-tuple-element.17.part_ref, f32[80,128]{1,0:T(8,128)} %get-tuple-element.18.own_ref, f32[80,128]{1,0:T(8,128)} %copy-done.4, f32[80,1]{1,0:T(8,128)} %copy.15.gain_ref), custom_call_target="tpu_custom_call" | custom-call | tf_op jit(solution)/shard_map/pallas_call | solution.py:222
  65.0 1.0 broadcast_in_dim.14
  66.0 35.7 %all_to_all.20 = bf16[16,80,512]{2,1,0:T(8,128)(2,1)} all-to-all(bf16[16,80,512]{2,1,0:T(8,128)(2,1)S(1)} %broadcast_in_dim.14), channel_id=1, replica_groups=mesh['ch'=16,'row'=32] {'ch'}, dimensions={0} | all-to-all | bytes 2621440 | tf_op jit(solution)/shard_map/all_to_all | solution.py:45
  101.8 4.0 %shard_map.122 = (f32[80,512]{1,0:T(8,128)}, f32[80,128]{1,0:T(8,128)}) custom-call(s32[1]{0:T(128)} %bitcast.place_ref, bf16[720,1280]{1,0:T(8,128)(2,1)} %bitcast.31, bf16[1280,512]{1,0:T(8,128)(2,1)} %bitcast.27, f32[80,512]{1,0:T(8,128)} %get-tuple-element.15.turned_ref.base_ref), custom_call_target="tpu_custom_call" | custom-call | tf_op jit(solution)/shard_map/pallas_call | solution.py:225
  105.7 3.8 %collective-permute-start.2 = (f32[80,128]{1,0:T(8,128)}, f32[80,128]{1,0:T(8,128)S(1)}, u32[]{:S(2)}, u32[]{:S(2)}) collective-permute-start(f32[80,128]{1,0:T(8,128)} %get-tuple-element.20.own_ref), channel_id=1, source_target_pairs={{0,1},{1,0},{2,3},{3,2},{4,5},{5,4},{6,7},{7,6},{8,9},{9,8},{10,11... | collective-permute-start | bytes 122888 | tf_op jit(solution)/shard_map/ppermute | solution.py:39
  109.6 0.7 copy.16.gain_ref
  110.7 0.6 copy-done.3
  111.3 2.0 %shard_map.123 = (bf16[80,512]{1,0:T(8,128)(2,1)}, f32[80,512]{1,0:T(8,128)}) custom-call(s32[1]{0:T(128)} %bitcast.place_ref, f32[80,512]{1,0:T(8,128)} %get-tuple-element.19.part_ref, f32[80,128]{1,0:T(8,128)} %get-tuple-element.20.own_ref, f32[80,128]{1,0:T(8,128)} %copy-done.3, f32[80,1]{1,0:T(8,128)} %copy.16.gain_ref), custom_call_target="tpu_custom_call" | custom-call | tf_op jit(solution)/shard_map/pallas_call | solution.py:226
  113.2 1.0 broadcast_in_dim.15
  114.2 35.7 %all_to_all.21 = bf16[16,80,512]{2,1,0:T(8,128)(2,1)} all-to-all(bf16[16,80,512]{2,1,0:T(8,128)(2,1)S(1)} %broadcast_in_dim.15), channel_id=1, replica_groups=mesh['ch'=16,'row'=32] {'ch'}, dimensions={0} | all-to-all | bytes 2621440 | tf_op jit(solution)/shard_map/all_to_all | solution.py:45
  150.0 2.7 %shard_map.124 = (bf16[64,512]{1,0:T(8,128)(2,1)}, bf16[128,512]{1,0:T(8,128)(2,1)}) custom-call(bf16[64,1280]{1,0:T(8,128)(2,1)} %query_ref.1, bf16[64,1280]{1,0:T(8,128)(2,1)} %key_ref.1, bf16[64,1280]{1,0:T(8,128)(2,1)} %value_ref.1, bf16[1280,512]{1,0:T(8,128)(2,1)} %bitcast.28), custom_call_target="tpu_custom_call" | custom-call | tf_op jit(solution)/shard_map/pallas_call | solution.py:229
  152.6 3.8 %collective-permute-start.3 = (bf16[128,512]{1,0:T(8,128)(2,1)}, bf16[128,512]{1,0:T(8,128)(2,1)S(1)}, u32[]{:S(2)}, u32[]{:S(2)}) collective-permute-start(bf16[128,512]{1,0:T(8,128)(2,1)} %get-tuple-element.23.own_ref), channel_id=1, source_target_pairs={{0,1},{1,0},{2,3},{3,2},{4,5},{5,4},{6,7},{7,6},{8,9},{9,8},{10,11... | collective-permute-start | bytes 393224 | tf_op jit(solution)/shard_map/ppermute | solution.py:39
  156.5 1.2 collective-permute-done.3.peer_ref
  157.7 0.7 copy-done.2
  158.3 2.8 %shard_map.125 = bf16[64,512]{1,0:T(8,128)(2,1)} custom-call(bf16[64,512]{1,0:T(8,128)(2,1)} %get-tuple-element.22.q_ref, bf16[128,512]{1,0:T(8,128)(2,1)} %get-tuple-element.23.own_ref, bf16[128,512]{1,0:T(8,128)(2,1)} %copy-done.2), custom_call_target="tpu_custom_call" | custom-call | tf_op jit(solution)/shard_map/pallas_call | solution.py:235
  161.1 0.9 broadcast_in_dim.16
  162.1 29.2 %all_to_all.22 = bf16[16,64,512]{2,1,0:T(8,128)(2,1)} all-to-all(bf16[16,64,512]{2,1,0:T(8,128)(2,1)S(1)} %broadcast_in_dim.16), channel_id=1, replica_groups=mesh['ch'=16,'row'=32] {'ch'}, dimensions={0} | all-to-all | bytes 2097152 | tf_op jit(solution)/shard_map/all_to_all | solution.py:45
  191.3 2.3 %shard_map.126 = bf16[512,80]{1,0:T(8,128)(2,1)} custom-call(bf16[80,1024]{1,0:T(8,128)(2,1)} %weight_ref.1, bf16[1024,512]{1,0:T(8,128)(2,1)} %bitcast.29, f32[80,512]{1,0:T(8,128)} %get-tuple-element.24.hidden_ref), custom_call_target="tpu_custom_call" | custom-call | tf_op jit(solution)/shard_map/pallas_call | solution.py:238
  (21 shorter events, 1.6 us)
Async XLA Ops:
  0.0 21.7 %copy-start = (bf16[320,80]{0,1:T(8,128)(2,1)S(1)}, bf16[320,80]{0,1:T(8,128)(2,1)}, u32[]{:S(2)}) copy-start(bf16[320,80]{0,1:T(8,128)(2,1)} %param.16) | copy-start | bytes 153604
  1.7 10.1 %collective-permute-start = (f32[80,128]{1,0:T(8,128)}, f32[80,128]{1,0:T(8,128)S(1)}, u32[]{:S(2)}, u32[]{:S(2)}) collective-permute-start(f32[80,128]{1,0:T(8,128)} %get-tuple-element.16.own_ref), channel_id=1, source_target_pairs={{0,1},{1,0},{2,3},{3,2},{4,5},{5,4},{6,7},{7,6},{8,9},{9,8},{10,11... | collective-permute-start | bytes 122888 | tf_op jit(solution)/shard_map/ppermute | solution.py:39
  11.9 0.6 copy-start.5
  16.4 3.9 %copy-start.8 = (s32[16]{0:T(128)S(1)}, s32[16]{0:T(128)}, u32[]{:S(2)}) copy-start(s32[16]{0:T(128)} %param.13) | copy-start | bytes 196
  16.4 37.0 %all-to-all-start = ((bf16[16,80,512]{2,1,0:T(8,128)(2,1)}), bf16[16,80,512]{2,1,0:T(8,128)(2,1)S(1)}, u32[]{:S(2)}, u32[]{:S(2)}) async-start(bf16[16,80,512]{2,1,0:T(8,128)(2,1)} %broadcast_in_dim.12), calls=%async_computation | async-start | bytes 2621440 | tf_op jit(solution)/shard_map/all_to_all | solution.py:45
  53.4 1.1 copy-start.1
  54.5 6.8 %copy-start.6 = (f32[80]{0:T(128)S(1)}, f32[80]{0:T(128)}, u32[]{:S(2)}) copy-start(f32[80]{0:T(128)} %param.17) | copy-start | bytes 964
  58.5 3.9 %collective-permute-start.1 = (f32[80,128]{1,0:T(8,128)}, f32[80,128]{1,0:T(8,128)S(1)}, u32[]{:S(2)}, u32[]{:S(2)}) collective-permute-start(f32[80,128]{1,0:T(8,128)} %get-tuple-element.18.own_ref), channel_id=1, source_target_pairs={{0,1},{1,0},{2,3},{3,2},{4,5},{5,4},{6,7},{7,6},{8,9},{9,8},{10,11... | collective-permute-start | bytes 122888 | tf_op jit(solution)/shard_map/ppermute | solution.py:39
  62.4 0.6 copy-start.4
  101.8 7.8 %copy-start.7 = (f32[80]{0:T(128)S(1)}, f32[80]{0:T(128)}, u32[]{:S(2)}) copy-start(f32[80]{0:T(128)} %param.19) | copy-start | bytes 964
  105.7 4.9 %collective-permute-start.2 = (f32[80,128]{1,0:T(8,128)}, f32[80,128]{1,0:T(8,128)S(1)}, u32[]{:S(2)}, u32[]{:S(2)}) collective-permute-start(f32[80,128]{1,0:T(8,128)} %get-tuple-element.20.own_ref), channel_id=1, source_target_pairs={{0,1},{1,0},{2,3},{3,2},{4,5},{5,4},{6,7},{7,6},{8,9},{9,8},{10,11... | collective-permute-start | bytes 122888 | tf_op jit(solution)/shard_map/ppermute | solution.py:39
  110.7 0.6 copy-start.3
  152.6 5.0 %collective-permute-start.3 = (bf16[128,512]{1,0:T(8,128)(2,1)}, bf16[128,512]{1,0:T(8,128)(2,1)S(1)}, u32[]{:S(2)}, u32[]{:S(2)}) collective-permute-start(bf16[128,512]{1,0:T(8,128)(2,1)} %get-tuple-element.23.own_ref), channel_id=1, source_target_pairs={{0,1},{1,0},{2,3},{3,2},{4,5},{5,4},{6,7},{7,6},{8,9},{9,8},{10,11... | collective-permute-start | bytes 393224 | tf_op jit(solution)/shard_map/ppermute | solution.py:39
  157.7 0.7 copy-start.2

commit v2 on v1

v2 whole, which is shorter than its diff:
```python
import functools
import math

import jax
import jax.numpy as jnp
from jax import lax
from jax.experimental import pallas as pl
from jax.experimental.pallas import tpu as pltpu
from jax.sharding import PartitionSpec as P

C = 1280
GROUPS = 32
HEAD_DIM = 64
TDIM = 320
H = 32
W = 32
WIDE = C // GROUPS
MEMBERS = float(H * W * WIDE)
EPS = 1e-06
F32 = jnp.float32
BF16 = jnp.bfloat16

VM = pl.BlockSpec(memory_space=pltpu.VMEM)
SM = pl.BlockSpec(memory_space=pltpu.SMEM)


def call(kernel, outs, specs, scratch=()):
    return pl.pallas_call(
        kernel,
        out_shape=[jax.ShapeDtypeStruct(s, d) for s, d in outs],
        in_specs=specs,
        out_specs=[VM] * len(outs),
        scratch_shapes=list(scratch),
    )


def device(ch, row):
    return ch * lax.axis_size("row") + row


def core_pairs():
    rows, chs = lax.axis_size("row"), lax.axis_size("ch")
    return [(device(k, r), device(k, r ^ 1)) for k in range(chs) for r in range(rows)]


def swapped(value):
    return lax.ppermute(value, ("ch", "row"), core_pairs())


def crossed(value):
    chs = lax.axis_size("ch")
    return lax.ppermute(value, "ch", [(k, (k + chs // 2) % chs) for k in range(chs)])


def from_beside(value):
    rows, chs = lax.axis_size("row"), lax.axis_size("ch")
    wide = 2 if rows % 4 == 0 else 1
    pairs = []
    for k in range(chs):
        for r in range(rows):
            core, high, rest = r % 2, r // 2 % wide, r // (2 * wide)
            x = (2 * high + k // (chs // 2) + (1 if core == 0 else -1)) % (2 * wide)
            source = device(x % 2 * (chs // 2) + k % (chs // 2), (rest * wide + x // 2) * 2 + core)
            pairs.append((source, device(k, r)))
    return lax.ppermute(value, ("ch", "row"), pairs)


def copies(block, count):
    return jnp.broadcast_to(block[None], (count, *block.shape))


def column_collect(block):
    half = lax.axis_size("ch") // 2
    groups = [list(range(half)), list(range(half, 2 * half))]
    return lax.all_to_all(copies(block, half), "ch", 0, 0, tiled=True, axis_index_groups=groups)


def image_collect(block):
    rows, half = lax.axis_size("row"), lax.axis_size("ch") // 2
    groups = [
        [device(k, r), device(k + half, r), device(k + half, r + 1), device(k, r + 1)]
        for r in range(0, rows, 2)
        for k in range(half)
    ]
    return lax.all_to_all(copies(block, 4), ("ch", "row"), 0, 0, tiled=True, axis_index_groups=groups)


def lanes(shape):
    return lax.broadcasted_iota(jnp.int32, shape, 1)


def silu(u):
    return u / (1.0 + jnp.exp(-u))


def scaled(value, total, squares, gain):
    mean = total / MEMBERS
    spread = squares / MEMBERS - mean * mean
    return (value - mean) * (lax.rsqrt(spread + EPS) * gain)


def by_group(per_channel):
    return [
        jnp.sum(per_channel[first : first + WIDE], axis=0, keepdims=True)
        for first in range(0, per_channel.shape[0], WIDE)
    ]


def enter_kernel(place_ref, latent_ref, turned_ref, keep_ref, send_ref, sums_ref):
    value = latent_ref[...].astype(F32).T
    turned_ref[...] = value
    half = value.shape[1] // 2
    first = place_ref[2] == 0
    keep_ref[...] = jnp.where(first, value[:, :half], value[:, half:])
    send_ref[...] = jnp.where(first, value[:, half:], value[:, :half])
    lane = lanes(sums_ref.shape)
    total = jnp.sum(value, axis=1, keepdims=True)
    squares = jnp.sum(value * value, axis=1, keepdims=True)
    sums_ref[...] = jnp.where(lane == 0, total, jnp.where(lane == 1, squares, 0.0))


def first_kernel(place_ref, turned_ref, own_ref, peer_ref, gain_ref, active_ref):
    sums = own_ref[...] + peer_ref[...]
    totals, squares = by_group(sums[:, 0:1]), by_group(sums[:, 1:2])
    pieces = []
    for group in range(len(totals)):
        rows = slice(group * WIDE, (group + 1) * WIDE)
        pieces.append(scaled(turned_ref[rows], totals[group], squares[group], gain_ref[rows]))
    value = silu(jnp.concatenate(pieces, axis=0)).astype(BF16)
    half = value.shape[1] // 2
    core = place_ref[1]
    active_ref[core] = value[:, :half]
    active_ref[1 - core] = value[:, half:]


def gather_into(full_ref, whole_ref):
    if len(full_ref.shape) == 3:
        whole_ref[...] = full_ref[...].reshape(whole_ref.shape)
        return
    peers, _, count, _ = full_ref.shape
    for side in range(2):
        for peer in range(peers):
            at = (side * peers + peer) * count
            whole_ref[at : at + count] = full_ref[peer, side]


def both(core, own, got, other, whole_ref):
    depth = got.shape[1]
    near = whole_ref[pl.ds(pl.multiple_of(core * depth, 128), depth), :]
    far = whole_ref[pl.ds(pl.multiple_of((1 - core) * depth, 128), depth), :]
    return (
        jnp.dot(own, whole_ref[...], preferred_element_type=F32),
        jnp.dot(got, near, preferred_element_type=F32) + jnp.dot(other, far, preferred_element_type=F32),
    )


def conv_kernel(place_ref, own_ref, got_ref, other_ref, full_ref, base_ref, far_ref, part_ref, note_ref, whole_ref, *, at):
    _, count, tokens = part_ref.shape
    side, core, quarter = place_ref[0], place_ref[1], place_ref[3]
    token = lanes((count, tokens))
    column = token % W
    lane = lanes((count, 128))
    begin = jnp.where(quarter > 0, W, 0)
    end = jnp.where(quarter < 3, tokens - W, tokens)
    gather_into(full_ref, whole_ref)
    taps = both(core, own_ref[...], got_ref[: 9 * count], other_ref[: 9 * count], whole_ref)
    bases = base_ref[...], far_ref[:, at]
    extra = jnp.zeros((16, 128), F32)
    spot = lanes((16, 128))
    for which in range(2):
        here = side if which == 0 else 1 - side
        combined = []
        for dy in range(3):
            left, middle, right = (
                taps[which][(3 * dy + dx) * count : (3 * dy + dx + 1) * count] for dx in range(3)
            )
            combined.append(
                middle
                + jnp.where(column == 0, 0.0, pltpu.roll(left, 1, 1))
                + jnp.where(column == W - 1, 0.0, pltpu.roll(right, tokens - 1, 1))
            )
        above, middle, below = combined
        part = (
            bases[which]
            + middle
            + jnp.where(token < W, 0.0, pltpu.roll(above, W, 1))
            + jnp.where(token >= tokens - W, 0.0, pltpu.roll(below, tokens - W, 1))
        )
        part_ref[here] = part
        kept = jnp.where(jnp.logical_and(token >= begin, token < end), part, 0.0)
        totals = by_group(jnp.sum(kept, axis=1, keepdims=True))
        squares = by_group(jnp.sum(kept * kept, axis=1, keepdims=True))
        bottom = pltpu.roll(part[:, tokens - 128 :], 2 * W, 1)
        up = pltpu.roll(below[:, :128], 2 * W, 1)
        note = jnp.where(lane < W, part[:, :128], jnp.where(lane < 2 * W, bottom, jnp.where(lane < 3 * W, up, above[:, tokens - 128 :])))
        note_ref[pl.ds(pl.multiple_of(here * count, 16), count), :] = note.astype(BF16)
        for group in range(len(totals)):
            for kind, value in enumerate((totals[group], squares[group])):
                for piece in range(3):
                    rounded = value.astype(BF16).astype(F32)
                    index = (here * len(totals) + group) * 6 + kind * 3 + piece
                    extra = jnp.where(spot == index, rounded, extra)
                    value = value - rounded
    note_ref[2 * count :, :] = extra.astype(BF16)


def finish_kernel(place_ref, part_ref, notes_ref, gains_ref, *outs, act, lane_of):
    _, count, tokens = part_ref.shape
    quarter = place_ref[3]
    lane = lanes((count, 128))
    sums = notes_ref[0, 2 * count :].astype(F32)
    for place in range(1, 4):
        sums = sums + notes_ref[place, 2 * count :].astype(F32)
    before = jnp.maximum(quarter - 1, 0)
    after = jnp.minimum(quarter + 1, 3)
    for side in range(2):
        rows = slice(side * count, (side + 1) * count)
        notes = [notes_ref[place, rows].astype(F32) for place in range(4)]
        total = jnp.zeros((count, 1), F32)
        squares = jnp.zeros((count, 1), F32)
        for low in range(3):
            one, two = notes[low], notes[low + 1]
            edges = jnp.where(
                lane < W,
                two + pltpu.roll(one, W, 1),
                jnp.where(lane < 2 * W, one + pltpu.roll(two, 128 - W, 1), 0.0),
            )
            total = total + jnp.sum(edges, axis=1, keepdims=True)
            squares = squares + jnp.sum(edges * edges, axis=1, keepdims=True)
        top = pltpu.roll(notes_ref[before, rows].astype(F32), W, 1)
        low = pltpu.roll(notes_ref[after, rows].astype(F32), W, 1)
        part = part_ref[side]
        value = jnp.concatenate(
            [
                part[:, :128] + jnp.where(lane < jnp.where(quarter > 0, W, 0), top, 0.0),
                part[:, tokens - 128 :] + jnp.where(lane >= jnp.where(quarter < 3, 128 - W, 128), low, 0.0),
            ],
            axis=1,
        )
        totals, squared = by_group(total), by_group(squares)
        gain = gains_ref[side][:, lane_of : lane_of + 1]
        pieces = []
        for group in range(len(totals)):
            first = (side * len(totals) + group) * 6
            whole = totals[group] + jnp.sum(sums[0:1, first : first + 3], axis=1, keepdims=True)
            whole_squares = squared[group] + jnp.sum(sums[0:1, first + 3 : first + 6], axis=1, keepdims=True)
            span = slice(group * WIDE, (group + 1) * WIDE)
            pieces.append(scaled(value[span], whole, whole_squares, gain[span]))
        result = jnp.concatenate(pieces, axis=0)
        if act:
            outs[0][side] = silu(result).astype(BF16)
        else:
            outs[0][side] = result.astype(BF16)
            outs[1][side] = value


def project_kernel(place_ref, query_ref, key_ref, value_ref, got_ref, other_ref, full_ref, q_ref, kv_ref, whole_ref, stack_ref, *, at):
    inner = query_ref.shape[0]
    side, core = place_ref[0], place_ref[1]
    stack_ref[:inner] = query_ref[...]
    stack_ref[inner : 2 * inner] = key_ref[...]
    stack_ref[2 * inner :] = value_ref[...]
    gather_into(full_ref, whole_ref)
    rows = slice(at, at + 3 * inner)
    mixed = both(core, stack_ref[...], got_ref[rows], other_ref[rows], whole_ref)
    for which in range(2):
        here = side if which == 0 else 1 - side
        q_ref[here] = mixed[which][:inner].astype(BF16)
        kv_ref[here] = mixed[which][inner:].astype(BF16)


def attend_kernel(q_ref, pairs_ref, out_ref):
    inner = q_ref.shape[1]
    for head in range(2):
        keys = jnp.concatenate([pairs_ref[place, head, :inner] for place in range(4)], axis=1)
        values = jnp.concatenate([pairs_ref[place, head, inner:] for place in range(4)], axis=1)
        scores = lax.dot_general(
            keys, q_ref[head], (((0,), (0,)), ((), ())), preferred_element_type=F32
        ) * (1.0 / math.sqrt(HEAD_DIM))
        raised = jnp.exp(scores - jnp.max(scores, axis=0, keepdims=True))
        weights = (raised * (1.0 / jnp.sum(raised, axis=0, keepdims=True))).astype(BF16)
        out_ref[head] = jnp.dot(values, weights, preferred_element_type=F32).astype(BF16)


def leave_kernel(place_ref, weight_ref, got_ref, other_ref, full_ref, hidden_ref, keep_ref, send_ref, whole_ref, *, at):
    count, depth = weight_ref.shape
    side, core = place_ref[0], place_ref[1]
    gather_into(full_ref, whole_ref)
    got, other = (ref[at : at + count, : depth // 2] for ref in (got_ref, other_ref))
    mine, theirs = both(core, weight_ref[...], got, other, whole_ref)
    keep_ref[...] = (hidden_ref[side] + mine).astype(BF16)
    send_ref[...] = (hidden_ref[1 - side] + theirs).astype(BF16)


def last_kernel(place_ref, keep_ref, peer_ref, result_ref):
    span = keep_ref.shape[1]
    part = place_ref[2]
    for ref, at in ((keep_ref, part), (peer_ref, 1 - part)):
        result_ref[pl.ds(pl.multiple_of(at * span, 16), span), :] = ref[...].astype(F32).T.astype(BF16)


def body(
    latent,
    timestep,
    norm_gain_a,
    conv_weight_a,
    time_weight,
    norm_gain_b,
    conv_weight_b,
    norm_gain_c,
    w_query,
    w_key,
    w_value,
    w_out,
):
    rows, width, count = latent.shape
    tokens = rows * width
    share = tokens // 2
    chs = lax.axis_size("ch")
    channel, place = lax.axis_index("ch"), lax.axis_index("row")
    side, core = channel // (chs // 2), place % 2
    part = side ^ core
    where = jnp.stack([side, core, part, 2 * core + part]).astype(jnp.int32)
    image_id = place // 2
    inner = w_query.shape[0]

    def tall(weight):
        return jnp.transpose(weight, (1, 2, 0, 3)).reshape(9 * count, C)

    def halved(weight):
        depth = weight.shape[1] // 2
        return lax.dynamic_slice_in_dim(weight, core * depth, depth, axis=1)

    step_value = jnp.sum(jnp.where(jnp.arange(timestep.shape[0]) == image_id, timestep, 0)).astype(F32)
    half = TDIM // 2
    freqs = jnp.exp(-math.log(10000.0) * jnp.arange(half, dtype=F32) / half)
    angles = step_value * freqs
    sinus = jnp.concatenate([jnp.cos(angles), jnp.sin(angles)])[None, :].astype(BF16)
    time_add = jax.nn.silu(jnp.dot(sinus, time_weight, preferred_element_type=F32))[0]
    vector = jnp.pad(jnp.stack([time_add, norm_gain_b, norm_gain_c], axis=1), ((0, 0), (0, 125)))

    field = ((2, count, share), F32)
    active = ((2, count, share), BF16)
    quarter = ((count, share), F32)
    note = ((2 * count + 16, 128), BF16)
    whole = pltpu.VMEM((C, share), BF16)

    turned, keep, send, sums = call(
        enter_kernel, [((count, tokens), F32), quarter, quarter, ((count, 128), F32)], [SM, VM]
    )(where, latent.reshape(tokens, count))
    (active_a,) = call(first_kernel, [active], [SM] + [VM] * 4)(
        where, turned, sums, swapped(sums), norm_gain_a.reshape(count, 1)
    )

    own_a, own_b = tall(conv_weight_a), tall(conv_weight_b)
    mail = crossed(jnp.concatenate([send, vector], axis=1))
    got_a = from_beside(halved(own_a))
    late = jnp.concatenate([w_query, w_key, w_value], axis=0)
    late_out = jnp.pad(halved(w_out), ((0, 0), (0, (C - w_out.shape[1]) // 2)))
    got_b = from_beside(jnp.concatenate([halved(own_b), halved(late), late_out], axis=0))
    theirs = mail[:, share:]
    vectors = jnp.where(side == 0, jnp.stack([vector, theirs]), jnp.stack([theirs, vector]))

    spread = jnp.broadcast_to(active_a[:, None], (2, chs // 2, count, share)).reshape(chs, count, share)
    full = lax.all_to_all(spread, "ch", 0, 0, tiled=True)
    other_a = swapped(got_a)

    def conv(full, own, got, other, base, at):
        return call(
            functools.partial(conv_kernel, at=at), [field, note], [SM] + [VM] * 6, [whole]
        )(where, own, got, other, full, base, mail)

    def finish(part, note, act, lane_of, outs):
        return call(
            functools.partial(finish_kernel, act=act, lane_of=lane_of), outs, [SM] + [VM] * 3
        )(where, part, image_collect(note), vectors)

    part_a, note_a = conv(full, own_a, got_a, other_a, vector[:, 0:1], slice(share, share + 1))
    (active_b,) = finish(part_a, note_a, True, 1, [active])
    other_b = swapped(got_b)
    part_b, note_b = conv(column_collect(active_b), own_b, got_b, other_b, keep, slice(0, share))
    normed, hidden_b = finish(part_b, note_b, False, 2, [active, field])

    query, key_value = call(
        functools.partial(project_kernel, at=9 * count),
        [((2, inner, share), BF16), ((2, 2 * inner, share), BF16)],
        [SM] + [VM] * 6,
        [whole, pltpu.VMEM((3 * inner, C), BF16)],
    )(where, w_query, w_key, w_value, got_b, other_b, column_collect(normed))
    (heads_out,) = call(attend_kernel, [((2, inner, share), BF16)], [VM] * 2)(
        query, image_collect(key_value)
    )
    kept, sent = call(
        functools.partial(leave_kernel, at=9 * count + 3 * inner),
        [((count, share), BF16)] * 2,
        [SM] + [VM] * 5,
        [pltpu.VMEM((w_out.shape[1], share), BF16)],
    )(where, w_out, got_b, other_b, column_collect(heads_out), hidden_b)
    (result,) = call(last_kernel, [((tokens, count), BF16)], [SM] + [VM] * 2)(where, kept, crossed(sent))
    return result.reshape(rows, width, count)


def solution(mesh):
    return jax.shard_map(
        body,
        mesh=mesh,
        in_specs=(
            P("row", None, "ch"),
            P(),
            P("ch"),
            P("ch", None, None, None),
            P(None, "ch"),
            P("ch"),
            P("ch", None, None, None),
            P("ch"),
            P("ch", None),
            P("ch", None),
            P("ch", None),
            P("ch", None),
        ),
        out_specs=P("row", None, "ch"),
        check_vma=False,
    )
```

time: 196 us -> 187 us (0.954)
  blocking collectives: 101 us -> 64.8 us
  starting transfers between devices: 23.1 us -> 43.3 us
  Pallas kernels: 23.2 us -> 29.4 us
  waiting for transfers between devices: 32.7 us -> 26.6 us
  local copies, waits for them, and re-layouts: 12.2 us -> 17 us
  other arithmetic: 0.76 us -> 3.16 us
    all_to_all x3 -> x4, blocking collectives: 101 us -> 64.8 us  [the longest x2 44.9 us: column_collect(): lax.all_to_all(copies(block, half), 'ch', 0, 0, tiled=True, axis_index_gr...]
    ppermute x4 -> x7, starting transfers between devices: 19.3 us -> 32.6 us  [the longest x3 19.3 us: swapped(): return lax.ppermute(value, ('ch', 'row'), core_pairs())]
    all_to_all x1 -> x3, waiting for transfers between devices: 30.8 us -> 23.7 us  [the longest x1 20.7 us: column_collect(): lax.all_to_all(copies(block, half), 'ch', 0, 0, tiled=True, axis_index_gr...]
    all_to_all x1 -> x3, starting transfers between devices: 3.83 us -> 10.8 us  [the longest x1 3.62 us: image_collect(): lax.all_to_all(copies(block, 4), ('ch', 'row'), 0, 0, tiled=True, axis_in...]
    pallas_call x9 -> x10, Pallas kernels: 23.2 us -> 29.4 us  [the longest x2 9.44 us: conv(): call(functools.partial(conv_kernel, at=at), [field, note], [SM] + [VM] *...]
    broadcast_in_dim x4 -> x7, local copies, waits for them, and re-layouts: 5.05 us -> 8.58 us  [the longest x6 6.82 us: copies(): return jnp.broadcast_to(block[None], (count, *block.shape))]
    reshape x4 -> x1, local copies, waits for them, and re-layouts: 3.53 us -> 0.71 us  [body(): norm_gain_a.reshape(count, 1)]
    dynamic_slice x0 -> x3, local copies, waits for them, and re-layouts: none -> 2.46 us  [halved(): return lax.dynamic_slice_in_dim(weight, core * depth, depth, axis=1)]
  transfers between devices with their start and end apart: 5 -> 10, of which waited for: 4 -> 3; matrix products, arithmetic and copies ran while one was open for 2% -> 6% of each run, Pallas kernels for 0% -> 6%
where the time goes in v2:
time: 187 us; the launch traced here: 185 us
  blocking collectives  64.8 us (35%)
  starting transfers between devices  43.3 us (23%)
  Pallas kernels  29.4 us (16%)
  waiting for transfers between devices  26.6 us (14%)
  local copies, waits for them, and re-layouts  17 us (9%)
  other arithmetic  3.16 us (2%)
    all_to_all x2, blocking collectives, column_collect(): lax.all_to_all(copies(block, half), 'ch', 0, 0, tiled=True, axis_index_gr...  44.9 us
    all_to_all x1, waiting for transfers between devices, column_collect(): lax.all_to_all(copies(block, half), 'ch', 0, 0, tiled=True, axis_index_gr...  20.7 us
    all_to_all x2, blocking collectives, image_collect(): lax.all_to_all(copies(block, 4), ('ch', 'row'), 0, 0, tiled=True, axis_in...  19.9 us
    ppermute x3, starting transfers between devices, swapped(): return lax.ppermute(value, ('ch', 'row'), core_pairs())  19.3 us
    pallas_call x2, Pallas kernels, conv(): call(functools.partial(conv_kernel, at=at), [field, note], [SM] + [VM] *...  9.44 us
    ppermute x2, starting transfers between devices, from_beside(): return lax.ppermute(value, ('ch', 'row'), pairs)  7.7 us
    broadcast_in_dim x6, local copies, waits for them, and re-layouts, copies(): return jnp.broadcast_to(block[None], (count, *block.shape))  6.82 us
    ppermute x2, starting transfers between devices, crossed(): lax.ppermute(value, 'ch', [(k, (k + chs // 2) % chs) for k in range(chs)])  5.61 us
  transfers between devices with their start and end apart: 10, of which 3 were waited for; matrix products, arithmetic and copies ran while one was open for 6% of the time, Pallas kernels for 6%

profile of v2, /device:TPU:1, one launch (start us, length us, event | category | flops | bytes accessed | tf_op | source)
XLA Modules:
  0.0 185.4 jit_solution(17234176981477525029)
XLA Ops:
  0.1 2.4 %constant_dynamic-slice_fusion = bf16[720,640]{1,0:T(8,128)(2,1)} fusion(bf16[720,1280]{1,0:T(8,128)(2,1)} %bitcast.30, s32[]{:T(128)S(6)} %select_n.36), kind=kLoop, calls=%fused_computation.14 | loop fusion | bytes 1843204 | tf_op jit(solution)/shard_map/dynamic_slice | solution.py:332
  2.4 3.9 %collective-permute-start.2 = (bf16[720,640]{1,0:T(8,128)(2,1)}, bf16[720,640]{1,0:T(8,128)(2,1)}, u32[]{:S(2)}, u32[]{:S(2)}) collective-permute-start(bf16[720,640]{1,0:T(8,128)(2,1)} %constant_dynamic-slice_fusion), channel_id=1, source_target_pairs={{256,0},{259,1},{258,2},{257,3},{260,4},{263,5},{262,6},{261,7},{2... | collective-permute-start | bytes 2764808 | tf_op jit(solution)/shard_map/ppermute | solution.py:65
  7.0 1.7 shard_map.118
  8.8 6.7 %collective-permute-start.4 = (f32[80,128]{1,0:T(8,128)}, f32[80,128]{1,0:T(8,128)S(1)}, u32[]{:S(2)}, u32[]{:S(2)}) collective-permute-start(f32[80,128]{1,0:T(8,128)} %get-tuple-element.20.own_ref), channel_id=1, source_target_pairs={{0,1},{1,0},{2,3},{3,2},{4,5},{5,4},{6,7},{7,6},{8,9},{9,8},{10,11... | collective-permute-start | bytes 122888 | tf_op jit(solution)/shard_map/ppermute | solution.py:47
  15.8 3.8 %collective-permute-start = (bf16[992,640]{1,0:T(8,128)(2,1)S(1)}, bf16[992,640]{1,0:T(8,128)(2,1)S(1)}, u32[]{:S(2)}, u32[]{:S(2)}) collective-permute-start(bf16[992,640]{1,0:T(8,128)(2,1)S(1)} %fusion.1), channel_id=1, source_target_pairs={{256,0},{259,1},{258,2},{257,3},{260,4},{263,5},{262,6},{261,7},{2... | collective-permute-start | bytes 3809288 | tf_op jit(solution)/shard_map/ppermute | solution.py:65
  21.0 1.8 shard_map.119
  22.8 1.8 broadcast_in_dim.18
  24.5 3.6 %all-to-all-start = ((bf16[16,80,256]{2,1,0:T(8,128)(2,1)}), bf16[16,80,256]{2,1,0:T(8,128)(2,1)S(1)}, u32[]{:S(2)}, u32[]{:S(2)}) async-start(bf16[16,80,256]{2,1,0:T(8,128)(2,1)} %bitcast.12), calls=%async_computation | async-start | bytes 1310720 | tf_op jit(solution)/shard_map/all_to_all | solution.py:365
  28.2 2.7 %collective-permute-start.3 = (bf16[720,640]{1,0:T(8,128)(2,1)}, bf16[720,640]{1,0:T(8,128)(2,1)}, u32[]{:S(2)}, u32[]{:S(2)}) collective-permute-start(bf16[720,640]{1,0:T(8,128)(2,1)} %collective-permute-done.2.got_ref), channel_id=1, source_target_pairs={{0,1},{1,0},{2,3},{3,2},{4,5},{5,4},{6,7},{7,6},{8,9},{9,8},{10,11... | collective-permute-start | bytes 2764808 | tf_op jit(solution)/shard_map/ppermute | solution.py:47
  33.6 3.6 %collective-permute-start.5 = (f32[80,384]{1,0:T(8,128)S(1)}, f32[80,384]{1,0:T(8,128)S(1)}, u32[]{:S(2)}, u32[]{:S(2)}) collective-permute-start(f32[80,384]{1,0:T(8,128)S(1)} %pad_maximum_fusion), channel_id=1, source_target_pairs={{0,256},{32,288},{64,320},{96,352},{128,384},{160,416},{192,448},{... | collective-permute-start | bytes 368648 | tf_op jit(solution)/shard_map/ppermute | solution.py:52
  37.8 9.9 %collective-permute-start.1 = (bf16[992,640]{1,0:T(8,128)(2,1)S(1)}, bf16[992,640]{1,0:T(8,128)(2,1)S(1)}, u32[]{:S(2)}, u32[]{:S(2)}) collective-permute-start(bf16[992,640]{1,0:T(8,128)(2,1)S(1)} %collective-permute-done.got_ref), channel_id=1, source_target_pairs={{0,1},{1,0},{2,3},{3,2},{4,5},{5,4},{6,7},{7,6},{8,9},{9,8},{10,11... | collective-permute-start | bytes 3809288 | tf_op jit(solution)/shard_map/ppermute | solution.py:47
  48.6 4.6 %shard_map.120 = (f32[2,80,256]{2,1,0:T(8,128)}, bf16[176,128]{1,0:T(8,128)(2,1)}) custom-call(s32[4]{0:T(128)} %pad_add_fusion.place_ref, bf16[720,1280]{1,0:T(8,128)(2,1)} %bitcast.31, bf16[720,640]{1,0:T(8,128)(2,1)} %collective-permute-done.2.got_ref, bf16[720,640]{1,0:T(8,128)(2,1)} %collective-permute-done.3.other_ref, bf16[16,80,256]{2,1,0:T(8,128)(2,1)} %copy-done.4, ...), custom_call_target="tpu_custom_call" | custom-call | tf_op jit(solution)/shard_map/pallas_call | solution.py:369
  53.2 1.5 broadcast_in_dim.20
  54.7 3.6 %all-to-all-start.1 = ((bf16[4,176,128]{2,1,0:T(8,128)(2,1)}), bf16[4,176,128]{2,1,0:T(8,128)(2,1)S(1)}, u32[]{:S(2)}, u32[]{:S(2)}) async-start(bf16[4,176,128]{2,1,0:T(8,128)(2,1)} %broadcast_in_dim.20), calls=%async_computation.1 | async-start | bytes 360448 | tf_op jit(solution)/shard_map/all_to_all | solution.py:85
  59.8 3.0 %all-to-all-done.1.notes_ref = bf16[4,176,128]{2,1,0:T(8,128)(2,1)S(1)} async-done(((bf16[4,176,128]{2,1,0:T(8,128)(2,1)}), bf16[4,176,128]{2,1,0:T(8,128)(2,1)S(1)}, u32[]{:S(2)}, u32[]{:S(2)}) %all-to-all-start.1) | async-done | bytes 180256 | tf_op jit(solution)/shard_map/all_to_all | solution.py:85
  63.4 2.6 %shard_map.121 = bf16[2,80,256]{2,1,0:T(8,128)(2,1)} custom-call(s32[4]{0:T(128)} %pad_add_fusion.place_ref, f32[2,80,256]{2,1,0:T(8,128)} %get-tuple-element.22.part_ref, bf16[4,176,128]{2,1,0:T(8,128)(2,1)} %copy-done.6, f32[2,80,128]{2,1,0:T(8,128)} %maximum_select_fusion.gains_ref), custom_call_target="tpu_custom_call" | custom-call | tf_op jit(solution)/shard_map/pallas_call | solution.py:374
  66.1 1.8 broadcast_in_dim.21
  67.8 3.5 %all-to-all-start.2 = ((bf16[8,2,80,256]{3,2,1,0:T(8,128)(2,1)}), bf16[8,2,80,256]{3,2,1,0:T(8,128)(2,1)S(1)}, u32[]{:S(2)}, u32[]{:S(2)}) async-start(bf16[8,2,80,256]{3,2,1,0:T(8,128)(2,1)} %broadcast_in_dim.21), calls=%async_computation.2 | async-start | bytes 1310720 | tf_op jit(solution)/shard_map/all_to_all | solution.py:75
  71.4 20.7 %all-to-all-done.2.full_ref = bf16[8,2,80,256]{3,2,1,0:T(8,128)(2,1)S(1)} async-done(((bf16[8,2,80,256]{3,2,1,0:T(8,128)(2,1)}), bf16[8,2,80,256]{3,2,1,0:T(8,128)(2,1)S(1)}, u32[]{:S(2)}, u32[]{:S(2)}) %all-to-all-start.2) | async-done | bytes 655392 | tf_op jit(solution)/shard_map/all_to_all | solution.py:75
  92.9 4.8 %shard_map.122 = (f32[2,80,256]{2,1,0:T(8,128)}, bf16[176,128]{1,0:T(8,128)(2,1)}) custom-call(s32[4]{0:T(128)} %pad_add_fusion.place_ref, bf16[720,1280]{1,0:T(8,128)(2,1)} %bitcast.32, bf16[992,640]{1,0:T(8,128)(2,1)} %copy-done.1, bf16[992,640]{1,0:T(8,128)(2,1)} %copy-done.2, bf16[8,2,80,256]{3,2,1,0:T(8,128)(2,1)} %copy-done.5, ...), custom_call_target="tpu_custom_call" | custom-call | tf_op jit(solution)/shard_map/pallas_call | solution.py:369
  98.6 8.1 %all_to_all.35.notes_ref = bf16[4,176,128]{2,1,0:T(8,128)(2,1)} all-to-all(bf16[4,176,128]{2,1,0:T(8,128)(2,1)S(1)} %broadcast_in_dim.22), channel_id=1, replica_groups={{0,256,257,1},{32,288,289,33},{64,320,321,65},{96,352,353,97},{128,384,..., dimensions={0} | all-to-all | bytes 360448 | tf_op jit(solution)/shard_map/all_to_all | solution.py:85
  106.7 2.7 %shard_map.123 = (bf16[2,80,256]{2,1,0:T(8,128)(2,1)}, f32[2,80,256]{2,1,0:T(8,128)}) custom-call(s32[4]{0:T(128)} %pad_add_fusion.place_ref, f32[2,80,256]{2,1,0:T(8,128)} %get-tuple-element.25.part_ref, bf16[4,176,128]{2,1,0:T(8,128)(2,1)} %all_to_all.35.notes_ref, f32[2,80,128]{2,1,0:T(8,128)} %maximum_select_fusion.gains_ref), custom_call_target="tpu_custom_call" | custom-call | tf_op jit(solution)/shard_map/pallas_call | solution.py:374
  110.3 23.8 %all_to_all.36.full_ref = bf16[8,2,80,256]{3,2,1,0:T(8,128)(2,1)} all-to-all(bf16[8,2,80,256]{3,2,1,0:T(8,128)(2,1)S(1)} %broadcast_in_dim.23), channel_id=1, replica_groups={{0,32,64,96,128,160,192,224},{256,288,320,352,384,416,448,480},{1,33,65..., dimensions={0} | all-to-all | bytes 1310720 | tf_op jit(solution)/shard_map/all_to_all | solution.py:75
  134.1 3.2 %shard_map.124 = (bf16[2,64,256]{2,1,0:T(8,128)(2,1)}, bf16[2,128,256]{2,1,0:T(8,128)(2,1)}) custom-call(s32[4]{0:T(128)} %pad_add_fusion.place_ref, bf16[64,1280]{1,0:T(8,128)(2,1)} %query_ref.1, bf16[64,1280]{1,0:T(8,128)(2,1)} %key_ref.1, bf16[64,1280]{1,0:T(8,128)(2,1)} %value_ref.1, bf16[992,640]{1,0:T(8,128)(2,1)} %copy-done.1, ...), custom_call_target="tpu_custom_call" | custom-call | tf_op jit(solution)/shard_map/pallas_call | solution.py:384
  137.3 0.9 broadcast_in_dim.24
  138.3 11.7 %all_to_all.37.pairs_ref = bf16[4,2,128,256]{3,2,1,0:T(8,128)(2,1)} all-to-all(bf16[4,2,128,256]{3,2,1,0:T(8,128)(2,1)S(1)} %broadcast_in_dim.24), channel_id=1, replica_groups={{0,256,257,1},{32,288,289,33},{64,320,321,65},{96,352,353,97},{128,384,..., dimensions={0} | all-to-all | bytes 1048576 | tf_op jit(solution)/shard_map/all_to_all | solution.py:85
  150.0 3.5 %shard_map.125 = bf16[2,64,256]{2,1,0:T(8,128)(2,1)} custom-call(bf16[2,64,256]{2,1,0:T(8,128)(2,1)} %get-tuple-element.28.q_ref, bf16[4,2,128,256]{3,2,1,0:T(8,128)(2,1)} %all_to_all.37.pairs_ref), custom_call_target="tpu_custom_call" | custom-call | tf_op jit(solution)/shard_map/pallas_call | solution.py:390
  154.4 21.1 %all_to_all.38.full_ref = bf16[8,2,64,256]{3,2,1,0:T(8,128)(2,1)} all-to-all(bf16[8,2,64,256]{3,2,1,0:T(8,128)(2,1)S(1)} %broadcast_in_dim.25), channel_id=1, replica_groups={{0,32,64,96,128,160,192,224},{256,288,320,352,384,416,448,480},{1,33,65..., dimensions={0} | all-to-all | bytes 1048576 | tf_op jit(solution)/shard_map/all_to_all | solution.py:75
  175.4 2.9 %shard_map.126 = (bf16[80,256]{1,0:T(8,128)(2,1)}, bf16[80,256]{1,0:T(8,128)(2,1)}) custom-call(s32[4]{0:T(128)} %pad_add_fusion.place_ref, bf16[80,1024]{1,0:T(8,128)(2,1)} %weight_ref.1, bf16[992,640]{1,0:T(8,128)(2,1)} %copy-done.1, bf16[992,640]{1,0:T(8,128)(2,1)} %copy-done.2, bf16[8,2,64,256]{3,2,1,0:T(8,128)(2,1)} %all_to_all.38.full_ref, ...), custom_call_target="tpu_custom_call" | custom-call | tf_op jit(solution)/shard_map/pallas_call | solution.py:393
  178.3 2.1 %collective-permute-start.6 = (bf16[80,256]{1,0:T(8,128)(2,1)}, bf16[80,256]{1,0:T(8,128)(2,1)S(1)}, u32[]{:S(2)}, u32[]{:S(2)}) collective-permute-start(bf16[80,256]{1,0:T(8,128)(2,1)} %get-tuple-element.32), channel_id=1, source_target_pairs={{0,256},{32,288},{64,320},{96,352},{128,384},{160,416},{192,448},{... | collective-permute-start | bytes 122888 | tf_op jit(solution)/shard_map/ppermute | solution.py:52
  180.4 2.9 %collective-permute-done.6.peer_ref = bf16[80,256]{1,0:T(8,128)(2,1)S(1)} collective-permute-done((bf16[80,256]{1,0:T(8,128)(2,1)}, bf16[80,256]{1,0:T(8,128)(2,1)S(1)}, u32[]{:S(2)}, u32[]{:S(2)}) %collective-permute-start.6) | collective-permute-done | bytes 40992 | tf_op jit(solution)/shard_map/ppermute | solution.py:52
  183.9 1.6 shard_map.127
  (64 shorter events, 12.0 us)
Async XLA Ops:
  0.0 32.4 %copy-start = (bf16[320,80]{0,1:T(8,128)(2,1)S(1)}, bf16[320,80]{0,1:T(8,128)(2,1)}, u32[]{:S(2)}) copy-start(bf16[320,80]{0,1:T(8,128)(2,1)} %param.16) | copy-start | bytes 153604
  0.0 15.5 %copy-start.11 = (bf16[80,1024]{1,0:T(8,128)(2,1)S(1)}, bf16[80,1024]{1,0:T(8,128)(2,1)}, u32[]{:S(2)}) copy-start(bf16[80,1024]{1,0:T(8,128)(2,1)} %weight_ref.1) | copy-start | bytes 491524
  0.0 15.5 %copy-start.8 = (bf16[64,1280]{1,0:T(8,128)(2,1)S(1)}, bf16[64,1280]{1,0:T(8,128)(2,1)}, u32[]{:S(2)}) copy-start(bf16[64,1280]{1,0:T(8,128)(2,1)} %query_ref.1) | copy-start | bytes 491524
  0.0 15.5 %copy-start.9 = (bf16[64,1280]{1,0:T(8,128)(2,1)S(1)}, bf16[64,1280]{1,0:T(8,128)(2,1)}, u32[]{:S(2)}) copy-start(bf16[64,1280]{1,0:T(8,128)(2,1)} %key_ref.1) | copy-start | bytes 491524
  0.0 15.5 %copy-start.10 = (bf16[64,1280]{1,0:T(8,128)(2,1)S(1)}, bf16[64,1280]{1,0:T(8,128)(2,1)}, u32[]{:S(2)}) copy-start(bf16[64,1280]{1,0:T(8,128)(2,1)} %value_ref.1) | copy-start | bytes 491524
  0.0 15.5 %copy-start.3 = (bf16[80,3,3,1280]{3,0,2,1:T(8,128)(2,1)S(1)}, bf16[80,3,3,1280]{3,0,2,1:T(8,128)(2,1)}, u32[]{:S(2)}) copy-start(bf16[80,3,3,1280]{3,0,2,1:T(8,128)(2,1)} %param.18) | copy-start | bytes 5529604
  2.4 25.7 %collective-permute-start.2 = (bf16[720,640]{1,0:T(8,128)(2,1)}, bf16[720,640]{1,0:T(8,128)(2,1)}, u32[]{:S(2)}, u32[]{:S(2)}) collective-permute-start(bf16[720,640]{1,0:T(8,128)(2,1)} %constant_dynamic-slice_fusion), channel_id=1, source_target_pairs={{256,0},{259,1},{258,2},{257,3},{260,4},{263,5},{262,6},{261,7},{2... | collective-permute-start | bytes 2764808 | tf_op jit(solution)/shard_map/ppermute | solution.py:65
  8.8 11.6 %collective-permute-start.4 = (f32[80,128]{1,0:T(8,128)}, f32[80,128]{1,0:T(8,128)S(1)}, u32[]{:S(2)}, u32[]{:S(2)}) collective-permute-start(f32[80,128]{1,0:T(8,128)} %get-tuple-element.20.own_ref), channel_id=1, source_target_pairs={{0,1},{1,0},{2,3},{3,2},{4,5},{5,4},{6,7},{7,6},{8,9},{9,8},{10,11... | collective-permute-start | bytes 122888 | tf_op jit(solution)/shard_map/ppermute | solution.py:47
  15.6 4.0 %copy-start.16 = (f32[80]{0:T(128)S(1)}, f32[80]{0:T(128)}, u32[]{:S(2)}) copy-start(f32[80]{0:T(128)} %param.14) | copy-start | bytes 964
  15.8 15.0 %copy-start.17 = (s32[16]{0:T(128)S(1)}, s32[16]{0:T(128)}, u32[]{:S(2)}) copy-start(s32[16]{0:T(128)} %param.13) | copy-start | bytes 196
  15.8 16.7 %copy-start.14 = (f32[80]{0:T(128)S(1)}, f32[80]{0:T(128)}, u32[]{:S(2)}) copy-start(f32[80]{0:T(128)} %param.19) | copy-start | bytes 964
  15.8 16.7 %copy-start.15 = (f32[80]{0:T(128)S(1)}, f32[80]{0:T(128)}, u32[]{:S(2)}) copy-start(f32[80]{0:T(128)} %param.17) | copy-start | bytes 964
  15.8 22.0 %collective-permute-start = (bf16[992,640]{1,0:T(8,128)(2,1)S(1)}, bf16[992,640]{1,0:T(8,128)(2,1)S(1)}, u32[]{:S(2)}, u32[]{:S(2)}) collective-permute-start(bf16[992,640]{1,0:T(8,128)(2,1)S(1)} %fusion.1), channel_id=1, source_target_pairs={{256,0},{259,1},{258,2},{257,3},{260,4},{263,5},{262,6},{261,7},{2... | collective-permute-start | bytes 3809288 | tf_op jit(solution)/shard_map/ppermute | solution.py:65
  20.4 0.6 copy-start.13
  24.5 23.2 %all-to-all-start = ((bf16[16,80,256]{2,1,0:T(8,128)(2,1)}), bf16[16,80,256]{2,1,0:T(8,128)(2,1)S(1)}, u32[]{:S(2)}, u32[]{:S(2)}) async-start(bf16[16,80,256]{2,1,0:T(8,128)(2,1)} %bitcast.12), calls=%async_computation | async-start | bytes 1310720 | tf_op jit(solution)/shard_map/all_to_all | solution.py:365
  28.2 19.6 %collective-permute-start.3 = (bf16[720,640]{1,0:T(8,128)(2,1)}, bf16[720,640]{1,0:T(8,128)(2,1)}, u32[]{:S(2)}, u32[]{:S(2)}) collective-permute-start(bf16[720,640]{1,0:T(8,128)(2,1)} %collective-permute-done.2.got_ref), channel_id=1, source_target_pairs={{0,1},{1,0},{2,3},{3,2},{4,5},{5,4},{6,7},{7,6},{8,9},{9,8},{10,11... | collective-permute-start | bytes 2764808 | tf_op jit(solution)/shard_map/ppermute | solution.py:47
  33.6 14.2 %collective-permute-start.5 = (f32[80,384]{1,0:T(8,128)S(1)}, f32[80,384]{1,0:T(8,128)S(1)}, u32[]{:S(2)}, u32[]{:S(2)}) collective-permute-start(f32[80,384]{1,0:T(8,128)S(1)} %pad_maximum_fusion), channel_id=1, source_target_pairs={{0,256},{32,288},{64,320},{96,352},{128,384},{160,416},{192,448},{... | collective-permute-start | bytes 368648 | tf_op jit(solution)/shard_map/ppermute | solution.py:52
  37.8 15.4 %copy-start.1 = (bf16[992,640]{1,0:T(8,128)(2,1)}, bf16[992,640]{1,0:T(8,128)(2,1)S(1)}, u32[]{:S(2)}) copy-start(bf16[992,640]{1,0:T(8,128)(2,1)S(1)} %collective-permute-done.got_ref) | copy-start | bytes 3809284
  37.8 33.5 %collective-permute-start.1 = (bf16[992,640]{1,0:T(8,128)(2,1)S(1)}, bf16[992,640]{1,0:T(8,128)(2,1)S(1)}, u32[]{:S(2)}, u32[]{:S(2)}) collective-permute-start(bf16[992,640]{1,0:T(8,128)(2,1)S(1)} %collective-permute-done.got_ref), channel_id=1, source_target_pairs={{0,1},{1,0},{2,3},{3,2},{4,5},{5,4},{6,7},{7,6},{8,9},{9,8},{10,11... | collective-permute-start | bytes 3809288 | tf_op jit(solution)/shard_map/ppermute | solution.py:47
  47.8 0.7 copy-start.7
  47.8 0.9 copy-start.4
  54.7 8.1 %all-to-all-start.1 = ((bf16[4,176,128]{2,1,0:T(8,128)(2,1)}), bf16[4,176,128]{2,1,0:T(8,128)(2,1)S(1)}, u32[]{:S(2)}, u32[]{:S(2)}) async-start(bf16[4,176,128]{2,1,0:T(8,128)(2,1)} %broadcast_in_dim.20), calls=%async_computation.1 | async-start | bytes 360448 | tf_op jit(solution)/shard_map/all_to_all | solution.py:85
  62.8 0.7 copy-start.6
  67.8 24.2 %all-to-all-start.2 = ((bf16[8,2,80,256]{3,2,1,0:T(8,128)(2,1)}), bf16[8,2,80,256]{3,2,1,0:T(8,128)(2,1)S(1)}, u32[]{:S(2)}, u32[]{:S(2)}) async-start(bf16[8,2,80,256]{3,2,1,0:T(8,128)(2,1)} %broadcast_in_dim.21), calls=%async_computation.2 | async-start | bytes 1310720 | tf_op jit(solution)/shard_map/all_to_all | solution.py:75
  71.4 20.7 %copy-start.2 = (bf16[992,640]{1,0:T(8,128)(2,1)}, bf16[992,640]{1,0:T(8,128)(2,1)S(1)}, u32[]{:S(2)}) copy-start(bf16[992,640]{1,0:T(8,128)(2,1)S(1)} %collective-permute-done.1.other_ref) | copy-start | bytes 3809284
  92.1 0.8 copy-start.5
  178.3 4.9 %collective-permute-start.6 = (bf16[80,256]{1,0:T(8,128)(2,1)}, bf16[80,256]{1,0:T(8,128)(2,1)S(1)}, u32[]{:S(2)}, u32[]{:S(2)}) collective-permute-start(bf16[80,256]{1,0:T(8,128)(2,1)} %get-tuple-element.32), channel_id=1, source_target_pairs={{0,256},{32,288},{64,320},{96,352},{128,384},{160,416},{192,448},{... | collective-permute-start | bytes 122888 | tf_op jit(solution)/shard_map/ppermute | solution.py:52
  183.2 0.6 copy-start.12

commit v3 on v2

--- a/solution.py
+++ b/solution.py
@@ -21,7 +21,6 @@
 BF16 = jnp.bfloat16
 
 VM = pl.BlockSpec(memory_space=pltpu.VMEM)
-SM = pl.BlockSpec(memory_space=pltpu.SMEM)
 
 
 def call(kernel, outs, specs, scratch=()):
@@ -31,6 +30,7 @@
         in_specs=specs,
         out_specs=[VM] * len(outs),
         scratch_shapes=list(scratch),
+        compiler_params=pltpu.CompilerParams(vmem_limit_bytes=20 * 2**20),
     )
 
 
@@ -65,14 +65,28 @@
     return lax.ppermute(value, ("ch", "row"), pairs)
 
 
+def spot():
+    side = lax.axis_index("ch") // (lax.axis_size("ch") // 2)
+    core = lax.axis_index("row") % 2
+    return side, core, 2 * core + (side ^ core)
+
+
+def after(value, first):
+    return lax.optimization_barrier((value, first))[0]
+
+
 def copies(block, count):
     return jnp.broadcast_to(block[None], (count, *block.shape))
 
 
-def column_collect(block):
+def column_copies(block):
+    return copies(block, lax.axis_size("ch") // 2)
+
+
+def column_collect(spread):
     half = lax.axis_size("ch") // 2
     groups = [list(range(half)), list(range(half, 2 * half))]
-    return lax.all_to_all(copies(block, half), "ch", 0, 0, tiled=True, axis_index_groups=groups)
+    return lax.all_to_all(spread, "ch", 0, 0, tiled=True, axis_index_groups=groups)
 
 
 def image_collect(block):
@@ -106,31 +120,51 @@
     ]
 
 
-def enter_kernel(place_ref, latent_ref, turned_ref, keep_ref, send_ref, sums_ref):
+def enter_kernel(latent_ref, gain_a_ref, gain_b_ref, gain_c_ref, turned_ref, keep_ref, send_ref, sums_ref):
+    side, core, _ = spot()
     value = latent_ref[...].astype(F32).T
     turned_ref[...] = value
     half = value.shape[1] // 2
-    first = place_ref[2] == 0
+    first = side == core
     keep_ref[...] = jnp.where(first, value[:, :half], value[:, half:])
     send_ref[...] = jnp.where(first, value[:, half:], value[:, :half])
     lane = lanes(sums_ref.shape)
+    gains = [ref[...] for ref in (gain_a_ref, gain_b_ref, gain_c_ref)]
+    gains = jnp.concatenate(gains + [jnp.zeros((5, gains[0].shape[1]), F32)], axis=0).T
     total = jnp.sum(value, axis=1, keepdims=True)
     squares = jnp.sum(value * value, axis=1, keepdims=True)
-    sums_ref[...] = jnp.where(lane == 0, total, jnp.where(lane == 1, squares, 0.0))
-
-
-def first_kernel(place_ref, turned_ref, own_ref, peer_ref, gain_ref, active_ref):
+    sums = jnp.where(lane == 0, total, jnp.where(lane == 1, squares, 0.0))
+    for kind in range(3):
+        sums = jnp.where(lane == 2 + kind, gains[:, kind : kind + 1], sums)
+    sums_ref[...] = sums
+
+
+def first_kernel(turned_ref, own_ref, peer_ref, active_ref):
+    _, core, _ = spot()
     sums = own_ref[...] + peer_ref[...]
     totals, squares = by_group(sums[:, 0:1]), by_group(sums[:, 1:2])
+    gain = own_ref[:, 2:3]
     pieces = []
     for group in range(len(totals)):
         rows = slice(group * WIDE, (group + 1) * WIDE)
-        pieces.append(scaled(turned_ref[rows], totals[group], squares[group], gain_ref[rows]))
+        pieces.append(scaled(turned_ref[rows], totals[group], squares[group], gain[rows]))
     value = silu(jnp.concatenate(pieces, axis=0)).astype(BF16)
     half = value.shape[1] // 2
-    core = place_ref[1]
     active_ref[core] = value[:, :half]
     active_ref[1 - core] = value[:, half:]
+
+
+def mail_kernel(weight_ref, sinus_ref, own_ref, send_ref, vector_ref, mail_ref):
+    product = weight_ref[...].astype(F32) * sinus_ref[...].astype(F32)
+    time_add = silu(jnp.sum(product, axis=1, keepdims=True))
+    lane = lanes(vector_ref.shape)
+    vector = jnp.where(lane == 0, time_add, 0.0)
+    for kind in range(2):
+        vector = jnp.where(lane == 1 + kind, own_ref[:, 3 + kind : 4 + kind], vector)
+    vector_ref[...] = vector
+    share = send_ref.shape[1]
+    mail_ref[:, :share] = send_ref[...]
+    mail_ref[:, share:] = vector
 
 
 def gather_into(full_ref, whole_ref):
@@ -154,9 +188,9 @@
     )
 
 
-def conv_kernel(place_ref, own_ref, got_ref, other_ref, full_ref, base_ref, far_ref, part_ref, note_ref, whole_ref, *, at):
+def conv_kernel(own_ref, got_ref, other_ref, full_ref, base_ref, far_ref, part_ref, note_ref, whole_ref, *, near, far):
     _, count, tokens = part_ref.shape
-    side, core, quarter = place_ref[0], place_ref[1], place_ref[3]
+    side, core, quarter = spot()
     token = lanes((count, tokens))
     column = token % W
     lane = lanes((count, 128))
@@ -164,9 +198,9 @@
     end = jnp.where(quarter < 3, tokens - W, tokens)
     gather_into(full_ref, whole_ref)
     taps = both(core, own_ref[...], got_ref[: 9 * count], other_ref[: 9 * count], whole_ref)
-    bases = base_ref[...], far_ref[:, at]
+    bases = base_ref[:, near], far_ref[:, far]
     extra = jnp.zeros((16, 128), F32)
-    spot = lanes((16, 128))
+    extra_lane = lanes((16, 128))
     for which in range(2):
         here = side if which == 0 else 1 - side
         combined = []
@@ -199,14 +233,14 @@
                 for piece in range(3):
                     rounded = value.astype(BF16).astype(F32)
                     index = (here * len(totals) + group) * 6 + kind * 3 + piece
-                    extra = jnp.where(spot == index, rounded, extra)
+                    extra = jnp.where(extra_lane == index, rounded, extra)
                     value = value - rounded
     note_ref[2 * count :, :] = extra.astype(BF16)
 
 
-def finish_kernel(place_ref, part_ref, notes_ref, gains_ref, *outs, act, lane_of):
+def finish_kernel(part_ref, notes_ref, vector_ref, mail_ref, *outs, act, lane_of):
     _, count, tokens = part_ref.shape
-    quarter = place_ref[3]
+    mine, _, quarter = spot()
     lane = lanes((count, 128))
     sums = notes_ref[0, 2 * count :].astype(F32)
     for place in range(1, 4):
@@ -238,7 +272,8 @@
             axis=1,
         )
         totals, squared = by_group(total), by_group(squares)
-        gain = gains_ref[side][:, lane_of : lane_of + 1]
+        at = tokens + lane_of
+        gain = jnp.where(side == mine, vector_ref[:, lane_of : lane_of + 1], mail_ref[:, at : at + 1])
         pieces = []
         for group in range(len(totals)):
             first = (side * len(totals) + group) * 6
@@ -254,19 +289,17 @@
             outs[1][side] = value
 
 
-def project_kernel(place_ref, query_ref, key_ref, value_ref, got_ref, other_ref, full_ref, q_ref, kv_ref, whole_ref, stack_ref, *, at):
-    inner = query_ref.shape[0]
-    side, core = place_ref[0], place_ref[1]
-    stack_ref[:inner] = query_ref[...]
-    stack_ref[inner : 2 * inner] = key_ref[...]
-    stack_ref[2 * inner :] = value_ref[...]
+def project_kernel(*refs, at):
+    *own_refs, got_ref, other_ref, full_ref, out_ref, whole_ref, stack_ref = refs
+    inner = own_refs[0].shape[0]
+    side, core, _ = spot()
+    for index, ref in enumerate(own_refs):
+        stack_ref[index * inner : (index + 1) * inner] = ref[...]
     gather_into(full_ref, whole_ref)
-    rows = slice(at, at + 3 * inner)
+    rows = slice(at, at + len(own_refs) * inner)
     mixed = both(core, stack_ref[...], got_ref[rows], other_ref[rows], whole_ref)
     for which in range(2):
-        here = side if which == 0 else 1 - side
-        q_ref[here] = mixed[which][:inner].astype(BF16)
-        kv_ref[here] = mixed[which][inner:].astype(BF16)
+        out_ref[side if which == 0 else 1 - side] = mixed[which].astype(BF16)
 
 
 def attend_kernel(q_ref, pairs_ref, out_ref):
@@ -282,9 +315,9 @@
         out_ref[head] = jnp.dot(values, weights, preferred_element_type=F32).astype(BF16)
 
 
-def leave_kernel(place_ref, weight_ref, got_ref, other_ref, full_ref, hidden_ref, keep_ref, send_ref, whole_ref, *, at):
+def leave_kernel(weight_ref, got_ref, other_ref, full_ref, hidden_ref, keep_ref, send_ref, whole_ref, *, at):
     count, depth = weight_ref.shape
-    side, core = place_ref[0], place_ref[1]
+    side, core, _ = spot()
     gather_into(full_ref, whole_ref)
     got, other = (ref[at : at + count, : depth // 2] for ref in (got_ref, other_ref))
     mine, theirs = both(core, weight_ref[...], got, other, whole_ref)
@@ -292,9 +325,10 @@
     send_ref[...] = (hidden_ref[1 - side] + theirs).astype(BF16)
 
 
-def last_kernel(place_ref, keep_ref, peer_ref, result_ref):
+def last_kernel(keep_ref, peer_ref, result_ref):
     span = keep_ref.shape[1]
-    part = place_ref[2]
+    side, core, _ = spot()
+    part = side ^ core
     for ref, at in ((keep_ref, part), (peer_ref, 1 - part)):
         result_ref[pl.ds(pl.multiple_of(at * span, 16), span), :] = ref[...].astype(F32).T.astype(BF16)
 
@@ -317,10 +351,8 @@
     tokens = rows * width
     share = tokens // 2
     chs = lax.axis_size("ch")
-    channel, place = lax.axis_index("ch"), lax.axis_index("row")
-    side, core = channel // (chs // 2), place % 2
-    part = side ^ core
-    where = jnp.stack([side, core, part, 2 * core + part]).astype(jnp.int32)
+    place = lax.axis_index("row")
+    core = place % 2
     image_id = place // 2
     inner = w_query.shape[0]
 
@@ -336,67 +368,71 @@
     freqs = jnp.exp(-math.log(10000.0) * jnp.arange(half, dtype=F32) / half)
     angles = step_value * freqs
     sinus = jnp.concatenate([jnp.cos(angles), jnp.sin(angles)])[None, :].astype(BF16)
-    time_add = jax.nn.silu(jnp.dot(sinus, time_weight, preferred_element_type=F32))[0]
-    vector = jnp.pad(jnp.stack([time_add, norm_gain_b, norm_gain_c], axis=1), ((0, 0), (0, 125)))
-
     field = ((2, count, share), F32)
     active = ((2, count, share), BF16)
     quarter = ((count, share), F32)
     note = ((2 * count + 16, 128), BF16)
     whole = pltpu.VMEM((C, share), BF16)
 
+    gains = [gain.reshape(1, count) for gain in (norm_gain_a, norm_gain_b, norm_gain_c)]
     turned, keep, send, sums = call(
-        enter_kernel, [((count, tokens), F32), quarter, quarter, ((count, 128), F32)], [SM, VM]
-    )(where, latent.reshape(tokens, count))
-    (active_a,) = call(first_kernel, [active], [SM] + [VM] * 4)(
-        where, turned, sums, swapped(sums), norm_gain_a.reshape(count, 1)
-    )
+        enter_kernel, [((count, tokens), F32), quarter, quarter, ((count, 128), F32)], [VM] * 4
+    )(latent.reshape(tokens, count), *gains)
+    (active_a,) = call(first_kernel, [active], [VM] * 3)(turned, sums, swapped(sums))
 
     own_a, own_b = tall(conv_weight_a), tall(conv_weight_b)
-    mail = crossed(jnp.concatenate([send, vector], axis=1))
-    got_a = from_beside(halved(own_a))
-    late = jnp.concatenate([w_query, w_key, w_value], axis=0)
-    late_out = jnp.pad(halved(w_out), ((0, 0), (0, (C - w_out.shape[1]) // 2)))
-    got_b = from_beside(jnp.concatenate([halved(own_b), halved(late), late_out], axis=0))
-    theirs = mail[:, share:]
-    vectors = jnp.where(side == 0, jnp.stack([vector, theirs]), jnp.stack([theirs, vector]))
-
     spread = jnp.broadcast_to(active_a[:, None], (2, chs // 2, count, share)).reshape(chs, count, share)
     full = lax.all_to_all(spread, "ch", 0, 0, tiled=True)
+    got_a = from_beside(halved(after(own_a, spread)))
+    vector, mail = call(mail_kernel, [((count, 128), F32), ((count, share + 128), F32)], [VM] * 4)(
+        time_weight.T, sinus, sums, after(send, spread)
+    )
+    mail = crossed(mail)
     other_a = swapped(got_a)
-
-    def conv(full, own, got, other, base, at):
+    qkv = jnp.concatenate([w_query, w_key, w_value], axis=0)
+    late_b, late, late_out, _ = lax.optimization_barrier((own_b, qkv, w_out, got_a))
+    late_out = jnp.pad(halved(late_out), ((0, 0), (0, (C - w_out.shape[1]) // 2)))
+    got_b = from_beside(jnp.concatenate([halved(late_b), halved(late), late_out], axis=0))
+
+    def conv(full, own, got, other, base, near, far):
         return call(
-            functools.partial(conv_kernel, at=at), [field, note], [SM] + [VM] * 6, [whole]
-        )(where, own, got, other, full, base, mail)
+            functools.partial(conv_kernel, near=near, far=far), [field, note], [VM] * 6, [whole]
+        )(own, got, other, full, base, mail)
 
     def finish(part, note, act, lane_of, outs):
         return call(
-            functools.partial(finish_kernel, act=act, lane_of=lane_of), outs, [SM] + [VM] * 3
-        )(where, part, image_collect(note), vectors)
-
-    part_a, note_a = conv(full, own_a, got_a, other_a, vector[:, 0:1], slice(share, share + 1))
+            functools.partial(finish_kernel, act=act, lane_of=lane_of), outs, [VM] * 4
+        )(part, image_collect(note), vector, mail)
+
+    part_a, note_a = conv(full, own_a, got_a, other_a, vector, slice(0, 1), slice(share, share + 1))
     (active_b,) = finish(part_a, note_a, True, 1, [active])
-    other_b = swapped(got_b)
-    part_b, note_b = conv(column_collect(active_b), own_b, got_b, other_b, keep, slice(0, share))
+    spread_b = column_copies(active_b)
+    other_b = swapped(after(got_b, spread_b))
+    part_b, note_b = conv(
+        column_collect(spread_b), own_b, got_b, other_b, keep, slice(0, share), slice(0, share)
+    )
     normed, hidden_b = finish(part_b, note_b, False, 2, [active, field])
 
-    query, key_value = call(
-        functools.partial(project_kernel, at=9 * count),
-        [((2, inner, share), BF16), ((2, 2 * inner, share), BF16)],
-        [SM] + [VM] * 6,
-        [whole, pltpu.VMEM((3 * inner, C), BF16)],
-    )(where, w_query, w_key, w_value, got_b, other_b, column_collect(normed))
-    (heads_out,) = call(attend_kernel, [((2, inner, share), BF16)], [VM] * 2)(
-        query, image_collect(key_value)
-    )
+    features = column_collect(column_copies(normed))
+
+    def project(weights, at):
+        return call(
+            functools.partial(project_kernel, at=at),
+            [((2, len(weights) * inner, share), BF16)],
+            [VM] * (len(weights) + 3),
+            [whole, pltpu.VMEM((len(weights) * inner, C), BF16)],
+        )(*weights, got_b, other_b, features)[0]
+
+    pairs = image_collect(project([w_key, w_value], 9 * count + inner))
+    query = project([w_query], 9 * count)
+    (heads_out,) = call(attend_kernel, [((2, inner, share), BF16)], [VM] * 2)(query, pairs)
     kept, sent = call(
         functools.partial(leave_kernel, at=9 * count + 3 * inner),
         [((count, share), BF16)] * 2,
-        [SM] + [VM] * 5,
+        [VM] * 5,
         [pltpu.VMEM((w_out.shape[1], share), BF16)],
-    )(where, w_out, got_b, other_b, column_collect(heads_out), hidden_b)
-    (result,) = call(last_kernel, [((tokens, count), BF16)], [SM] + [VM] * 2)(where, kept, crossed(sent))
+    )(w_out, got_b, other_b, column_collect(column_copies(heads_out)), hidden_b)
+    (result,) = call(last_kernel, [((tokens, count), BF16)], [VM] * 2)(kept, crossed(sent))
     return result.reshape(rows, width, count)
 
 

time: 187 us -> 177 us (0.947)
  blocking collectives: 64.8 us -> 86.1 us
  Pallas kernels: 29.4 us -> 12 us
  starting transfers between devices: 43.3 us -> 35.4 us
  local copies, waits for them, and re-layouts: 17 us -> 12 us
    all_to_all x2 -> x3, blocking collectives: 44.9 us -> 66.7 us  [column_collect(): lax.all_to_all(spread, 'ch', 0, 0, tiled=True, axis_index_groups=groups)]
    all_to_all x1 -> x0, waiting for transfers between devices: 20.7 us -> none  [column_collect(): lax.all_to_all(copies(block, half), 'ch', 0, 0, tiled=True, axis_index_gr...]
    pallas_call x8 -> x10, Pallas kernels: 24.8 us -> 11.5 us  [the longest x2 4.87 us: conv(): call(functools.partial(conv_kernel, near=near, far=far), [field, note], [...]
    ppermute x2, waiting for transfers between devices: 0.01 us -> 9.23 us  [from_beside(): return lax.ppermute(value, ('ch', 'row'), pairs)]
    ppermute x2, waiting for transfers between devices: 2.89 us -> 9.93 us  [crossed(): lax.ppermute(value, 'ch', [(k, (k + chs // 2) % chs) for k in range(chs)])]
    broadcast_in_dim x6, local copies, waits for them, and re-layouts: 6.82 us -> 1.05 us  [copies(): return jnp.broadcast_to(block[None], (count, *block.shape))]
    ppermute x3, starting transfers between devices: 19.3 us -> 14.7 us  [swapped(): return lax.ppermute(value, ('ch', 'row'), core_pairs())]
    all_to_all x1, waiting for transfers between devices: 3.02 us -> 6.91 us  [image_collect(): lax.all_to_all(copies(block, 4), ('ch', 'row'), 0, 0, tiled=True, axis_in...]
  transfers between devices with their start and end apart: 10 -> 9, of which waited for: 3 -> 5; matrix products, arithmetic and copies ran while one was open for 6% -> 2% of each run, Pallas kernels for 6% -> 3%
where the time goes in v3:
time: 177 us; the launch traced here: 176 us
  blocking collectives  86.1 us (49%)
  starting transfers between devices  35.4 us (20%)
  waiting for transfers between devices  26.9 us (15%)
  local copies, waits for them, and re-layouts  12 us (7%)
  Pallas kernels  12 us (7%)
  other arithmetic  2.77 us (2%)
    all_to_all x3, blocking collectives, column_collect(): lax.all_to_all(spread, 'ch', 0, 0, tiled=True, axis_index_groups=groups)  66.7 us
    all_to_all x2, blocking collectives, image_collect(): lax.all_to_all(copies(block, 4), ('ch', 'row'), 0, 0, tiled=True, axis_in...  19.4 us
    ppermute x3, starting transfers between devices, swapped(): return lax.ppermute(value, ('ch', 'row'), core_pairs())  14.7 us
    ppermute x2, waiting for transfers between devices, crossed(): lax.ppermute(value, 'ch', [(k, (k + chs // 2) % chs) for k in range(chs)])  9.93 us
    ppermute x2, waiting for transfers between devices, from_beside(): return lax.ppermute(value, ('ch', 'row'), pairs)  9.23 us
    all_to_all x1, waiting for transfers between devices, image_collect(): lax.all_to_all(copies(block, 4), ('ch', 'row'), 0, 0, tiled=True, axis_in...  6.91 us
    unnamed x40, local copies, waits for them, and re-layouts  6.55 us
    ppermute x2, starting transfers between devices, from_beside(): return lax.ppermute(value, ('ch', 'row'), pairs)  6.16 us
  transfers between devices with their start and end apart: 9, of which 5 were waited for; matrix products, arithmetic and copies ran while one was open for 2% of the time, Pallas kernels for 3%

profile of v3, /device:TPU:1, one launch (start us, length us, event | category | flops | bytes accessed | tf_op | source)
XLA Modules:
  0.0 176.3 jit_solution(13083191880700723145)
XLA Ops:
  0.0 1.0 copy-done.14
  3.2 8.7 %collective-permute-start = (f32[80,128]{1,0:T(8,128)S(1)}, f32[80,128]{1,0:T(8,128)S(1)}, u32[]{:S(2)}, u32[]{:S(2)}) collective-permute-start(f32[80,128]{1,0:T(8,128)S(1)} %get-tuple-element.26.own_ref), channel_id=1, source_target_pairs={{0,1},{1,0},{2,3},{3,2},{4,5},{5,4},{6,7},{7,6},{8,9},{9,8},{10,11... | collective-permute-start | bytes 122888 | tf_op jit(solution)/shard_map/ppermute | solution.py:47
  13.0 0.9 broadcast_in_dim.18
  13.9 2.2 %constant_dynamic-slice_fusion.3 = bf16[720,640]{1,0:T(8,128)(2,1)} fusion(bf16[720,1280]{1,0:T(8,128)(2,1)} %bitcast.13, s32[]{:T(128)S(6)} %select_n.24), kind=kLoop, calls=%fused_computation.12 | loop fusion | bytes 1843204 | tf_op jit(solution)/shard_map/dynamic_slice | solution.py:364
  16.1 2.0 %collective-permute-start.1 = (bf16[720,640]{1,0:T(8,128)(2,1)}, bf16[720,640]{1,0:T(8,128)(2,1)S(1)}, u32[]{:S(2)}, u32[]{:S(2)}) collective-permute-start(bf16[720,640]{1,0:T(8,128)(2,1)} %constant_dynamic-slice_fusion.3), channel_id=1, source_target_pairs={{256,0},{259,1},{258,2},{257,3},{260,4},{263,5},{262,6},{261,7},{2... | collective-permute-start | bytes 2764808 | tf_op jit(solution)/shard_map/ppermute | solution.py:65
  18.2 0.8 pad_maximum_fusion
  19.0 4.3 %all-to-all-start = ((bf16[16,80,256]{2,1,0:T(8,128)(2,1)}), bf16[16,80,256]{2,1,0:T(8,128)(2,1)}, u32[]{:S(2)}, u32[]{:S(2)}) async-start(bf16[16,80,256]{2,1,0:T(8,128)(2,1)} %bitcast.22), calls=%async_computation | async-start | bytes 1310720 | tf_op jit(solution)/shard_map/all_to_all | solution.py:385
  23.3 9.2 %collective-permute-done.1.got_ref = bf16[720,640]{1,0:T(8,128)(2,1)S(1)} collective-permute-done((bf16[720,640]{1,0:T(8,128)(2,1)}, bf16[720,640]{1,0:T(8,128)(2,1)S(1)}, u32[]{:S(2)}, u32[]{:S(2)}) %collective-permute-start.1) | collective-permute-done | bytes 921632 | tf_op jit(solution)/shard_map/ppermute | solution.py:65
  32.6 1.2 constant_dynamic-slice_fusion.1
  34.0 1.2 fusion.1
  35.1 4.1 %collective-permute-start.2 = (bf16[992,640]{1,0:T(8,128)(2,1)}, bf16[992,640]{1,0:T(8,128)(2,1)S(1)}, u32[]{:S(2)}, u32[]{:S(2)}) collective-permute-start(bf16[992,640]{1,0:T(8,128)(2,1)} %fusion.1), channel_id=1, source_target_pairs={{256,0},{259,1},{258,2},{257,3},{260,4},{263,5},{262,6},{261,7},{2... | collective-permute-start | bytes 3809288 | tf_op jit(solution)/shard_map/ppermute | solution.py:65
  39.3 3.6 %collective-permute-start.3 = (bf16[720,640]{1,0:T(8,128)(2,1)}, bf16[720,640]{1,0:T(8,128)(2,1)}, u32[]{:S(2)}, u32[]{:S(2)}) collective-permute-start(bf16[720,640]{1,0:T(8,128)(2,1)} %copy-done.3), channel_id=1, source_target_pairs={{0,1},{1,0},{2,3},{3,2},{4,5},{5,4},{6,7},{7,6},{8,9},{9,8},{10,11... | collective-permute-start | bytes 2764808 | tf_op jit(solution)/shard_map/ppermute | solution.py:47
  45.3 3.6 %collective-permute-start.4 = (f32[80,384]{1,0:T(8,128)S(1)}, f32[80,384]{1,0:T(8,128)S(1)}, u32[]{:S(2)}, u32[]{:S(2)}) collective-permute-start(f32[80,384]{1,0:T(8,128)S(1)} %get-tuple-element.34), channel_id=1, source_target_pairs={{0,256},{32,288},{64,320},{96,352},{128,384},{160,416},{192,448},{... | collective-permute-start | bytes 368648 | tf_op jit(solution)/shard_map/ppermute | solution.py:52
  49.0 7.2 %collective-permute-done.4.far_ref.mail_ref = f32[80,384]{1,0:T(8,128)S(1)} collective-permute-done((f32[80,384]{1,0:T(8,128)S(1)}, f32[80,384]{1,0:T(8,128)S(1)}, u32[]{:S(2)}, u32[]{:S(2)}) %collective-permute-start.4) | collective-permute-done | bytes 122912 | tf_op jit(solution)/shard_map/ppermute | solution.py:52
  56.2 1.2 copy-done.4
  57.4 3.1 %shard_map.121 = (f32[2,80,256]{2,1,0:T(8,128)S(1)}, bf16[176,128]{1,0:T(8,128)(2,1)S(1)}) custom-call(bf16[720,1280]{1,0:T(8,128)(2,1)S(1)} %bitcast.14, bf16[720,640]{1,0:T(8,128)(2,1)S(1)} %copy-done.4, bf16[720,640]{1,0:T(8,128)(2,1)} %collective-permute-done.3.other_ref, bf16[16,80,256]{2,1,0:T(8,128)(2,1)} %all-to-all-done.full_ref, ...), custom_call_target="tpu_custom_call" | custom-call | tf_op jit(solution)/shard_map/pallas_call | solution.py:398
  60.6 11.8 %all_to_all.35.notes_ref = bf16[4,176,128]{2,1,0:T(8,128)(2,1)S(1)} all-to-all(bf16[4,176,128]{2,1,0:T(8,128)(2,1)S(1)} %broadcast_in_dim.20), channel_id=1, replica_groups={{0,256,257,1},{32,288,289,33},{64,320,321,65},{96,352,353,97},{128,384,..., dimensions={0} | all-to-all | bytes 360448 | tf_op jit(solution)/shard_map/all_to_all | solution.py:99
  72.4 0.9 shard_map.122
  73.4 2.3 %collective-permute-start.5 = (bf16[992,640]{1,0:T(8,128)(2,1)S(1)}, bf16[992,640]{1,0:T(8,128)(2,1)S(1)}, u32[]{:S(2)}, u32[]{:S(2)}) collective-permute-start(bf16[992,640]{1,0:T(8,128)(2,1)S(1)} %collective-permute-done.2.got_ref.refs_1_.refs_2_), channel_id=1, source_target_pairs={{0,1},{1,0},{2,3},{3,2},{4,5},{5,4},{6,7},{7,6},{8,9},{9,8},{10,11... | collective-permute-start | bytes 3809288 | tf_op jit(solution)/shard_map/ppermute | solution.py:47
  75.7 23.2 %all_to_all.36.full_ref = bf16[8,2,80,256]{3,2,1,0:T(8,128)(2,1)S(1)} all-to-all(bf16[8,2,80,256]{3,2,1,0:T(8,128)(2,1)S(1)} %broadcast_in_dim.21), channel_id=1, replica_groups={{0,32,64,96,128,160,192,224},{256,288,320,352,384,416,448,480},{1,33,65..., dimensions={0} | all-to-all | bytes 1310720 | tf_op jit(solution)/shard_map/all_to_all | solution.py:89
  98.9 1.8 shard_map.123
  100.7 7.5 %all_to_all.37.notes_ref = bf16[4,176,128]{2,1,0:T(8,128)(2,1)S(1)} all-to-all(bf16[4,176,128]{2,1,0:T(8,128)(2,1)S(1)} %broadcast_in_dim.22), channel_id=1, replica_groups={{0,256,257,1},{32,288,289,33},{64,320,321,65},{96,352,353,97},{128,384,..., dimensions={0} | all-to-all | bytes 360448 | tf_op jit(solution)/shard_map/all_to_all | solution.py:99
  108.3 0.9 shard_map.124
  109.9 23.1 %all_to_all.38.refs_3_.refs_4_ = bf16[8,2,80,256]{3,2,1,0:T(8,128)(2,1)S(1)} all-to-all(bf16[8,2,80,256]{3,2,1,0:T(8,128)(2,1)S(1)} %broadcast_in_dim.23), channel_id=1, replica_groups={{0,32,64,96,128,160,192,224},{256,288,320,352,384,416,448,480},{1,33,65..., dimensions={0} | all-to-all | bytes 1310720 | tf_op jit(solution)/shard_map/all_to_all | solution.py:89
  133.5 0.9 broadcast_in_dim.24
  134.3 4.6 %all-to-all-start.5 = ((bf16[4,2,128,256]{3,2,1,0:T(8,128)(2,1)}), bf16[4,2,128,256]{3,2,1,0:T(8,128)(2,1)}, u32[]{:S(2)}, u32[]{:S(2)}) async-start(bf16[4,2,128,256]{3,2,1,0:T(8,128)(2,1)} %broadcast_in_dim.24), calls=%async_computation.5 | async-start | bytes 1048576 | tf_op jit(solution)/shard_map/all_to_all | solution.py:99
  139.0 0.9 copy-done.9
  140.3 6.9 %all-to-all-done.5.pairs_ref = bf16[4,2,128,256]{3,2,1,0:T(8,128)(2,1)} async-done(((bf16[4,2,128,256]{3,2,1,0:T(8,128)(2,1)}), bf16[4,2,128,256]{3,2,1,0:T(8,128)(2,1)}, u32[]{:S(2)}, u32[]{:S(2)}) %all-to-all-start.5) | async-done | bytes 524320 | tf_op jit(solution)/shard_map/all_to_all | solution.py:99
  147.2 2.8 %shard_map.127 = bf16[2,64,256]{2,1,0:T(8,128)(2,1)S(1)} custom-call(bf16[2,64,256]{2,1,0:T(8,128)(2,1)S(1)} %shard_map.125.q_ref, bf16[4,2,128,256]{3,2,1,0:T(8,128)(2,1)} %all-to-all-done.5.pairs_ref), custom_call_target="tpu_custom_call" | custom-call | tf_op jit(solution)/shard_map/pallas_call | solution.py:428
  150.1 20.4 %all_to_all.39.full_ref = bf16[8,2,64,256]{3,2,1,0:T(8,128)(2,1)S(1)} all-to-all(bf16[8,2,64,256]{3,2,1,0:T(8,128)(2,1)S(1)} %broadcast_in_dim.25), channel_id=1, replica_groups={{0,32,64,96,128,160,192,224},{256,288,320,352,384,416,448,480},{1,33,65..., dimensions={0} | all-to-all | bytes 1048576 | tf_op jit(solution)/shard_map/all_to_all | solution.py:89
  170.8 2.0 %collective-permute-start.6 = (bf16[80,256]{1,0:T(8,128)(2,1)S(1)}, bf16[80,256]{1,0:T(8,128)(2,1)S(1)}, u32[]{:S(2)}, u32[]{:S(2)}) collective-permute-start(bf16[80,256]{1,0:T(8,128)(2,1)S(1)} %get-tuple-element.44), channel_id=1, source_target_pairs={{0,256},{32,288},{64,320},{96,352},{128,384},{160,416},{192,448},{... | collective-permute-start | bytes 122888 | tf_op jit(solution)/shard_map/ppermute | solution.py:52
  172.8 2.7 %collective-permute-done.6.peer_ref = bf16[80,256]{1,0:T(8,128)(2,1)S(1)} collective-permute-done((bf16[80,256]{1,0:T(8,128)(2,1)S(1)}, bf16[80,256]{1,0:T(8,128)(2,1)S(1)}, u32[]{:S(2)}, u32[]{:S(2)}) %collective-permute-start.6) | collective-permute-done | bytes 40992 | tf_op jit(solution)/shard_map/ppermute | solution.py:52
  (61 shorter events, 7.9 us)
Async XLA Ops:
  0.0 18.2 %copy-start.5 = (bf16[64,1280]{1,0:T(8,128)(2,1)S(1)}, bf16[64,1280]{1,0:T(8,128)(2,1)}, u32[]{:S(2)}) copy-start(bf16[64,1280]{1,0:T(8,128)(2,1)} %refs_1_.1) | copy-start | bytes 491524
  0.0 18.2 %copy-start.6 = (bf16[64,1280]{1,0:T(8,128)(2,1)S(1)}, bf16[64,1280]{1,0:T(8,128)(2,1)}, u32[]{:S(2)}) copy-start(bf16[64,1280]{1,0:T(8,128)(2,1)} %refs_0_.3) | copy-start | bytes 491524
  0.0 18.2 %copy-start.8 = (bf16[64,1280]{1,0:T(8,128)(2,1)S(1)}, bf16[64,1280]{1,0:T(8,128)(2,1)}, u32[]{:S(2)}) copy-start(bf16[64,1280]{1,0:T(8,128)(2,1)} %refs_0_.2) | copy-start | bytes 491524
  0.0 1.0 copy-start.14
  1.0 0.7 copy-start.16
  1.6 0.7 copy-start.17
  2.3 0.7 copy-start.18
  3.2 9.6 %collective-permute-start = (f32[80,128]{1,0:T(8,128)S(1)}, f32[80,128]{1,0:T(8,128)S(1)}, u32[]{:S(2)}, u32[]{:S(2)}) collective-permute-start(f32[80,128]{1,0:T(8,128)S(1)} %get-tuple-element.26.own_ref), channel_id=1, source_target_pairs={{0,1},{1,0},{2,3},{3,2},{4,5},{5,4},{6,7},{7,6},{8,9},{9,8},{10,11... | collective-permute-start | bytes 122888 | tf_op jit(solution)/shard_map/ppermute | solution.py:47
  16.1 17.7 %copy-start.1 = (bf16[80,3,3,1280]{3,0,2,1:T(8,128)(2,1)S(1)}, bf16[80,3,3,1280]{3,0,2,1:T(8,128)(2,1)}, u32[]{:S(2)}) copy-start(bf16[80,3,3,1280]{3,0,2,1:T(8,128)(2,1)} %param.18) | copy-start | bytes 5529604
  16.1 16.4 %collective-permute-start.1 = (bf16[720,640]{1,0:T(8,128)(2,1)}, bf16[720,640]{1,0:T(8,128)(2,1)S(1)}, u32[]{:S(2)}, u32[]{:S(2)}) collective-permute-start(bf16[720,640]{1,0:T(8,128)(2,1)} %constant_dynamic-slice_fusion.3), channel_id=1, source_target_pairs={{256,0},{259,1},{258,2},{257,3},{260,4},{263,5},{262,6},{261,7},{2... | collective-permute-start | bytes 2764808 | tf_op jit(solution)/shard_map/ppermute | solution.py:65
  19.0 37.2 %all-to-all-start = ((bf16[16,80,256]{2,1,0:T(8,128)(2,1)}), bf16[16,80,256]{2,1,0:T(8,128)(2,1)}, u32[]{:S(2)}, u32[]{:S(2)}) async-start(bf16[16,80,256]{2,1,0:T(8,128)(2,1)} %bitcast.22), calls=%async_computation | async-start | bytes 1310720 | tf_op jit(solution)/shard_map/all_to_all | solution.py:385
  23.3 10.6 %copy-start.10 = (bf16[80,1024]{1,0:T(8,128)(2,1)S(1)}, bf16[80,1024]{1,0:T(8,128)(2,1)}, u32[]{:S(2)}) copy-start(bf16[80,1024]{1,0:T(8,128)(2,1)} %weight_ref.1) | copy-start | bytes 491524
  32.5 1.2 copy-start.3
  33.8 9.1 %copy-start.19 = (s32[16]{0:T(128)S(1)}, s32[16]{0:T(128)}, u32[]{:S(2)}) copy-start(s32[16]{0:T(128)} %param.13) | copy-start | bytes 196
  33.9 22.3 %copy-start = (bf16[80,3,3,1280]{3,0,2,1:T(8,128)(2,1)S(1)}, bf16[80,3,3,1280]{3,0,2,1:T(8,128)(2,1)}, u32[]{:S(2)}) copy-start(bf16[80,3,3,1280]{3,0,2,1:T(8,128)(2,1)} %param.15) | copy-start | bytes 5529604
  35.1 38.2 %collective-permute-start.2 = (bf16[992,640]{1,0:T(8,128)(2,1)}, bf16[992,640]{1,0:T(8,128)(2,1)S(1)}, u32[]{:S(2)}, u32[]{:S(2)}) collective-permute-start(bf16[992,640]{1,0:T(8,128)(2,1)} %fusion.1), channel_id=1, source_target_pairs={{256,0},{259,1},{258,2},{257,3},{260,4},{263,5},{262,6},{261,7},{2... | collective-permute-start | bytes 3809288 | tf_op jit(solution)/shard_map/ppermute | solution.py:65
  39.3 17.0 %collective-permute-start.3 = (bf16[720,640]{1,0:T(8,128)(2,1)}, bf16[720,640]{1,0:T(8,128)(2,1)}, u32[]{:S(2)}, u32[]{:S(2)}) collective-permute-start(bf16[720,640]{1,0:T(8,128)(2,1)} %copy-done.3), channel_id=1, source_target_pairs={{0,1},{1,0},{2,3},{3,2},{4,5},{5,4},{6,7},{7,6},{8,9},{9,8},{10,11... | collective-permute-start | bytes 2764808 | tf_op jit(solution)/shard_map/ppermute | solution.py:47
  44.4 0.8 copy-start.15
  45.3 10.9 %collective-permute-start.4 = (f32[80,384]{1,0:T(8,128)S(1)}, f32[80,384]{1,0:T(8,128)S(1)}, u32[]{:S(2)}, u32[]{:S(2)}) collective-permute-start(f32[80,384]{1,0:T(8,128)S(1)} %get-tuple-element.34), channel_id=1, source_target_pairs={{0,256},{32,288},{64,320},{96,352},{128,384},{160,416},{192,448},{... | collective-permute-start | bytes 368648 | tf_op jit(solution)/shard_map/ppermute | solution.py:52
  56.2 1.2 copy-start.4
  60.5 38.4 %copy-start.2 = (bf16[80,3,3,1280]{3,0,2,1:T(8,128)(2,1)S(1)}, bf16[80,3,3,1280]{3,0,2,1:T(8,128)(2,1)}, u32[]{:S(2)}) copy-start(bf16[80,3,3,1280]{3,0,2,1:T(8,128)(2,1)} %param.18) | copy-start | bytes 5529604
  73.4 25.5 %collective-permute-start.5 = (bf16[992,640]{1,0:T(8,128)(2,1)S(1)}, bf16[992,640]{1,0:T(8,128)(2,1)S(1)}, u32[]{:S(2)}, u32[]{:S(2)}) collective-permute-start(bf16[992,640]{1,0:T(8,128)(2,1)S(1)} %collective-permute-done.2.got_ref.refs_1_.refs_2_), channel_id=1, source_target_pairs={{0,1},{1,0},{2,3},{3,2},{4,5},{5,4},{6,7},{7,6},{8,9},{9,8},{10,11... | collective-permute-start | bytes 3809288 | tf_op jit(solution)/shard_map/ppermute | solution.py:47
  100.7 32.4 %copy-start.7 = (bf16[64,1280]{1,0:T(8,128)(2,1)S(1)}, bf16[64,1280]{1,0:T(8,128)(2,1)}, u32[]{:S(2)}) copy-start(bf16[64,1280]{1,0:T(8,128)(2,1)} %refs_0_.3) | copy-start | bytes 491524
  109.2 0.7 copy-start.12
  134.3 12.8 %all-to-all-start.5 = ((bf16[4,2,128,256]{3,2,1,0:T(8,128)(2,1)}), bf16[4,2,128,256]{3,2,1,0:T(8,128)(2,1)}, u32[]{:S(2)}, u32[]{:S(2)}) async-start(bf16[4,2,128,256]{3,2,1,0:T(8,128)(2,1)} %broadcast_in_dim.24), calls=%async_computation.5 | async-start | bytes 1048576 | tf_op jit(solution)/shard_map/all_to_all | solution.py:99
  139.0 0.9 copy-start.9
  140.3 30.2 %copy-start.11 = (bf16[80,1024]{1,0:T(8,128)(2,1)S(1)}, bf16[80,1024]{1,0:T(8,128)(2,1)}, u32[]{:S(2)}) copy-start(bf16[80,1024]{1,0:T(8,128)(2,1)} %weight_ref.1) | copy-start | bytes 491524
  140.3 30.2 %copy-start.13 = (f32[2,80,256]{2,1,0:T(8,128)S(1)}, f32[2,80,256]{2,1,0:T(8,128)}, u32[]{:S(2)}) copy-start(f32[2,80,256]{2,1,0:T(8,128)} %copy-done.12) | copy-start | bytes 491524
  170.8 4.7 %collective-permute-start.6 = (bf16[80,256]{1,0:T(8,128)(2,1)S(1)}, bf16[80,256]{1,0:T(8,128)(2,1)S(1)}, u32[]{:S(2)}, u32[]{:S(2)}) collective-permute-start(bf16[80,256]{1,0:T(8,128)(2,1)S(1)} %get-tuple-element.44), channel_id=1, source_target_pairs={{0,256},{32,288},{64,320},{96,352},{128,384},{160,416},{192,448},{... | collective-permute-start | bytes 122888 | tf_op jit(solution)/shard_map/ppermute | solution.py:52

commit v4 on v3

--- a/solution.py
+++ b/solution.py
@@ -7,6 +7,7 @@
 from jax.experimental import pallas as pl
 from jax.experimental.pallas import tpu as pltpu
 from jax.sharding import PartitionSpec as P
+
 
 C = 1280
 GROUPS = 32
@@ -21,6 +22,7 @@
 BF16 = jnp.bfloat16
 
 VM = pl.BlockSpec(memory_space=pltpu.VMEM)
+FAR = pl.BlockSpec(memory_space=pltpu.HBM)
 
 
 def call(kernel, outs, specs, scratch=()):
@@ -120,7 +122,7 @@
     ]
 
 
-def enter_kernel(latent_ref, gain_a_ref, gain_b_ref, gain_c_ref, turned_ref, keep_ref, send_ref, sums_ref):
+def enter_kernel(latent_ref, turned_ref, keep_ref, send_ref, sums_ref):
     side, core, _ = spot()
     value = latent_ref[...].astype(F32).T
     turned_ref[...] = value
@@ -129,21 +131,28 @@
     keep_ref[...] = jnp.where(first, value[:, :half], value[:, half:])
     send_ref[...] = jnp.where(first, value[:, half:], value[:, :half])
     lane = lanes(sums_ref.shape)
-    gains = [ref[...] for ref in (gain_a_ref, gain_b_ref, gain_c_ref)]
-    gains = jnp.concatenate(gains + [jnp.zeros((5, gains[0].shape[1]), F32)], axis=0).T
     total = jnp.sum(value, axis=1, keepdims=True)
     squares = jnp.sum(value * value, axis=1, keepdims=True)
-    sums = jnp.where(lane == 0, total, jnp.where(lane == 1, squares, 0.0))
-    for kind in range(3):
-        sums = jnp.where(lane == 2 + kind, gains[:, kind : kind + 1], sums)
-    sums_ref[...] = sums
-
-
-def first_kernel(turned_ref, own_ref, peer_ref, active_ref):
+    sums_ref[...] = jnp.where(lane == 0, total, jnp.where(lane == 1, squares, 0.0))
+
+
+def upright(rows):
+    return jnp.concatenate(rows + [jnp.zeros((8 - len(rows), rows[0].shape[1]), F32)], axis=0).T
+
+
+def half_kernel(weight_ref, out_ref, sem):
+    _, core, _ = spot()
+    depth = out_ref.shape[1]
+    copy = pltpu.make_async_copy(weight_ref.at[:, pl.ds(pl.multiple_of(core * depth, 128), depth)], out_ref, sem)
+    copy.start()
+    copy.wait()
+
+
+def first_kernel(turned_ref, own_ref, peer_ref, gain_ref, active_ref):
     _, core, _ = spot()
     sums = own_ref[...] + peer_ref[...]
     totals, squares = by_group(sums[:, 0:1]), by_group(sums[:, 1:2])
-    gain = own_ref[:, 2:3]
+    gain = upright([gain_ref[...]])[:, 0:1]
     pieces = []
     for group in range(len(totals)):
         rows = slice(group * WIDE, (group + 1) * WIDE)
@@ -154,13 +163,14 @@
     active_ref[1 - core] = value[:, half:]
 
 
-def mail_kernel(weight_ref, sinus_ref, own_ref, send_ref, vector_ref, mail_ref):
+def mail_kernel(weight_ref, sinus_ref, gain_b_ref, gain_c_ref, send_ref, vector_ref, mail_ref):
     product = weight_ref[...].astype(F32) * sinus_ref[...].astype(F32)
     time_add = silu(jnp.sum(product, axis=1, keepdims=True))
     lane = lanes(vector_ref.shape)
+    gains = upright([gain_b_ref[...], gain_c_ref[...]])
     vector = jnp.where(lane == 0, time_add, 0.0)
     for kind in range(2):
-        vector = jnp.where(lane == 1 + kind, own_ref[:, 3 + kind : 4 + kind], vector)
+        vector = jnp.where(lane == 1 + kind, gains[:, kind : kind + 1], vector)
     vector_ref[...] = vector
     share = send_ref.shape[1]
     mail_ref[:, :share] = send_ref[...]
@@ -178,26 +188,29 @@
             whole_ref[at : at + count] = full_ref[peer, side]
 
 
-def both(core, own, got, other, whole_ref):
-    depth = got.shape[1]
+def both(own, gots, whole_ref):
+    mine = jnp.dot(own, whole_ref[...], preferred_element_type=F32)
+    if len(gots) == 1:
+        return mine, jnp.dot(gots[0], whole_ref[...], preferred_element_type=F32)
+    _, core, _ = spot()
+    depth = gots[0].shape[1]
     near = whole_ref[pl.ds(pl.multiple_of(core * depth, 128), depth), :]
     far = whole_ref[pl.ds(pl.multiple_of((1 - core) * depth, 128), depth), :]
-    return (
-        jnp.dot(own, whole_ref[...], preferred_element_type=F32),
-        jnp.dot(got, near, preferred_element_type=F32) + jnp.dot(other, far, preferred_element_type=F32),
-    )
-
-
-def conv_kernel(own_ref, got_ref, other_ref, full_ref, base_ref, far_ref, part_ref, note_ref, whole_ref, *, near, far):
+    theirs = jnp.dot(gots[0], near, preferred_element_type=F32)
+    return mine, theirs + jnp.dot(gots[1], far, preferred_element_type=F32)
+
+
+def conv_kernel(own_ref, *refs, near, far):
+    *got_refs, full_ref, base_ref, far_ref, part_ref, note_ref, whole_ref = refs
     _, count, tokens = part_ref.shape
-    side, core, quarter = spot()
+    side, _, quarter = spot()
     token = lanes((count, tokens))
     column = token % W
     lane = lanes((count, 128))
     begin = jnp.where(quarter > 0, W, 0)
     end = jnp.where(quarter < 3, tokens - W, tokens)
     gather_into(full_ref, whole_ref)
-    taps = both(core, own_ref[...], got_ref[: 9 * count], other_ref[: 9 * count], whole_ref)
+    taps = both(own_ref[...], [ref[...] for ref in got_refs], whole_ref)
     bases = base_ref[:, near], far_ref[:, far]
     extra = jnp.zeros((16, 128), F32)
     extra_lane = lanes((16, 128))
@@ -290,14 +303,14 @@
 
 
 def project_kernel(*refs, at):
-    *own_refs, got_ref, other_ref, full_ref, out_ref, whole_ref, stack_ref = refs
+    *own_refs, got_ref, full_ref, out_ref, whole_ref, stack_ref = refs
     inner = own_refs[0].shape[0]
-    side, core, _ = spot()
+    side, _, _ = spot()
     for index, ref in enumerate(own_refs):
         stack_ref[index * inner : (index + 1) * inner] = ref[...]
     gather_into(full_ref, whole_ref)
     rows = slice(at, at + len(own_refs) * inner)
-    mixed = both(core, stack_ref[...], got_ref[rows], other_ref[rows], whole_ref)
+    mixed = both(stack_ref[...], [got_ref[rows]], whole_ref)
     for which in range(2):
         out_ref[side if which == 0 else 1 - side] = mixed[which].astype(BF16)
 
@@ -315,12 +328,11 @@
         out_ref[head] = jnp.dot(values, weights, preferred_element_type=F32).astype(BF16)
 
 
-def leave_kernel(weight_ref, got_ref, other_ref, full_ref, hidden_ref, keep_ref, send_ref, whole_ref, *, at):
+def leave_kernel(weight_ref, got_ref, full_ref, hidden_ref, keep_ref, send_ref, whole_ref, *, at):
     count, depth = weight_ref.shape
-    side, core, _ = spot()
+    side, _, _ = spot()
     gather_into(full_ref, whole_ref)
-    got, other = (ref[at : at + count, : depth // 2] for ref in (got_ref, other_ref))
-    mine, theirs = both(core, weight_ref[...], got, other, whole_ref)
+    mine, theirs = both(weight_ref[...], [got_ref[at : at + count, :depth]], whole_ref)
     keep_ref[...] = (hidden_ref[side] + mine).astype(BF16)
     send_ref[...] = (hidden_ref[1 - side] + theirs).astype(BF16)
 
@@ -352,16 +364,11 @@
     share = tokens // 2
     chs = lax.axis_size("ch")
     place = lax.axis_index("row")
-    core = place % 2
     image_id = place // 2
     inner = w_query.shape[0]
 
     def tall(weight):
         return jnp.transpose(weight, (1, 2, 0, 3)).reshape(9 * count, C)
-
-    def halved(weight):
-        depth = weight.shape[1] // 2
-        return lax.dynamic_slice_in_dim(weight, core * depth, depth, axis=1)
 
     step_value = jnp.sum(jnp.where(jnp.arange(timestep.shape[0]) == image_id, timestep, 0)).astype(F32)
     half = TDIM // 2
@@ -374,64 +381,67 @@
     note = ((2 * count + 16, 128), BF16)
     whole = pltpu.VMEM((C, share), BF16)
 
-    gains = [gain.reshape(1, count) for gain in (norm_gain_a, norm_gain_b, norm_gain_c)]
+    gain_a, gain_b, gain_c = (gain.reshape(1, count) for gain in (norm_gain_a, norm_gain_b, norm_gain_c))
+    own_a, own_b = tall(conv_weight_a), tall(conv_weight_b)
     turned, keep, send, sums = call(
-        enter_kernel, [((count, tokens), F32), quarter, quarter, ((count, 128), F32)], [VM] * 4
-    )(latent.reshape(tokens, count), *gains)
-    (active_a,) = call(first_kernel, [active], [VM] * 3)(turned, sums, swapped(sums))
-
-    own_a, own_b = tall(conv_weight_a), tall(conv_weight_b)
+        enter_kernel, [((count, tokens), F32), quarter, quarter, ((count, 128), F32)], [VM]
+    )(latent.reshape(tokens, count))
+    peer = swapped(sums)
+    (half_a,) = call(half_kernel, [((9 * count, C // 2), BF16)], [FAR], [pltpu.SemaphoreType.DMA])(
+        after(own_a, sums)
+    )
+    got_a = from_beside(half_a)
+    (active_a,) = call(first_kernel, [active], [VM] * 4)(turned, sums, peer, gain_a)
+
     spread = jnp.broadcast_to(active_a[:, None], (2, chs // 2, count, share)).reshape(chs, count, share)
     full = lax.all_to_all(spread, "ch", 0, 0, tiled=True)
-    got_a = from_beside(halved(after(own_a, spread)))
-    vector, mail = call(mail_kernel, [((count, 128), F32), ((count, share + 128), F32)], [VM] * 4)(
-        time_weight.T, sinus, sums, after(send, spread)
+    vector, mail = call(mail_kernel, [((count, 128), F32), ((count, share + 128), F32)], [VM] * 5)(
+        time_weight.T, sinus, gain_b, gain_c, after(send, spread)
     )
     mail = crossed(mail)
-    other_a = swapped(got_a)
-    qkv = jnp.concatenate([w_query, w_key, w_value], axis=0)
-    late_b, late, late_out, _ = lax.optimization_barrier((own_b, qkv, w_out, got_a))
-    late_out = jnp.pad(halved(late_out), ((0, 0), (0, (C - w_out.shape[1]) // 2)))
-    got_b = from_beside(jnp.concatenate([halved(late_b), halved(late), late_out], axis=0))
-
-    def conv(full, own, got, other, base, near, far):
+    other_a = swapped(after(got_a, spread))
+
+    def conv(full, own, gots, base, near, far):
         return call(
-            functools.partial(conv_kernel, near=near, far=far), [field, note], [VM] * 6, [whole]
-        )(own, got, other, full, base, mail)
+            functools.partial(conv_kernel, near=near, far=far), [field, note], [VM] * (4 + len(gots)), [whole]
+        )(own, *gots, full, base, mail)
 
     def finish(part, note, act, lane_of, outs):
         return call(
             functools.partial(finish_kernel, act=act, lane_of=lane_of), outs, [VM] * 4
         )(part, image_collect(note), vector, mail)
 
-    part_a, note_a = conv(full, own_a, got_a, other_a, vector, slice(0, 1), slice(share, share + 1))
+    part_a, note_a = conv(full, own_a, [got_a, other_a], vector, slice(0, 1), slice(share, share + 1))
     (active_b,) = finish(part_a, note_a, True, 1, [active])
     spread_b = column_copies(active_b)
-    other_b = swapped(after(got_b, spread_b))
-    part_b, note_b = conv(
-        column_collect(spread_b), own_b, got_b, other_b, keep, slice(0, share), slice(0, share)
-    )
+    full_b = column_collect(spread_b)
+    got_b = from_beside(after(own_b, spread_b))
+    part_b, note_b = conv(full_b, own_b, [got_b], keep, slice(0, share), slice(0, share))
     normed, hidden_b = finish(part_b, note_b, False, 2, [active, field])
 
-    features = column_collect(column_copies(normed))
+    spread_c = column_copies(normed)
+    features = column_collect(spread_c)
+    late = [after(weight, note_b) for weight in (w_query, w_key, w_value)]
+    late.append(jnp.pad(after(w_out, note_b), ((0, 0), (0, C - w_out.shape[1]))))
+    got_c = from_beside(after(jnp.concatenate(late, axis=0), spread_c))
 
     def project(weights, at):
         return call(
             functools.partial(project_kernel, at=at),
             [((2, len(weights) * inner, share), BF16)],
-            [VM] * (len(weights) + 3),
+            [VM] * (len(weights) + 2),
             [whole, pltpu.VMEM((len(weights) * inner, C), BF16)],
-        )(*weights, got_b, other_b, features)[0]
-
-    pairs = image_collect(project([w_key, w_value], 9 * count + inner))
-    query = project([w_query], 9 * count)
+        )(*weights, got_c, features)[0]
+
+    pairs = image_collect(project([w_key, w_value], inner))
+    query = project([w_query], 0)
     (heads_out,) = call(attend_kernel, [((2, inner, share), BF16)], [VM] * 2)(query, pairs)
     kept, sent = call(
-        functools.partial(leave_kernel, at=9 * count + 3 * inner),
+        functools.partial(leave_kernel, at=3 * inner),
         [((count, share), BF16)] * 2,
-        [VM] * 5,
+        [VM] * 4,
         [pltpu.VMEM((w_out.shape[1], share), BF16)],
-    )(w_out, got_b, other_b, column_collect(column_copies(heads_out)), hidden_b)
+    )(w_out, got_c, column_collect(column_copies(heads_out)), hidden_b)
     (result,) = call(last_kernel, [((tokens, count), BF16)], [VM] * 2)(kept, crossed(sent))
     return result.reshape(rows, width, count)
 

time: 177 us -> 157 us (0.89)
  blocking collectives: 86.1 us -> 58.7 us
  waiting for transfers between devices: 26.9 us -> 36.6 us
  local copies, waits for them, and re-layouts: 12 us -> 8.05 us
  starting transfers between devices: 35.4 us -> 39.2 us
  other arithmetic: 2.77 us -> 0.86 us
    all_to_all x3 -> x2, blocking collectives: 66.7 us -> 42.7 us  [column_collect(): lax.all_to_all(spread, 'ch', 0, 0, tiled=True, axis_index_groups=groups)]
    all_to_all x0 -> x1, waiting for transfers between devices: none -> 7.32 us  [column_collect(): lax.all_to_all(spread, 'ch', 0, 0, tiled=True, axis_index_groups=groups)]
    all_to_all x0 -> x1, starting transfers between devices: none -> 3.54 us  [column_collect(): lax.all_to_all(spread, 'ch', 0, 0, tiled=True, axis_index_groups=groups)]
    dynamic_slice x4 -> x0, local copies, waits for them, and re-layouts: 3.51 us -> none  [halved(): return lax.dynamic_slice_in_dim(weight, core * depth, depth, axis=1)]
    all_to_all x2, blocking collectives: 19.4 us -> 15.9 us  [image_collect(): lax.all_to_all(copies(block, 4), ('ch', 'row'), 0, 0, tiled=True, axis_in...]
    ppermute x2 -> x3, waiting for transfers between devices: 9.23 us -> 12.4 us  [from_beside(): return lax.ppermute(value, ('ch', 'row'), pairs)]
    concatenate x2 -> x1, other arithmetic: 2.01 us -> 0.05 us  [body(): got_c = from_beside(after(jnp.concatenate(late, axis=0), spread_c))]
    ppermute x2 -> x3, starting transfers between devices: 6.16 us -> 8.12 us  [from_beside(): return lax.ppermute(value, ('ch', 'row'), pairs)]
  transfers between devices with their start and end apart: 9 -> 10, of which waited for: 5 -> 7; matrix products, arithmetic and copies ran while one was open for 2% -> 1% of each run, Pallas kernels for 3% -> 1%
where the time goes in v4:
time: 157 us; the launch traced here: 156 us
  blocking collectives  58.7 us (37%)
  starting transfers between devices  39.2 us (25%)
  waiting for transfers between devices  36.6 us (23%)
  Pallas kernels  11.6 us (7%)
  local copies, waits for them, and re-layouts  8.05 us (5%)
    all_to_all x2, blocking collectives, column_collect(): lax.all_to_all(spread, 'ch', 0, 0, tiled=True, axis_index_groups=groups)  42.7 us
    all_to_all x2, blocking collectives, image_collect(): lax.all_to_all(copies(block, 4), ('ch', 'row'), 0, 0, tiled=True, axis_in...  15.9 us
    ppermute x2, starting transfers between devices, swapped(): return lax.ppermute(value, ('ch', 'row'), core_pairs())  15.3 us
    ppermute x3, waiting for transfers between devices, from_beside(): return lax.ppermute(value, ('ch', 'row'), pairs)  12.4 us
    ppermute x2, waiting for transfers between devices, crossed(): lax.ppermute(value, 'ch', [(k, (k + chs // 2) % chs) for k in range(chs)])  8.18 us
    ppermute x3, starting transfers between devices, from_beside(): return lax.ppermute(value, ('ch', 'row'), pairs)  8.12 us
    all_to_all x1, waiting for transfers between devices, image_collect(): lax.all_to_all(copies(block, 4), ('ch', 'row'), 0, 0, tiled=True, axis_in...  7.78 us
    all_to_all x1, waiting for transfers between devices, column_collect(): lax.all_to_all(spread, 'ch', 0, 0, tiled=True, axis_index_groups=groups)  7.32 us
  transfers between devices with their start and end apart: 10, of which 7 were waited for; matrix products, arithmetic and copies ran while one was open for 1% of the time, Pallas kernels for 1%

profile of v4, /device:TPU:1, one launch (start us, length us, event | category | flops | bytes accessed | tf_op | source)
XLA Modules:
  0.0 155.9 jit_solution(9084128268189339128)
XLA Ops:
  0.0 0.9 copy-done.9
  1.7 1.5 copy-done
  3.2 1.0 shard_map.119
  4.3 4.1 %collective-permute-start = (bf16[720,640]{1,0:T(8,128)(2,1)}, bf16[720,640]{1,0:T(8,128)(2,1)S(1)}, u32[]{:S(2)}, u32[]{:S(2)}) collective-permute-start(bf16[720,640]{1,0:T(8,128)(2,1)} %shard_map.119), channel_id=1, source_target_pairs={{256,0},{259,1},{258,2},{257,3},{260,4},{263,5},{262,6},{261,7},{2... | collective-permute-start | bytes 2764808 | tf_op jit(solution)/shard_map/ppermute | solution.py:67
  8.4 6.7 %collective-permute-start.1 = (f32[80,128]{1,0:T(8,128)S(1)}, f32[80,128]{1,0:T(8,128)S(1)}, u32[]{:S(2)}, u32[]{:S(2)}) collective-permute-start(f32[80,128]{1,0:T(8,128)S(1)} %get-tuple-element.28.own_ref), channel_id=1, source_target_pairs={{0,1},{1,0},{2,3},{3,2},{4,5},{5,4},{6,7},{7,6},{8,9},{9,8},{10,11... | collective-permute-start | bytes 122888 | tf_op jit(solution)/shard_map/ppermute | solution.py:49
  15.1 0.8 collective-permute-done.1.peer_ref
  16.3 0.9 broadcast_in_dim.18
  17.1 4.3 %all-to-all-start = ((bf16[16,80,256]{2,1,0:T(8,128)(2,1)}), bf16[16,80,256]{2,1,0:T(8,128)(2,1)S(1)}, u32[]{:S(2)}, u32[]{:S(2)}) async-start(bf16[16,80,256]{2,1,0:T(8,128)(2,1)} %bitcast.22), calls=%async_computation | async-start | bytes 1310720 | tf_op jit(solution)/shard_map/all_to_all | solution.py:397
  21.5 8.6 %collective-permute-start.2 = (bf16[720,640]{1,0:T(8,128)(2,1)S(1)}, bf16[720,640]{1,0:T(8,128)(2,1)}, u32[]{:S(2)}, u32[]{:S(2)}) collective-permute-start(bf16[720,640]{1,0:T(8,128)(2,1)S(1)} %collective-permute-done.refs_0_), channel_id=1, source_target_pairs={{0,1},{1,0},{2,3},{3,2},{4,5},{5,4},{6,7},{7,6},{8,9},{9,8},{10,11... | collective-permute-start | bytes 2764808 | tf_op jit(solution)/shard_map/ppermute | solution.py:49
  33.2 1.9 %collective-permute-start.3 = (f32[80,384]{1,0:T(8,128)S(1)}, f32[80,384]{1,0:T(8,128)S(1)}, u32[]{:S(2)}, u32[]{:S(2)}) collective-permute-start(f32[80,384]{1,0:T(8,128)S(1)} %get-tuple-element.35), channel_id=1, source_target_pairs={{0,256},{32,288},{64,320},{96,352},{128,384},{160,416},{192,448},{... | collective-permute-start | bytes 368648 | tf_op jit(solution)/shard_map/ppermute | solution.py:54
  35.2 5.5 %collective-permute-done.3.refs_4_.mail_ref.refs_3_ = f32[80,384]{1,0:T(8,128)S(1)} collective-permute-done((f32[80,384]{1,0:T(8,128)S(1)}, f32[80,384]{1,0:T(8,128)S(1)}, u32[]{:S(2)}, u32[]{:S(2)}) %collective-permute-start.3) | collective-permute-done | bytes 122912 | tf_op jit(solution)/shard_map/ppermute | solution.py:54
  41.4 2.9 %shard_map.122 = (f32[2,80,256]{2,1,0:T(8,128)S(1)}, bf16[176,128]{1,0:T(8,128)(2,1)S(1)}) custom-call(bf16[720,1280]{1,0:T(8,128)(2,1)S(1)} %bitcast.14, bf16[720,640]{1,0:T(8,128)(2,1)S(1)} %collective-permute-done.refs_0_, bf16[720,640]{1,0:T(8,128)(2,1)} %collective-permute-done.2.refs_1_, bf16[16,80,256]{2,1,0:T(8,128)(2,1)S(1)} %all-to-all-done.refs_2_, ...), custom_call_target="tpu_custom_call" | custom-call | tf_op jit(solution)/shard_map/pallas_call | solution.py:405
  44.4 7.9 %all_to_all.35.notes_ref = bf16[4,176,128]{2,1,0:T(8,128)(2,1)S(1)} all-to-all(bf16[4,176,128]{2,1,0:T(8,128)(2,1)S(1)} %broadcast_in_dim.20), channel_id=1, replica_groups={{0,256,257,1},{32,288,289,33},{64,320,321,65},{96,352,353,97},{128,384,..., dimensions={0} | all-to-all | bytes 360448 | tf_op jit(solution)/shard_map/all_to_all | solution.py:101
  52.3 0.9 shard_map.123
  53.3 2.0 %collective-permute-start.4 = (bf16[720,1280]{1,0:T(8,128)(2,1)S(1)}, bf16[720,1280]{1,0:T(8,128)(2,1)S(1)}, u32[]{:S(2)}, u32[]{:S(2)}) collective-permute-start(bf16[720,1280]{1,0:T(8,128)(2,1)S(1)} %bitcast.15), channel_id=1, source_target_pairs={{256,0},{259,1},{258,2},{257,3},{260,4},{263,5},{262,6},{261,7},{2... | collective-permute-start | bytes 5529608 | tf_op jit(solution)/shard_map/ppermute | solution.py:67
  55.4 22.3 %all_to_all.36.refs_1_ = bf16[8,2,80,256]{3,2,1,0:T(8,128)(2,1)S(1)} all-to-all(bf16[8,2,80,256]{3,2,1,0:T(8,128)(2,1)S(1)} %broadcast_in_dim.21), channel_id=1, replica_groups={{0,32,64,96,128,160,192,224},{256,288,320,352,384,416,448,480},{1,33,65..., dimensions={0} | all-to-all | bytes 1310720 | tf_op jit(solution)/shard_map/all_to_all | solution.py:91
  77.7 1.2 collective-permute-done.4.refs_0_
  78.9 1.6 shard_map.124
  80.5 8.0 %all_to_all.37.notes_ref = bf16[4,176,128]{2,1,0:T(8,128)(2,1)S(1)} all-to-all(bf16[4,176,128]{2,1,0:T(8,128)(2,1)S(1)} %broadcast_in_dim.22), channel_id=1, replica_groups={{0,256,257,1},{32,288,289,33},{64,320,321,65},{96,352,353,97},{128,384,..., dimensions={0} | all-to-all | bytes 360448 | tf_op jit(solution)/shard_map/all_to_all | solution.py:101
  88.6 0.9 shard_map.125
  89.5 0.9 broadcast_in_dim.23
  90.4 3.5 %all-to-all-start.4 = ((bf16[8,2,80,256]{3,2,1,0:T(8,128)(2,1)}), bf16[8,2,80,256]{3,2,1,0:T(8,128)(2,1)S(1)}, u32[]{:S(2)}, u32[]{:S(2)}) async-start(bf16[8,2,80,256]{3,2,1,0:T(8,128)(2,1)} %broadcast_in_dim.23), calls=%async_computation.4 | async-start | bytes 1310720 | tf_op jit(solution)/shard_map/all_to_all | solution.py:91
  94.0 2.0 %collective-permute-start.5 = (bf16[272,1280]{1,0:T(8,128)(2,1)S(1)}, bf16[272,1280]{1,0:T(8,128)(2,1)S(1)}, u32[]{:S(2)}, u32[]{:S(2)}) collective-permute-start(bf16[272,1280]{1,0:T(8,128)(2,1)S(1)} %fusion.1), channel_id=1, source_target_pairs={{256,0},{259,1},{258,2},{257,3},{260,4},{263,5},{262,6},{261,7},{2... | collective-permute-start | bytes 2088968 | tf_op jit(solution)/shard_map/ppermute | solution.py:67
  96.1 11.2 %collective-permute-done.5.refs_1_.refs_2_.got_ref = bf16[272,1280]{1,0:T(8,128)(2,1)S(1)} collective-permute-done((bf16[272,1280]{1,0:T(8,128)(2,1)S(1)}, bf16[272,1280]{1,0:T(8,128)(2,1)S(1)}, u32[]{:S(2)}, u32[]{:S(2)}) %collective-permute-start.5) | collective-permute-done | bytes 696352 | tf_op jit(solution)/shard_map/ppermute | solution.py:67
  107.3 7.3 %all-to-all-done.4.refs_2_.refs_3_ = bf16[8,2,80,256]{3,2,1,0:T(8,128)(2,1)S(1)} async-done(((bf16[8,2,80,256]{3,2,1,0:T(8,128)(2,1)}), bf16[8,2,80,256]{3,2,1,0:T(8,128)(2,1)S(1)}, u32[]{:S(2)}, u32[]{:S(2)}) %all-to-all-start.4) | async-done | bytes 655392 | tf_op jit(solution)/shard_map/all_to_all | solution.py:91
  115.0 0.8 broadcast_in_dim.24
  115.8 3.9 %all-to-all-start.5 = ((bf16[4,2,128,256]{3,2,1,0:T(8,128)(2,1)}), bf16[4,2,128,256]{3,2,1,0:T(8,128)(2,1)S(1)}, u32[]{:S(2)}, u32[]{:S(2)}) async-start(bf16[4,2,128,256]{3,2,1,0:T(8,128)(2,1)} %broadcast_in_dim.24), calls=%async_computation.5 | async-start | bytes 1048576 | tf_op jit(solution)/shard_map/all_to_all | solution.py:101
  120.1 7.8 %all-to-all-done.5.pairs_ref = bf16[4,2,128,256]{3,2,1,0:T(8,128)(2,1)S(1)} async-done(((bf16[4,2,128,256]{3,2,1,0:T(8,128)(2,1)}), bf16[4,2,128,256]{3,2,1,0:T(8,128)(2,1)S(1)}, u32[]{:S(2)}, u32[]{:S(2)}) %all-to-all-start.5) | async-done | bytes 524320 | tf_op jit(solution)/shard_map/all_to_all | solution.py:101
  127.9 1.8 %shard_map.128 = bf16[2,64,256]{2,1,0:T(8,128)(2,1)S(1)} custom-call(bf16[2,64,256]{2,1,0:T(8,128)(2,1)S(1)} %shard_map.126.q_ref, bf16[4,2,128,256]{3,2,1,0:T(8,128)(2,1)S(1)} %all-to-all-done.5.pairs_ref), custom_call_target="tpu_custom_call" | custom-call | tf_op jit(solution)/shard_map/pallas_call | solution.py:438
  129.7 20.4 %all_to_all.38.full_ref = bf16[8,2,64,256]{3,2,1,0:T(8,128)(2,1)S(1)} all-to-all(bf16[8,2,64,256]{3,2,1,0:T(8,128)(2,1)S(1)} %broadcast_in_dim.25), channel_id=1, replica_groups={{0,32,64,96,128,160,192,224},{256,288,320,352,384,416,448,480},{1,33,65..., dimensions={0} | all-to-all | bytes 1048576 | tf_op jit(solution)/shard_map/all_to_all | solution.py:91
  150.4 2.0 %collective-permute-start.6 = (bf16[80,256]{1,0:T(8,128)(2,1)S(1)}, bf16[80,256]{1,0:T(8,128)(2,1)S(1)}, u32[]{:S(2)}, u32[]{:S(2)}) collective-permute-start(bf16[80,256]{1,0:T(8,128)(2,1)S(1)} %get-tuple-element.50), channel_id=1, source_target_pairs={{0,256},{32,288},{64,320},{96,352},{128,384},{160,416},{192,448},{... | collective-permute-start | bytes 122888 | tf_op jit(solution)/shard_map/ppermute | solution.py:54
  152.5 2.7 %collective-permute-done.6.peer_ref = bf16[80,256]{1,0:T(8,128)(2,1)S(1)} collective-permute-done((bf16[80,256]{1,0:T(8,128)(2,1)S(1)}, bf16[80,256]{1,0:T(8,128)(2,1)S(1)}, u32[]{:S(2)}, u32[]{:S(2)}) %collective-permute-start.6) | collective-permute-done | bytes 40992 | tf_op jit(solution)/shard_map/ppermute | solution.py:54
  (52 shorter events, 6.3 us)
Async XLA Ops:
  0.0 0.9 copy-start.9
  1.1 0.6 copy-start.10
  1.7 14.3 %copy-start.13 = (f32[80]{0:T(128)S(1)}, f32[80]{0:T(128)}, u32[]{:S(2)}) copy-start(f32[80]{0:T(128)} %param.14) | copy-start | bytes 964
  1.7 1.5 copy-start
  4.3 25.8 %copy-start.16 = (s32[16]{0:T(128)S(1)}, s32[16]{0:T(128)}, u32[]{:S(2)}) copy-start(s32[16]{0:T(128)} %param.13) | copy-start | bytes 196
  4.3 27.3 %copy-start.14 = (f32[80]{0:T(128)S(1)}, f32[80]{0:T(128)}, u32[]{:S(2)}) copy-start(f32[80]{0:T(128)} %param.17) | copy-start | bytes 964
  4.3 27.3 %copy-start.15 = (f32[80]{0:T(128)S(1)}, f32[80]{0:T(128)}, u32[]{:S(2)}) copy-start(f32[80]{0:T(128)} %param.19) | copy-start | bytes 964
  4.3 36.3 %copy-start.1 = (bf16[80,3,3,1280]{3,0,2,1:T(8,128)(2,1)S(1)}, bf16[80,3,3,1280]{3,0,2,1:T(8,128)(2,1)}, u32[]{:S(2)}) copy-start(bf16[80,3,3,1280]{3,0,2,1:T(8,128)(2,1)} %param.15) | copy-start | bytes 5529604
  4.3 17.1 %collective-permute-start = (bf16[720,640]{1,0:T(8,128)(2,1)}, bf16[720,640]{1,0:T(8,128)(2,1)S(1)}, u32[]{:S(2)}, u32[]{:S(2)}) collective-permute-start(bf16[720,640]{1,0:T(8,128)(2,1)} %shard_map.119), channel_id=1, source_target_pairs={{256,0},{259,1},{258,2},{257,3},{260,4},{263,5},{262,6},{261,7},{2... | collective-permute-start | bytes 2764808 | tf_op jit(solution)/shard_map/ppermute | solution.py:67
  8.4 7.6 %collective-permute-start.1 = (f32[80,128]{1,0:T(8,128)S(1)}, f32[80,128]{1,0:T(8,128)S(1)}, u32[]{:S(2)}, u32[]{:S(2)}) collective-permute-start(f32[80,128]{1,0:T(8,128)S(1)} %get-tuple-element.28.own_ref), channel_id=1, source_target_pairs={{0,1},{1,0},{2,3},{3,2},{4,5},{5,4},{6,7},{7,6},{8,9},{9,8},{10,11... | collective-permute-start | bytes 122888 | tf_op jit(solution)/shard_map/ppermute | solution.py:49
  17.1 23.5 %all-to-all-start = ((bf16[16,80,256]{2,1,0:T(8,128)(2,1)}), bf16[16,80,256]{2,1,0:T(8,128)(2,1)S(1)}, u32[]{:S(2)}, u32[]{:S(2)}) async-start(bf16[16,80,256]{2,1,0:T(8,128)(2,1)} %bitcast.22), calls=%async_computation | async-start | bytes 1310720 | tf_op jit(solution)/shard_map/all_to_all | solution.py:397
  21.5 19.2 %collective-permute-start.2 = (bf16[720,640]{1,0:T(8,128)(2,1)S(1)}, bf16[720,640]{1,0:T(8,128)(2,1)}, u32[]{:S(2)}, u32[]{:S(2)}) collective-permute-start(bf16[720,640]{1,0:T(8,128)(2,1)S(1)} %collective-permute-done.refs_0_), channel_id=1, source_target_pairs={{0,1},{1,0},{2,3},{3,2},{4,5},{5,4},{6,7},{7,6},{8,9},{9,8},{10,11... | collective-permute-start | bytes 2764808 | tf_op jit(solution)/shard_map/ppermute | solution.py:49
  31.6 0.8 copy-start.12
  32.6 0.6 copy-start.7
  33.2 7.4 %collective-permute-start.3 = (f32[80,384]{1,0:T(8,128)S(1)}, f32[80,384]{1,0:T(8,128)S(1)}, u32[]{:S(2)}, u32[]{:S(2)}) collective-permute-start(f32[80,384]{1,0:T(8,128)S(1)} %get-tuple-element.35), channel_id=1, source_target_pairs={{0,256},{32,288},{64,320},{96,352},{128,384},{160,416},{192,448},{... | collective-permute-start | bytes 368648 | tf_op jit(solution)/shard_map/ppermute | solution.py:54
  40.7 0.8 copy-start.8
  44.4 9.0 %copy-start.2 = (bf16[80,3,3,1280]{3,0,2,1:T(8,128)(2,1)S(1)}, bf16[80,3,3,1280]{3,0,2,1:T(8,128)(2,1)}, u32[]{:S(2)}) copy-start(bf16[80,3,3,1280]{3,0,2,1:T(8,128)(2,1)} %param.18) | copy-start | bytes 5529604
  52.3 26.6 %copy-start.11 = (f32[80,256]{1,0:T(8,128)S(1)}, f32[80,256]{1,0:T(8,128)}, u32[]{:S(2)}) copy-start(f32[80,256]{1,0:T(8,128)} %copy-done.10) | copy-start | bytes 245764
  53.3 25.6 %collective-permute-start.4 = (bf16[720,1280]{1,0:T(8,128)(2,1)S(1)}, bf16[720,1280]{1,0:T(8,128)(2,1)S(1)}, u32[]{:S(2)}, u32[]{:S(2)}) collective-permute-start(bf16[720,1280]{1,0:T(8,128)(2,1)S(1)} %bitcast.15), channel_id=1, source_target_pairs={{256,0},{259,1},{258,2},{257,3},{260,4},{263,5},{262,6},{261,7},{2... | collective-permute-start | bytes 5529608 | tf_op jit(solution)/shard_map/ppermute | solution.py:67
  80.5 13.4 %copy-start.3 = (bf16[64,1280]{1,0:T(8,128)(2,1)S(1)}, bf16[64,1280]{1,0:T(8,128)(2,1)}, u32[]{:S(2)}) copy-start(bf16[64,1280]{1,0:T(8,128)(2,1)} %refs_1_.1) | copy-start | bytes 491524
  80.5 13.4 %copy-start.4 = (bf16[64,1280]{1,0:T(8,128)(2,1)S(1)}, bf16[64,1280]{1,0:T(8,128)(2,1)}, u32[]{:S(2)}) copy-start(bf16[64,1280]{1,0:T(8,128)(2,1)} %refs_0_.3) | copy-start | bytes 491524
  80.5 13.4 %copy-start.5 = (bf16[64,1280]{1,0:T(8,128)(2,1)S(1)}, bf16[64,1280]{1,0:T(8,128)(2,1)}, u32[]{:S(2)}) copy-start(bf16[64,1280]{1,0:T(8,128)(2,1)} %refs_0_.2) | copy-start | bytes 491524
  80.5 13.4 %copy-start.6 = (bf16[80,1024]{1,0:T(8,128)(2,1)S(1)}, bf16[80,1024]{1,0:T(8,128)(2,1)}, u32[]{:S(2)}) copy-start(bf16[80,1024]{1,0:T(8,128)(2,1)} %weight_ref.1) | copy-start | bytes 491524
  90.4 24.2 %all-to-all-start.4 = ((bf16[8,2,80,256]{3,2,1,0:T(8,128)(2,1)}), bf16[8,2,80,256]{3,2,1,0:T(8,128)(2,1)S(1)}, u32[]{:S(2)}, u32[]{:S(2)}) async-start(bf16[8,2,80,256]{3,2,1,0:T(8,128)(2,1)} %broadcast_in_dim.23), calls=%async_computation.4 | async-start | bytes 1310720 | tf_op jit(solution)/shard_map/all_to_all | solution.py:91
  94.0 13.3 %collective-permute-start.5 = (bf16[272,1280]{1,0:T(8,128)(2,1)S(1)}, bf16[272,1280]{1,0:T(8,128)(2,1)S(1)}, u32[]{:S(2)}, u32[]{:S(2)}) collective-permute-start(bf16[272,1280]{1,0:T(8,128)(2,1)S(1)} %fusion.1), channel_id=1, source_target_pairs={{256,0},{259,1},{258,2},{257,3},{260,4},{263,5},{262,6},{261,7},{2... | collective-permute-start | bytes 2088968 | tf_op jit(solution)/shard_map/ppermute | solution.py:67
  115.8 12.0 %all-to-all-start.5 = ((bf16[4,2,128,256]{3,2,1,0:T(8,128)(2,1)}), bf16[4,2,128,256]{3,2,1,0:T(8,128)(2,1)S(1)}, u32[]{:S(2)}, u32[]{:S(2)}) async-start(bf16[4,2,128,256]{3,2,1,0:T(8,128)(2,1)} %broadcast_in_dim.24), calls=%async_computation.5 | async-start | bytes 1048576 | tf_op jit(solution)/shard_map/all_to_all | solution.py:101
  150.4 4.7 %collective-permute-start.6 = (bf16[80,256]{1,0:T(8,128)(2,1)S(1)}, bf16[80,256]{1,0:T(8,128)(2,1)S(1)}, u32[]{:S(2)}, u32[]{:S(2)}) collective-permute-start(bf16[80,256]{1,0:T(8,128)(2,1)S(1)} %get-tuple-element.50), channel_id=1, source_target_pairs={{0,256},{32,288},{64,320},{96,352},{128,384},{160,416},{192,448},{... | collective-permute-start | bytes 122888 | tf_op jit(solution)/shard_map/ppermute | solution.py:54

commit v5 on v4

--- a/solution.py
+++ b/solution.py
@@ -61,7 +61,8 @@
     for k in range(chs):
         for r in range(rows):
             core, high, rest = r % 2, r // 2 % wide, r // (2 * wide)
-            x = (2 * high + k // (chs // 2) + (1 if core == 0 else -1)) % (2 * wide)
+            side = k // (chs // 2)
+            x = (2 * high + side + (1 if side else -1)) % (2 * wide)
             source = device(x % 2 * (chs // 2) + k % (chs // 2), (rest * wide + x // 2) * 2 + core)
             pairs.append((source, device(k, r)))
     return lax.ppermute(value, ("ch", "row"), pairs)
@@ -77,28 +78,20 @@
     return lax.optimization_barrier((value, first))[0]
 
 
-def copies(block, count):
-    return jnp.broadcast_to(block[None], (count, *block.shape))
-
-
-def column_copies(block):
-    return copies(block, lax.axis_size("ch") // 2)
-
-
 def column_collect(spread):
     half = lax.axis_size("ch") // 2
     groups = [list(range(half)), list(range(half, 2 * half))]
     return lax.all_to_all(spread, "ch", 0, 0, tiled=True, axis_index_groups=groups)
 
 
-def image_collect(block):
+def image_collect(spread):
     rows, half = lax.axis_size("row"), lax.axis_size("ch") // 2
     groups = [
         [device(k, r), device(k + half, r), device(k + half, r + 1), device(k, r + 1)]
         for r in range(0, rows, 2)
         for k in range(half)
     ]
-    return lax.all_to_all(copies(block, 4), ("ch", "row"), 0, 0, tiled=True, axis_index_groups=groups)
+    return lax.all_to_all(spread, ("ch", "row"), 0, 0, tiled=True, axis_index_groups=groups)
 
 
 def lanes(shape):
@@ -122,30 +115,23 @@
     ]
 
 
-def enter_kernel(latent_ref, turned_ref, keep_ref, send_ref, sums_ref):
-    side, core, _ = spot()
+def enter_kernel(latent_ref, weight_ref, turned_ref, sums_ref, half_ref, sem):
+    _, core, _ = spot()
+    depth = half_ref.shape[1]
+    columns = pl.ds(pl.multiple_of(core * depth, 128), depth)
+    copy = pltpu.make_async_copy(weight_ref.at[:, columns], half_ref, sem)
+    copy.start()
     value = latent_ref[...].astype(F32).T
     turned_ref[...] = value
-    half = value.shape[1] // 2
-    first = side == core
-    keep_ref[...] = jnp.where(first, value[:, :half], value[:, half:])
-    send_ref[...] = jnp.where(first, value[:, half:], value[:, :half])
     lane = lanes(sums_ref.shape)
     total = jnp.sum(value, axis=1, keepdims=True)
     squares = jnp.sum(value * value, axis=1, keepdims=True)
     sums_ref[...] = jnp.where(lane == 0, total, jnp.where(lane == 1, squares, 0.0))
+    copy.wait()
 
 
 def upright(rows):
     return jnp.concatenate(rows + [jnp.zeros((8 - len(rows), rows[0].shape[1]), F32)], axis=0).T
-
-
-def half_kernel(weight_ref, out_ref, sem):
-    _, core, _ = spot()
-    depth = out_ref.shape[1]
-    copy = pltpu.make_async_copy(weight_ref.at[:, pl.ds(pl.multiple_of(core * depth, 128), depth)], out_ref, sem)
-    copy.start()
-    copy.wait()
 
 
 def first_kernel(turned_ref, own_ref, peer_ref, gain_ref, active_ref):
@@ -159,21 +145,31 @@
         pieces.append(scaled(turned_ref[rows], totals[group], squares[group], gain[rows]))
     value = silu(jnp.concatenate(pieces, axis=0)).astype(BF16)
     half = value.shape[1] // 2
-    active_ref[core] = value[:, :half]
-    active_ref[1 - core] = value[:, half:]
-
-
-def mail_kernel(weight_ref, sinus_ref, gain_b_ref, gain_c_ref, send_ref, vector_ref, mail_ref):
+    each = active_ref.shape[0] // 2
+    for copy in range(each):
+        active_ref[core * each + copy] = value[:, :half]
+        active_ref[(1 - core) * each + copy] = value[:, half:]
+
+
+def time_of(weight_ref, sinus_ref):
     product = weight_ref[...].astype(F32) * sinus_ref[...].astype(F32)
-    time_add = silu(jnp.sum(product, axis=1, keepdims=True))
-    lane = lanes(vector_ref.shape)
+    return silu(jnp.sum(product, axis=1, keepdims=True))
+
+
+def turned_share(latent_ref, part, share):
+    rows = pl.ds(pl.multiple_of(part * share, 16), share)
+    return latent_ref[rows, :].astype(F32).T
+
+
+def mail_kernel(weight_ref, sinus_ref, gain_b_ref, gain_c_ref, latent_ref, mail_ref):
+    side, core, _ = spot()
+    share = latent_ref.shape[0] // 2
+    lane = lanes((mail_ref.shape[0], 128))
     gains = upright([gain_b_ref[...], gain_c_ref[...]])
-    vector = jnp.where(lane == 0, time_add, 0.0)
+    vector = jnp.where(lane == 0, time_of(weight_ref, sinus_ref), 0.0)
     for kind in range(2):
         vector = jnp.where(lane == 1 + kind, gains[:, kind : kind + 1], vector)
-    vector_ref[...] = vector
-    share = send_ref.shape[1]
-    mail_ref[:, :share] = send_ref[...]
+    mail_ref[:, :share] = turned_share(latent_ref, 1 - (side ^ core), share)
     mail_ref[:, share:] = vector
 
 
@@ -190,20 +186,22 @@
 
 def both(own, gots, whole_ref):
     mine = jnp.dot(own, whole_ref[...], preferred_element_type=F32)
-    if len(gots) == 1:
-        return mine, jnp.dot(gots[0], whole_ref[...], preferred_element_type=F32)
+    depth = gots[0].shape[1]
+    if depth == own.shape[1]:
+        pieces = [jnp.dot(got, whole_ref[...], preferred_element_type=F32) for got in gots]
+        return mine, jnp.concatenate(pieces, axis=0)
     _, core, _ = spot()
-    depth = gots[0].shape[1]
     near = whole_ref[pl.ds(pl.multiple_of(core * depth, 128), depth), :]
     far = whole_ref[pl.ds(pl.multiple_of((1 - core) * depth, 128), depth), :]
     theirs = jnp.dot(gots[0], near, preferred_element_type=F32)
     return mine, theirs + jnp.dot(gots[1], far, preferred_element_type=F32)
 
 
-def conv_kernel(own_ref, *refs, near, far):
-    *got_refs, full_ref, base_ref, far_ref, part_ref, note_ref, whole_ref = refs
+def conv_kernel(own_ref, *refs, gots):
+    got_refs, refs = refs[:gots], refs[gots:]
+    full_ref, mail_ref, *base_refs, part_ref, note_ref, whole_ref = refs
     _, count, tokens = part_ref.shape
-    side, _, quarter = spot()
+    side, core, quarter = spot()
     token = lanes((count, tokens))
     column = token % W
     lane = lanes((count, 128))
@@ -211,7 +209,10 @@
     end = jnp.where(quarter < 3, tokens - W, tokens)
     gather_into(full_ref, whole_ref)
     taps = both(own_ref[...], [ref[...] for ref in got_refs], whole_ref)
-    bases = base_ref[:, near], far_ref[:, far]
+    if len(base_refs) == 2:
+        bases = time_of(*base_refs), mail_ref[:, tokens : tokens + 1]
+    else:
+        bases = turned_share(base_refs[0], side ^ core, tokens), mail_ref[:, :tokens]
     extra = jnp.zeros((16, 128), F32)
     extra_lane = lanes((16, 128))
     for which in range(2):
@@ -240,7 +241,8 @@
         bottom = pltpu.roll(part[:, tokens - 128 :], 2 * W, 1)
         up = pltpu.roll(below[:, :128], 2 * W, 1)
         note = jnp.where(lane < W, part[:, :128], jnp.where(lane < 2 * W, bottom, jnp.where(lane < 3 * W, up, above[:, tokens - 128 :])))
-        note_ref[pl.ds(pl.multiple_of(here * count, 16), count), :] = note.astype(BF16)
+        for copy in range(note_ref.shape[0]):
+            note_ref[copy, pl.ds(pl.multiple_of(here * count, 16), count), :] = note.astype(BF16)
         for group in range(len(totals)):
             for kind, value in enumerate((totals[group], squares[group])):
                 for piece in range(3):
@@ -248,12 +250,14 @@
                     index = (here * len(totals) + group) * 6 + kind * 3 + piece
                     extra = jnp.where(extra_lane == index, rounded, extra)
                     value = value - rounded
-    note_ref[2 * count :, :] = extra.astype(BF16)
-
-
-def finish_kernel(part_ref, notes_ref, vector_ref, mail_ref, *outs, act, lane_of):
+    for copy in range(note_ref.shape[0]):
+        note_ref[copy, 2 * count :, :] = extra.astype(BF16)
+
+
+def finish_kernel(part_ref, notes_ref, gain_ref, mail_ref, *outs, act, lane_of):
     _, count, tokens = part_ref.shape
     mine, _, quarter = spot()
+    own_gain = upright([gain_ref[...]])[:, 0:1]
     lane = lanes((count, 128))
     sums = notes_ref[0, 2 * count :].astype(F32)
     for place in range(1, 4):
@@ -286,7 +290,7 @@
         )
         totals, squared = by_group(total), by_group(squares)
         at = tokens + lane_of
-        gain = jnp.where(side == mine, vector_ref[:, lane_of : lane_of + 1], mail_ref[:, at : at + 1])
+        gain = jnp.where(side == mine, own_gain, mail_ref[:, at : at + 1])
         pieces = []
         for group in range(len(totals)):
             first = (side * len(totals) + group) * 6
@@ -295,24 +299,25 @@
             span = slice(group * WIDE, (group + 1) * WIDE)
             pieces.append(scaled(value[span], whole, whole_squares, gain[span]))
         result = jnp.concatenate(pieces, axis=0)
-        if act:
-            outs[0][side] = silu(result).astype(BF16)
-        else:
-            outs[0][side] = result.astype(BF16)
+        result = (silu(result) if act else result).astype(BF16)
+        for copy in range(outs[0].shape[0]):
+            outs[0][copy, side] = result
+        if not act:
             outs[1][side] = value
 
 
-def project_kernel(*refs, at):
-    *own_refs, got_ref, full_ref, out_ref, whole_ref, stack_ref = refs
-    inner = own_refs[0].shape[0]
+def project_kernel(query_ref, key_ref, value_ref, got_ref, full_ref, q_ref, kv_ref, whole_ref, stack_ref):
+    inner = query_ref.shape[0]
     side, _, _ = spot()
-    for index, ref in enumerate(own_refs):
+    for index, ref in enumerate((query_ref, key_ref, value_ref)):
         stack_ref[index * inner : (index + 1) * inner] = ref[...]
     gather_into(full_ref, whole_ref)
-    rows = slice(at, at + len(own_refs) * inner)
-    mixed = both(stack_ref[...], [got_ref[rows]], whole_ref)
+    mixed = both(stack_ref[...], [got_ref[: 3 * inner]], whole_ref)
     for which in range(2):
-        out_ref[side if which == 0 else 1 - side] = mixed[which].astype(BF16)
+        here = side if which == 0 else 1 - side
+        q_ref[here] = mixed[which][:inner].astype(BF16)
+        for copy in range(kv_ref.shape[0]):
+            kv_ref[copy, here] = mixed[which][inner:].astype(BF16)
 
 
 def attend_kernel(q_ref, pairs_ref, out_ref):
@@ -325,7 +330,9 @@
         ) * (1.0 / math.sqrt(HEAD_DIM))
         raised = jnp.exp(scores - jnp.max(scores, axis=0, keepdims=True))
         weights = (raised * (1.0 / jnp.sum(raised, axis=0, keepdims=True))).astype(BF16)
-        out_ref[head] = jnp.dot(values, weights, preferred_element_type=F32).astype(BF16)
+        mixed = jnp.dot(values, weights, preferred_element_type=F32).astype(BF16)
+        for copy in range(out_ref.shape[0]):
+            out_ref[copy, head] = mixed
 
 
 def leave_kernel(weight_ref, got_ref, full_ref, hidden_ref, keep_ref, send_ref, whole_ref, *, at):
@@ -376,72 +383,72 @@
     angles = step_value * freqs
     sinus = jnp.concatenate([jnp.cos(angles), jnp.sin(angles)])[None, :].astype(BF16)
     field = ((2, count, share), F32)
-    active = ((2, count, share), BF16)
-    quarter = ((count, share), F32)
-    note = ((2 * count + 16, 128), BF16)
+    half_chs = chs // 2
+    active = ((half_chs, 2, count, share), BF16)
+    note = ((4, 2 * count + 16, 128), BF16)
     whole = pltpu.VMEM((C, share), BF16)
 
     gain_a, gain_b, gain_c = (gain.reshape(1, count) for gain in (norm_gain_a, norm_gain_b, norm_gain_c))
     own_a, own_b = tall(conv_weight_a), tall(conv_weight_b)
-    turned, keep, send, sums = call(
-        enter_kernel, [((count, tokens), F32), quarter, quarter, ((count, 128), F32)], [VM]
-    )(latent.reshape(tokens, count))
+    flat = latent.reshape(tokens, count)
+    turned, sums, half_a = call(
+        enter_kernel,
+        [((count, tokens), F32), ((count, 128), F32), ((9 * count, C // 2), BF16)],
+        [VM, FAR],
+        [pltpu.SemaphoreType.DMA],
+    )(flat, own_a)
     peer = swapped(sums)
-    (half_a,) = call(half_kernel, [((9 * count, C // 2), BF16)], [FAR], [pltpu.SemaphoreType.DMA])(
-        after(own_a, sums)
-    )
     got_a = from_beside(half_a)
-    (active_a,) = call(first_kernel, [active], [VM] * 4)(turned, sums, peer, gain_a)
-
-    spread = jnp.broadcast_to(active_a[:, None], (2, chs // 2, count, share)).reshape(chs, count, share)
-    full = lax.all_to_all(spread, "ch", 0, 0, tiled=True)
-    vector, mail = call(mail_kernel, [((count, 128), F32), ((count, share + 128), F32)], [VM] * 5)(
-        time_weight.T, sinus, gain_b, gain_c, after(send, spread)
+    (spread_a,) = call(first_kernel, [((chs, count, share), BF16)], [VM] * 4)(turned, sums, peer, gain_a)
+
+    full = lax.all_to_all(spread_a, "ch", 0, 0, tiled=True)
+    (mail,) = call(mail_kernel, [((count, share + 128), F32)], [VM] * 5)(
+        time_weight.T, sinus, gain_b, gain_c, after(flat, spread_a)
     )
     mail = crossed(mail)
-    other_a = swapped(after(got_a, spread))
-
-    def conv(full, own, gots, base, near, far):
+    cut = 6 * count
+    late_b = after(own_b, spread_a)
+    low_b = crossed(late_b[cut:])
+    high_b = from_beside(late_b[:cut])
+    late = [w_query, w_key, w_value, jnp.pad(w_out, ((0, 0), (0, C - w_out.shape[1])))]
+    got_c = from_beside(after(jnp.concatenate(late, axis=0), spread_a))
+    other_a = swapped(after(got_a, spread_a))
+
+    def conv(full, own, gots, *bases):
         return call(
-            functools.partial(conv_kernel, near=near, far=far), [field, note], [VM] * (4 + len(gots)), [whole]
-        )(own, *gots, full, base, mail)
-
-    def finish(part, note, act, lane_of, outs):
+            functools.partial(conv_kernel, gots=len(gots)),
+            [field, note],
+            [VM] * (3 + len(gots) + len(bases)),
+            [whole],
+        )(own, *gots, full, mail, *bases)
+
+    def finish(part, notes, gain, act, lane_of, outs):
         return call(
             functools.partial(finish_kernel, act=act, lane_of=lane_of), outs, [VM] * 4
-        )(part, image_collect(note), vector, mail)
-
-    part_a, note_a = conv(full, own_a, [got_a, other_a], vector, slice(0, 1), slice(share, share + 1))
-    (active_b,) = finish(part_a, note_a, True, 1, [active])
-    spread_b = column_copies(active_b)
-    full_b = column_collect(spread_b)
-    got_b = from_beside(after(own_b, spread_b))
-    part_b, note_b = conv(full_b, own_b, [got_b], keep, slice(0, share), slice(0, share))
-    normed, hidden_b = finish(part_b, note_b, False, 2, [active, field])
-
-    spread_c = column_copies(normed)
+        )(part, notes, gain, mail)
+
+    part_a, note_a = conv(full, own_a, [got_a, other_a], time_weight.T, sinus)
+    notes_a = image_collect(note_a)
+    (spread_b,) = finish(part_a, notes_a, gain_b, True, 1, [active])
+    part_b, note_b = conv(column_collect(spread_b), own_b, [high_b, low_b], flat)
+    notes_b = image_collect(note_b)
+    spread_c, hidden_b = finish(part_b, notes_b, gain_c, False, 2, [active, field])
     features = column_collect(spread_c)
-    late = [after(weight, note_b) for weight in (w_query, w_key, w_value)]
-    late.append(jnp.pad(after(w_out, note_b), ((0, 0), (0, C - w_out.shape[1]))))
-    got_c = from_beside(after(jnp.concatenate(late, axis=0), spread_c))
-
-    def project(weights, at):
-        return call(
-            functools.partial(project_kernel, at=at),
-            [((2, len(weights) * inner, share), BF16)],
-            [VM] * (len(weights) + 2),
-            [whole, pltpu.VMEM((len(weights) * inner, C), BF16)],
-        )(*weights, got_c, features)[0]
-
-    pairs = image_collect(project([w_key, w_value], inner))
-    query = project([w_query], 0)
-    (heads_out,) = call(attend_kernel, [((2, inner, share), BF16)], [VM] * 2)(query, pairs)
+
+    query, key_value = call(
+        project_kernel,
+        [((2, inner, share), BF16), ((4, 2, 2 * inner, share), BF16)],
+        [VM] * 5,
+        [whole, pltpu.VMEM((3 * inner, C), BF16)],
+    )(w_query, w_key, w_value, got_c, features)
+    pairs = image_collect(key_value)
+    (heads_out,) = call(attend_kernel, [((half_chs, 2, inner, share), BF16)], [VM] * 2)(query, pairs)
     kept, sent = call(
         functools.partial(leave_kernel, at=3 * inner),
         [((count, share), BF16)] * 2,
         [VM] * 4,
         [pltpu.VMEM((w_out.shape[1], share), BF16)],
-    )(w_out, got_c, column_collect(column_copies(heads_out)), hidden_b)
+    )(w_out, got_c, column_collect(heads_out), hidden_b)
     (result,) = call(last_kernel, [((tokens, count), BF16)], [VM] * 2)(kept, crossed(sent))
     return result.reshape(rows, width, count)
 

time: 157 us -> 169 us (1.076)
  blocking collectives: 58.7 us -> 41.9 us
  waiting for transfers between devices: 36.6 us -> 49.9 us
  starting transfers between devices: 39.2 us -> 51.8 us
  Pallas kernels: 11.6 us -> 16.4 us
  local copies, waits for them, and re-layouts: 8.05 us -> 4.94 us
    all_to_all x2 -> x1, blocking collectives: 42.7 us -> 23.3 us  [column_collect(): lax.all_to_all(spread, 'ch', 0, 0, tiled=True, axis_index_groups=groups)]
    ppermute x2 -> x3, waiting for transfers between devices: 8.18 us -> 22.4 us  [crossed(): lax.ppermute(value, 'ch', [(k, (k + chs // 2) % chs) for k in range(chs)])]
    ppermute x3, waiting for transfers between devices: 12.4 us -> 23.7 us  [from_beside(): return lax.ppermute(value, ('ch', 'row'), pairs)]
    all_to_all x1 -> x2, starting transfers between devices: 3.54 us -> 12 us  [column_collect(): lax.all_to_all(spread, 'ch', 0, 0, tiled=True, axis_index_groups=groups)]
    all_to_all x2, waiting for transfers between devices: 7.78 us -> 0.01 us  [the longest x1 0.01 us: image_collect(): lax.all_to_all(spread, ('ch', 'row'), 0, 0, tiled=True, axis_index_groups...]
    ppermute x3, starting transfers between devices: 8.12 us -> 13.2 us  [from_beside(): return lax.ppermute(value, ('ch', 'row'), pairs)]
    all_to_all x1 -> x2, waiting for transfers between devices: 7.32 us -> 2.9 us  [column_collect(): lax.all_to_all(spread, 'ch', 0, 0, tiled=True, axis_index_groups=groups)]
    ppermute x2, starting transfers between devices: 15.3 us -> 12.2 us  [swapped(): return lax.ppermute(value, ('ch', 'row'), core_pairs())]
  transfers between devices with their start and end apart: 10 -> 12, of which waited for: 7 -> 9; matrix products, arithmetic and copies ran while one was open for 1% -> 2% of each run, Pallas kernels for 1% -> 2%
where the time goes in v5:
time: 169 us; the launch traced here: 167 us
  starting transfers between devices  51.8 us (31%)
  waiting for transfers between devices  49.9 us (30%)
  blocking collectives  41.9 us (25%)
  Pallas kernels  16.4 us (10%)
  local copies, waits for them, and re-layouts  4.94 us (3%)
    ppermute x3, waiting for transfers between devices, from_beside(): return lax.ppermute(value, ('ch', 'row'), pairs)  23.7 us
    all_to_all x1, blocking collectives, column_collect(): lax.all_to_all(spread, 'ch', 0, 0, tiled=True, axis_index_groups=groups)  23.3 us
    ppermute x3, waiting for transfers between devices, crossed(): lax.ppermute(value, 'ch', [(k, (k + chs // 2) % chs) for k in range(chs)])  22.4 us
    all_to_all x2, blocking collectives, image_collect(): lax.all_to_all(spread, ('ch', 'row'), 0, 0, tiled=True, axis_index_groups...  18.6 us
    ppermute x3, starting transfers between devices, from_beside(): return lax.ppermute(value, ('ch', 'row'), pairs)  13.2 us
    ppermute x2, starting transfers between devices, swapped(): return lax.ppermute(value, ('ch', 'row'), core_pairs())  12.2 us
    all_to_all x2, starting transfers between devices, column_collect(): lax.all_to_all(spread, 'ch', 0, 0, tiled=True, axis_index_groups=groups)  12 us
    pallas_call x2, Pallas kernels, conv(): call(functools.partial(conv_kernel, gots=len(gots)), [field, note], [VM]...  6.68 us
  transfers between devices with their start and end apart: 12, of which 9 were waited for; matrix products, arithmetic and copies ran while one was open for 2% of the time, Pallas kernels for 2%

profile of v5, /device:TPU:1, one launch (start us, length us, event | category | flops | bytes accessed | tf_op | source)
XLA Modules:
  0.0 166.7 jit_solution(6731966000935231738)
XLA Ops:
  0.0 1.5 copy-done
  2.4 1.2 shard_map.118
  3.7 5.3 %collective-permute-start.4 = (bf16[720,640]{1,0:T(8,128)(2,1)}, bf16[720,640]{1,0:T(8,128)(2,1)}, u32[]{:S(2)}, u32[]{:S(2)}) collective-permute-start(bf16[720,640]{1,0:T(8,128)(2,1)} %get-tuple-element.26), channel_id=1, source_target_pairs={{258,0},{259,1},{256,2},{257,3},{262,4},{263,5},{260,6},{261,7},{2... | collective-permute-start | bytes 2764808 | tf_op jit(solution)/shard_map/ppermute | solution.py:68
  9.1 5.5 %collective-permute-start = (f32[80,128]{1,0:T(8,128)S(1)}, f32[80,128]{1,0:T(8,128)S(1)}, u32[]{:S(2)}, u32[]{:S(2)}) collective-permute-start(f32[80,128]{1,0:T(8,128)S(1)} %get-tuple-element.23.own_ref), channel_id=1, source_target_pairs={{0,1},{1,0},{2,3},{3,2},{4,5},{5,4},{6,7},{7,6},{8,9},{9,8},{10,11... | collective-permute-start | bytes 122888 | tf_op jit(solution)/shard_map/ppermute | solution.py:49
  15.4 1.1 shard_map.119
  16.5 4.3 %all-to-all-start = ((bf16[16,80,256]{2,1,0:T(8,128)(2,1)}), bf16[16,80,256]{2,1,0:T(8,128)(2,1)S(1)}, u32[]{:S(2)}, u32[]{:S(2)}) async-start(bf16[16,80,256]{2,1,0:T(8,128)(2,1)} %shard_map.119), calls=%async_computation | async-start | bytes 1310720 | tf_op jit(solution)/shard_map/all_to_all | solution.py:404
  20.8 5.0 %collective-permute-done.4.refs_0_ = bf16[720,640]{1,0:T(8,128)(2,1)} collective-permute-done((bf16[720,640]{1,0:T(8,128)(2,1)}, bf16[720,640]{1,0:T(8,128)(2,1)}, u32[]{:S(2)}, u32[]{:S(2)}) %collective-permute-start.4) | collective-permute-done | bytes 921632 | tf_op jit(solution)/shard_map/ppermute | solution.py:68
  25.9 6.8 %collective-permute-start.5 = (bf16[720,640]{1,0:T(8,128)(2,1)}, bf16[720,640]{1,0:T(8,128)(2,1)}, u32[]{:S(2)}, u32[]{:S(2)}) collective-permute-start(bf16[720,640]{1,0:T(8,128)(2,1)} %collective-permute-done.4.refs_0_), channel_id=1, source_target_pairs={{0,1},{1,0},{2,3},{3,2},{4,5},{5,4},{6,7},{7,6},{8,9},{9,8},{10,11... | collective-permute-start | bytes 2764808 | tf_op jit(solution)/shard_map/ppermute | solution.py:49
  34.4 2.1 %collective-permute-start.6 = (f32[80,384]{1,0:T(8,128)S(1)}, f32[80,384]{1,0:T(8,128)S(1)}, u32[]{:S(2)}, u32[]{:S(2)}) collective-permute-start(f32[80,384]{1,0:T(8,128)S(1)} %shard_map.120), channel_id=1, source_target_pairs={{0,256},{32,288},{64,320},{96,352},{128,384},{160,416},{192,448},{... | collective-permute-start | bytes 368648 | tf_op jit(solution)/shard_map/ppermute | solution.py:54
  36.5 5.1 %collective-permute-done.6.refs_3_.mail_ref = f32[80,384]{1,0:T(8,128)S(1)} collective-permute-done((f32[80,384]{1,0:T(8,128)S(1)}, f32[80,384]{1,0:T(8,128)S(1)}, u32[]{:S(2)}, u32[]{:S(2)}) %collective-permute-start.6) | collective-permute-done | bytes 122912 | tf_op jit(solution)/shard_map/ppermute | solution.py:54
  41.6 3.9 %shard_map.121 = (f32[2,80,256]{2,1,0:T(8,128)S(1)}, bf16[4,176,128]{2,1,0:T(8,128)(2,1)}) custom-call(bf16[720,1280]{1,0:T(8,128)(2,1)S(1)} %bitcast.13, bf16[720,640]{1,0:T(8,128)(2,1)} %collective-permute-done.4.refs_0_, bf16[720,640]{1,0:T(8,128)(2,1)} %collective-permute-done.5.refs_1_, bf16[16,80,256]{2,1,0:T(8,128)(2,1)S(1)} %all-to-all-done.refs_2_, ...), custom_call_target="tpu_custom_call" | custom-call | tf_op jit(solution)/shard_map/pallas_call | solution.py:418
  45.4 4.0 %all-to-all-start.1 = ((bf16[4,176,128]{2,1,0:T(8,128)(2,1)}), bf16[4,176,128]{2,1,0:T(8,128)(2,1)S(1)}, u32[]{:S(2)}, u32[]{:S(2)}) async-start(bf16[4,176,128]{2,1,0:T(8,128)(2,1)} %get-tuple-element.30), calls=%async_computation.1 | async-start | bytes 360448 | tf_op jit(solution)/shard_map/all_to_all | solution.py:94
  49.5 2.4 %slice.6 = bf16[480,1280]{1,0:T(8,128)(2,1)} slice(bf16[720,1280]{1,0:T(8,128)(2,1)} %bitcast.14), slice={[0:480], [0:1280]} | slice | bytes 2457600 | tf_op jit(solution)/shard_map/slice | solution.py:412
  51.9 4.5 %collective-permute-start.2 = (bf16[480,1280]{1,0:T(8,128)(2,1)}, bf16[480,1280]{1,0:T(8,128)(2,1)}, u32[]{:S(2)}, u32[]{:S(2)}) collective-permute-start(bf16[480,1280]{1,0:T(8,128)(2,1)} %slice.6), channel_id=1, source_target_pairs={{258,0},{259,1},{256,2},{257,3},{262,4},{263,5},{260,6},{261,7},{2... | collective-permute-start | bytes 3686408 | tf_op jit(solution)/shard_map/ppermute | solution.py:68
  56.3 2.0 %shard_map.122 = bf16[8,2,80,256]{3,2,1,0:T(8,128)(2,1)} custom-call(f32[2,80,256]{2,1,0:T(8,128)S(1)} %get-tuple-element.29.part_ref, bf16[4,176,128]{2,1,0:T(8,128)(2,1)S(1)} %all-to-all-done.1.notes_ref, f32[1,80]{1,0:T(1,128)S(1)} %bitcast.23, f32[80,384]{1,0:T(8,128)S(1)} %collective-permute-done.6.refs_3_.mail_ref), custom_call_target="tpu_custom_call" | custom-call | tf_op jit(solution)/shard_map/pallas_call | solution.py:426
  58.3 6.7 %all-to-all-start.2 = ((bf16[8,2,80,256]{3,2,1,0:T(8,128)(2,1)}), bf16[8,2,80,256]{3,2,1,0:T(8,128)(2,1)S(1)}, u32[]{:S(2)}, u32[]{:S(2)}) async-start(bf16[8,2,80,256]{3,2,1,0:T(8,128)(2,1)} %shard_map.122), calls=%async_computation.2 | async-start | bytes 1310720 | tf_op jit(solution)/shard_map/all_to_all | solution.py:84
  65.0 1.9 %collective-permute-start.3 = (bf16[240,1280]{1,0:T(8,128)(2,1)S(1)}, bf16[240,1280]{1,0:T(8,128)(2,1)S(1)}, u32[]{:S(2)}, u32[]{:S(2)}) collective-permute-start(bf16[240,1280]{1,0:T(8,128)(2,1)S(1)} %slice.7), channel_id=1, source_target_pairs={{0,256},{32,288},{64,320},{96,352},{128,384},{160,416},{192,448},{... | collective-permute-start | bytes 1843208 | tf_op jit(solution)/shard_map/ppermute | solution.py:54
  67.0 14.5 %collective-permute-done.3.refs_1_ = bf16[240,1280]{1,0:T(8,128)(2,1)S(1)} collective-permute-done((bf16[240,1280]{1,0:T(8,128)(2,1)S(1)}, bf16[240,1280]{1,0:T(8,128)(2,1)S(1)}, u32[]{:S(2)}, u32[]{:S(2)}) %collective-permute-start.3) | collective-permute-done | bytes 614432 | tf_op jit(solution)/shard_map/ppermute | solution.py:54
  81.5 2.4 %collective-permute-done.2.refs_0_ = bf16[480,1280]{1,0:T(8,128)(2,1)} collective-permute-done((bf16[480,1280]{1,0:T(8,128)(2,1)}, bf16[480,1280]{1,0:T(8,128)(2,1)}, u32[]{:S(2)}, u32[]{:S(2)}) %collective-permute-start.2) | collective-permute-done | bytes 1228832 | tf_op jit(solution)/shard_map/ppermute | solution.py:68
  83.9 1.8 %all-to-all-done.2.refs_2_ = bf16[8,2,80,256]{3,2,1,0:T(8,128)(2,1)S(1)} async-done(((bf16[8,2,80,256]{3,2,1,0:T(8,128)(2,1)}), bf16[8,2,80,256]{3,2,1,0:T(8,128)(2,1)S(1)}, u32[]{:S(2)}, u32[]{:S(2)}) %all-to-all-start.2) | async-done | bytes 655392 | tf_op jit(solution)/shard_map/all_to_all | solution.py:84
  85.8 2.8 %shard_map.123 = (f32[2,80,256]{2,1,0:T(8,128)S(1)}, bf16[4,176,128]{2,1,0:T(8,128)(2,1)S(1)}) custom-call(bf16[720,1280]{1,0:T(8,128)(2,1)S(1)} %bitcast.16, bf16[480,1280]{1,0:T(8,128)(2,1)} %collective-permute-done.2.refs_0_, bf16[240,1280]{1,0:T(8,128)(2,1)S(1)} %collective-permute-done.3.refs_1_, bf16[8,2,80,256]{3,2,1,0:T(8,128)(2,1)S(1)} %all-to-all-done.2.refs_2_, ...), custom_call_target="tpu_custom_call" | custom-call | tf_op jit(solution)/shard_map/pallas_call | solution.py:418
  88.6 7.6 %all_to_all.35.notes_ref = bf16[4,176,128]{2,1,0:T(8,128)(2,1)S(1)} all-to-all(bf16[4,176,128]{2,1,0:T(8,128)(2,1)S(1)} %get-tuple-element.32), channel_id=1, replica_groups={{0,256,257,1},{32,288,289,33},{64,320,321,65},{96,352,353,97},{128,384,..., dimensions={0} | all-to-all | bytes 360448 | tf_op jit(solution)/shard_map/all_to_all | solution.py:94
  96.2 2.0 %shard_map.124 = (bf16[8,2,80,256]{3,2,1,0:T(8,128)(2,1)}, f32[2,80,256]{2,1,0:T(8,128)S(1)}) custom-call(f32[2,80,256]{2,1,0:T(8,128)S(1)} %get-tuple-element.31.part_ref, bf16[4,176,128]{2,1,0:T(8,128)(2,1)S(1)} %all_to_all.35.notes_ref, f32[1,80]{1,0:T(1,128)S(1)} %bitcast.25, f32[80,384]{1,0:T(8,128)S(1)} %collective-permute-done.6.refs_3_.mail_ref), custom_call_target="tpu_custom_call" | custom-call | tf_op jit(solution)/shard_map/pallas_call | solution.py:426
  98.2 5.3 %all-to-all-start.4 = ((bf16[8,2,80,256]{3,2,1,0:T(8,128)(2,1)}), bf16[8,2,80,256]{3,2,1,0:T(8,128)(2,1)S(1)}, u32[]{:S(2)}, u32[]{:S(2)}) async-start(bf16[8,2,80,256]{3,2,1,0:T(8,128)(2,1)} %get-tuple-element.33), calls=%async_computation.4 | async-start | bytes 1310720 | tf_op jit(solution)/shard_map/all_to_all | solution.py:84
  103.6 3.4 %collective-permute-start.1 = (bf16[272,1280]{1,0:T(8,128)(2,1)S(1)}, bf16[272,1280]{1,0:T(8,128)(2,1)S(1)}, u32[]{:S(2)}, u32[]{:S(2)}) collective-permute-start(bf16[272,1280]{1,0:T(8,128)(2,1)S(1)} %fusion.1), channel_id=1, source_target_pairs={{258,0},{259,1},{256,2},{257,3},{262,4},{263,5},{260,6},{261,7},{2... | collective-permute-start | bytes 2088968 | tf_op jit(solution)/shard_map/ppermute | solution.py:68
  107.0 16.2 %collective-permute-done.1.got_ref = bf16[272,1280]{1,0:T(8,128)(2,1)S(1)} collective-permute-done((bf16[272,1280]{1,0:T(8,128)(2,1)S(1)}, bf16[272,1280]{1,0:T(8,128)(2,1)S(1)}, u32[]{:S(2)}, u32[]{:S(2)}) %collective-permute-start.1) | collective-permute-done | bytes 696352 | tf_op jit(solution)/shard_map/ppermute | solution.py:68
  123.2 1.1 all-to-all-done.4.full_ref
  124.8 11.0 %all_to_all.36.pairs_ref = bf16[4,2,128,256]{3,2,1,0:T(8,128)(2,1)S(1)} all-to-all(bf16[4,2,128,256]{3,2,1,0:T(8,128)(2,1)S(1)} %get-tuple-element.35), channel_id=1, replica_groups={{0,256,257,1},{32,288,289,33},{64,320,321,65},{96,352,353,97},{128,384,..., dimensions={0} | all-to-all | bytes 1048576 | tf_op jit(solution)/shard_map/all_to_all | solution.py:94
  135.8 1.8 %shard_map.126 = bf16[8,2,64,256]{3,2,1,0:T(8,128)(2,1)S(1)} custom-call(bf16[2,64,256]{2,1,0:T(8,128)(2,1)S(1)} %get-tuple-element.34.q_ref, bf16[4,2,128,256]{3,2,1,0:T(8,128)(2,1)S(1)} %all_to_all.36.pairs_ref), custom_call_target="tpu_custom_call" | custom-call | tf_op jit(solution)/shard_map/pallas_call | solution.py:445
  137.6 23.3 %all_to_all.37.full_ref = bf16[8,2,64,256]{3,2,1,0:T(8,128)(2,1)S(1)} all-to-all(bf16[8,2,64,256]{3,2,1,0:T(8,128)(2,1)S(1)} %shard_map.126), channel_id=1, replica_groups={{0,32,64,96,128,160,192,224},{256,288,320,352,384,416,448,480},{1,33,65..., dimensions={0} | all-to-all | bytes 1048576 | tf_op jit(solution)/shard_map/all_to_all | solution.py:84
  161.1 1.9 %collective-permute-start.7 = (bf16[80,256]{1,0:T(8,128)(2,1)S(1)}, bf16[80,256]{1,0:T(8,128)(2,1)S(1)}, u32[]{:S(2)}, u32[]{:S(2)}) collective-permute-start(bf16[80,256]{1,0:T(8,128)(2,1)S(1)} %get-tuple-element.38), channel_id=1, source_target_pairs={{0,256},{32,288},{64,320},{96,352},{128,384},{160,416},{192,448},{... | collective-permute-start | bytes 122888 | tf_op jit(solution)/shard_map/ppermute | solution.py:54
  163.1 2.8 %collective-permute-done.7.peer_ref = bf16[80,256]{1,0:T(8,128)(2,1)S(1)} collective-permute-done((bf16[80,256]{1,0:T(8,128)(2,1)S(1)}, bf16[80,256]{1,0:T(8,128)(2,1)S(1)}, u32[]{:S(2)}, u32[]{:S(2)}) %collective-permute-start.7) | collective-permute-done | bytes 40992 | tf_op jit(solution)/shard_map/ppermute | solution.py:54
  (42 shorter events, 4.4 us)
Async XLA Ops:
  0.0 15.4 %copy-start.12 = (f32[80]{0:T(128)S(1)}, f32[80]{0:T(128)}, u32[]{:S(2)}) copy-start(f32[80]{0:T(128)} %param.14) | copy-start | bytes 964
  0.0 1.5 copy-start
  1.5 0.9 copy-start.3
  3.6 29.0 %copy-start.13 = (s32[16]{0:T(128)S(1)}, s32[16]{0:T(128)}, u32[]{:S(2)}) copy-start(s32[16]{0:T(128)} %param.13) | copy-start | bytes 196
  3.7 30.5 %copy-start.4 = (bf16[16,32,80]{2,1,0:T(8,128)(2,1)S(1)}, bf16[16,32,80]{2,1,0:T(8,128)(2,1)}, u32[]{:S(2)}) copy-start(bf16[16,32,80]{2,1,0:T(8,128)(2,1)} %param.12) | copy-start | bytes 245764
  3.7 30.5 %copy-start.9 = (bf16[320,80]{0,1:T(8,128)(2,1)S(1)}, bf16[320,80]{0,1:T(8,128)(2,1)}, u32[]{:S(2)}) copy-start(bf16[320,80]{0,1:T(8,128)(2,1)} %param.16) | copy-start | bytes 153604
  3.7 30.4 %copy-start.10 = (f32[80]{0:T(128)S(1)}, f32[80]{0:T(128)}, u32[]{:S(2)}) copy-start(f32[80]{0:T(128)} %param.17) | copy-start | bytes 964
  3.7 30.4 %copy-start.11 = (f32[80]{0:T(128)S(1)}, f32[80]{0:T(128)}, u32[]{:S(2)}) copy-start(f32[80]{0:T(128)} %param.19) | copy-start | bytes 964
  3.7 37.9 %copy-start.1 = (bf16[80,3,3,1280]{3,0,2,1:T(8,128)(2,1)S(1)}, bf16[80,3,3,1280]{3,0,2,1:T(8,128)(2,1)}, u32[]{:S(2)}) copy-start(bf16[80,3,3,1280]{3,0,2,1:T(8,128)(2,1)} %param.15) | copy-start | bytes 5529604
  3.7 22.2 %collective-permute-start.4 = (bf16[720,640]{1,0:T(8,128)(2,1)}, bf16[720,640]{1,0:T(8,128)(2,1)}, u32[]{:S(2)}, u32[]{:S(2)}) collective-permute-start(bf16[720,640]{1,0:T(8,128)(2,1)} %get-tuple-element.26), channel_id=1, source_target_pairs={{258,0},{259,1},{256,2},{257,3},{262,4},{263,5},{260,6},{261,7},{2... | collective-permute-start | bytes 2764808 | tf_op jit(solution)/shard_map/ppermute | solution.py:68
  9.1 6.3 %collective-permute-start = (f32[80,128]{1,0:T(8,128)S(1)}, f32[80,128]{1,0:T(8,128)S(1)}, u32[]{:S(2)}, u32[]{:S(2)}) collective-permute-start(f32[80,128]{1,0:T(8,128)S(1)} %get-tuple-element.23.own_ref), channel_id=1, source_target_pairs={{0,1},{1,0},{2,3},{3,2},{4,5},{5,4},{6,7},{7,6},{8,9},{9,8},{10,11... | collective-permute-start | bytes 122888 | tf_op jit(solution)/shard_map/ppermute | solution.py:49
  16.5 25.1 %all-to-all-start = ((bf16[16,80,256]{2,1,0:T(8,128)(2,1)}), bf16[16,80,256]{2,1,0:T(8,128)(2,1)S(1)}, u32[]{:S(2)}, u32[]{:S(2)}) async-start(bf16[16,80,256]{2,1,0:T(8,128)(2,1)} %shard_map.119), calls=%async_computation | async-start | bytes 1310720 | tf_op jit(solution)/shard_map/all_to_all | solution.py:404
  25.9 15.7 %collective-permute-start.5 = (bf16[720,640]{1,0:T(8,128)(2,1)}, bf16[720,640]{1,0:T(8,128)(2,1)}, u32[]{:S(2)}, u32[]{:S(2)}) collective-permute-start(bf16[720,640]{1,0:T(8,128)(2,1)} %collective-permute-done.4.refs_0_), channel_id=1, source_target_pairs={{0,1},{1,0},{2,3},{3,2},{4,5},{5,4},{6,7},{7,6},{8,9},{9,8},{10,11... | collective-permute-start | bytes 2764808 | tf_op jit(solution)/shard_map/ppermute | solution.py:49
  34.4 7.2 %collective-permute-start.6 = (f32[80,384]{1,0:T(8,128)S(1)}, f32[80,384]{1,0:T(8,128)S(1)}, u32[]{:S(2)}, u32[]{:S(2)}) collective-permute-start(f32[80,384]{1,0:T(8,128)S(1)} %shard_map.120), channel_id=1, source_target_pairs={{0,256},{32,288},{64,320},{96,352},{128,384},{160,416},{192,448},{... | collective-permute-start | bytes 368648 | tf_op jit(solution)/shard_map/ppermute | solution.py:54
  45.4 10.9 %all-to-all-start.1 = ((bf16[4,176,128]{2,1,0:T(8,128)(2,1)}), bf16[4,176,128]{2,1,0:T(8,128)(2,1)S(1)}, u32[]{:S(2)}, u32[]{:S(2)}) async-start(bf16[4,176,128]{2,1,0:T(8,128)(2,1)} %get-tuple-element.30), calls=%async_computation.1 | async-start | bytes 360448 | tf_op jit(solution)/shard_map/all_to_all | solution.py:94
  51.9 13.1 %copy-start.2 = (bf16[80,3,3,1280]{3,0,2,1:T(8,128)(2,1)S(1)}, bf16[80,3,3,1280]{3,0,2,1:T(8,128)(2,1)}, u32[]{:S(2)}) copy-start(bf16[80,3,3,1280]{3,0,2,1:T(8,128)(2,1)} %param.18) | copy-start | bytes 5529604
  51.9 32.1 %collective-permute-start.2 = (bf16[480,1280]{1,0:T(8,128)(2,1)}, bf16[480,1280]{1,0:T(8,128)(2,1)}, u32[]{:S(2)}, u32[]{:S(2)}) collective-permute-start(bf16[480,1280]{1,0:T(8,128)(2,1)} %slice.6), channel_id=1, source_target_pairs={{258,0},{259,1},{256,2},{257,3},{262,4},{263,5},{260,6},{261,7},{2... | collective-permute-start | bytes 3686408 | tf_op jit(solution)/shard_map/ppermute | solution.py:68
  58.3 27.5 %all-to-all-start.2 = ((bf16[8,2,80,256]{3,2,1,0:T(8,128)(2,1)}), bf16[8,2,80,256]{3,2,1,0:T(8,128)(2,1)S(1)}, u32[]{:S(2)}, u32[]{:S(2)}) async-start(bf16[8,2,80,256]{3,2,1,0:T(8,128)(2,1)} %shard_map.122), calls=%async_computation.2 | async-start | bytes 1310720 | tf_op jit(solution)/shard_map/all_to_all | solution.py:84
  65.0 16.5 %collective-permute-start.3 = (bf16[240,1280]{1,0:T(8,128)(2,1)S(1)}, bf16[240,1280]{1,0:T(8,128)(2,1)S(1)}, u32[]{:S(2)}, u32[]{:S(2)}) collective-permute-start(bf16[240,1280]{1,0:T(8,128)(2,1)S(1)} %slice.7), channel_id=1, source_target_pairs={{0,256},{32,288},{64,320},{96,352},{128,384},{160,416},{192,448},{... | collective-permute-start | bytes 1843208 | tf_op jit(solution)/shard_map/ppermute | solution.py:54
  88.6 14.9 %copy-start.5 = (bf16[64,1280]{1,0:T(8,128)(2,1)S(1)}, bf16[64,1280]{1,0:T(8,128)(2,1)}, u32[]{:S(2)}) copy-start(bf16[64,1280]{1,0:T(8,128)(2,1)} %value_ref.1) | copy-start | bytes 491524
  88.6 14.9 %copy-start.6 = (bf16[64,1280]{1,0:T(8,128)(2,1)S(1)}, bf16[64,1280]{1,0:T(8,128)(2,1)}, u32[]{:S(2)}) copy-start(bf16[64,1280]{1,0:T(8,128)(2,1)} %key_ref.1) | copy-start | bytes 491524
  88.6 14.9 %copy-start.7 = (bf16[64,1280]{1,0:T(8,128)(2,1)S(1)}, bf16[64,1280]{1,0:T(8,128)(2,1)}, u32[]{:S(2)}) copy-start(bf16[64,1280]{1,0:T(8,128)(2,1)} %query_ref.1) | copy-start | bytes 491524
  88.6 14.9 %copy-start.8 = (bf16[80,1024]{1,0:T(8,128)(2,1)S(1)}, bf16[80,1024]{1,0:T(8,128)(2,1)}, u32[]{:S(2)}) copy-start(bf16[80,1024]{1,0:T(8,128)(2,1)} %weight_ref.1) | copy-start | bytes 491524
  98.2 26.1 %all-to-all-start.4 = ((bf16[8,2,80,256]{3,2,1,0:T(8,128)(2,1)}), bf16[8,2,80,256]{3,2,1,0:T(8,128)(2,1)S(1)}, u32[]{:S(2)}, u32[]{:S(2)}) async-start(bf16[8,2,80,256]{3,2,1,0:T(8,128)(2,1)} %get-tuple-element.33), calls=%async_computation.4 | async-start | bytes 1310720 | tf_op jit(solution)/shard_map/all_to_all | solution.py:84
  103.6 19.6 %collective-permute-start.1 = (bf16[272,1280]{1,0:T(8,128)(2,1)S(1)}, bf16[272,1280]{1,0:T(8,128)(2,1)S(1)}, u32[]{:S(2)}, u32[]{:S(2)}) collective-permute-start(bf16[272,1280]{1,0:T(8,128)(2,1)S(1)} %fusion.1), channel_id=1, source_target_pairs={{258,0},{259,1},{256,2},{257,3},{262,4},{263,5},{260,6},{261,7},{2... | collective-permute-start | bytes 2088968 | tf_op jit(solution)/shard_map/ppermute | solution.py:68
  161.1 4.7 %collective-permute-start.7 = (bf16[80,256]{1,0:T(8,128)(2,1)S(1)}, bf16[80,256]{1,0:T(8,128)(2,1)S(1)}, u32[]{:S(2)}, u32[]{:S(2)}) collective-permute-start(bf16[80,256]{1,0:T(8,128)(2,1)S(1)} %get-tuple-element.38), channel_id=1, source_target_pairs={{0,256},{32,288},{64,320},{96,352},{128,384},{160,416},{192,448},{... | collective-permute-start | bytes 122888 | tf_op jit(solution)/shard_map/ppermute | solution.py:54

commit v6 on v5

--- a/solution.py
+++ b/solution.py
@@ -25,14 +25,14 @@
 FAR = pl.BlockSpec(memory_space=pltpu.HBM)
 
 
-def call(kernel, outs, specs, scratch=()):
+def call(kernel, outs, specs, scratch=(), limit=20 * 2**20):
     return pl.pallas_call(
         kernel,
         out_shape=[jax.ShapeDtypeStruct(s, d) for s, d in outs],
         in_specs=specs,
         out_specs=[VM] * len(outs),
         scratch_shapes=list(scratch),
-        compiler_params=pltpu.CompilerParams(vmem_limit_bytes=20 * 2**20),
+        compiler_params=pltpu.CompilerParams(vmem_limit_bytes=limit),
     )
 
 
@@ -187,9 +187,8 @@
 def both(own, gots, whole_ref):
     mine = jnp.dot(own, whole_ref[...], preferred_element_type=F32)
     depth = gots[0].shape[1]
-    if depth == own.shape[1]:
-        pieces = [jnp.dot(got, whole_ref[...], preferred_element_type=F32) for got in gots]
-        return mine, jnp.concatenate(pieces, axis=0)
+    if len(gots) == 1:
+        return mine, jnp.dot(gots[0], whole_ref[...], preferred_element_type=F32)
     _, core, _ = spot()
     near = whole_ref[pl.ds(pl.multiple_of(core * depth, 128), depth), :]
     far = whole_ref[pl.ds(pl.multiple_of((1 - core) * depth, 128), depth), :]
@@ -377,11 +376,6 @@
     def tall(weight):
         return jnp.transpose(weight, (1, 2, 0, 3)).reshape(9 * count, C)
 
-    step_value = jnp.sum(jnp.where(jnp.arange(timestep.shape[0]) == image_id, timestep, 0)).astype(F32)
-    half = TDIM // 2
-    freqs = jnp.exp(-math.log(10000.0) * jnp.arange(half, dtype=F32) / half)
-    angles = step_value * freqs
-    sinus = jnp.concatenate([jnp.cos(angles), jnp.sin(angles)])[None, :].astype(BF16)
     field = ((2, count, share), F32)
     half_chs = chs // 2
     active = ((half_chs, 2, count, share), BF16)
@@ -396,30 +390,35 @@
         [((count, tokens), F32), ((count, 128), F32), ((9 * count, C // 2), BF16)],
         [VM, FAR],
         [pltpu.SemaphoreType.DMA],
+        limit=65_500_000,
     )(flat, own_a)
     peer = swapped(sums)
     got_a = from_beside(half_a)
     (spread_a,) = call(first_kernel, [((chs, count, share), BF16)], [VM] * 4)(turned, sums, peer, gain_a)
 
     full = lax.all_to_all(spread_a, "ch", 0, 0, tiled=True)
+    step_value = jnp.sum(jnp.where(jnp.arange(timestep.shape[0]) == image_id, after(timestep, spread_a), 0)).astype(F32)
+    half = TDIM // 2
+    freqs = jnp.exp(-math.log(10000.0) * jnp.arange(half, dtype=F32) / half)
+    angles = step_value * freqs
+    sinus = jnp.concatenate([jnp.cos(angles), jnp.sin(angles)])[None, :].astype(BF16)
     (mail,) = call(mail_kernel, [((count, share + 128), F32)], [VM] * 5)(
         time_weight.T, sinus, gain_b, gain_c, after(flat, spread_a)
     )
     mail = crossed(mail)
-    cut = 6 * count
-    late_b = after(own_b, spread_a)
-    low_b = crossed(late_b[cut:])
-    high_b = from_beside(late_b[:cut])
-    late = [w_query, w_key, w_value, jnp.pad(w_out, ((0, 0), (0, C - w_out.shape[1])))]
-    got_c = from_beside(after(jnp.concatenate(late, axis=0), spread_a))
+    got_b = from_beside(after(own_b, spread_a))
+    *late, late_out = [after(weight, spread_a) for weight in (w_query, w_key, w_value, w_out)]
+    late.append(jnp.pad(late_out, ((0, 0), (0, C - w_out.shape[1]))))
+    got_c = from_beside(jnp.concatenate(late, axis=0))
     other_a = swapped(after(got_a, spread_a))
 
-    def conv(full, own, gots, *bases):
+    def conv(limit, full, own, gots, *bases):
         return call(
             functools.partial(conv_kernel, gots=len(gots)),
             [field, note],
             [VM] * (3 + len(gots) + len(bases)),
             [whole],
+            limit=limit,
         )(own, *gots, full, mail, *bases)
 
     def finish(part, notes, gain, act, lane_of, outs):
@@ -427,13 +426,13 @@
             functools.partial(finish_kernel, act=act, lane_of=lane_of), outs, [VM] * 4
         )(part, notes, gain, mail)
 
-    part_a, note_a = conv(full, own_a, [got_a, other_a], time_weight.T, sinus)
+    part_a, note_a = conv(20 * 2**20, full, own_a, [got_a, other_a], time_weight.T, sinus)
     notes_a = image_collect(note_a)
     (spread_b,) = finish(part_a, notes_a, gain_b, True, 1, [active])
-    part_b, note_b = conv(column_collect(spread_b), own_b, [high_b, low_b], flat)
+    part_b, note_b = conv(65_000_000, column_collect(spread_b), own_b, [got_b], flat)
     notes_b = image_collect(note_b)
     spread_c, hidden_b = finish(part_b, notes_b, gain_c, False, 2, [active, field])
-    features = column_collect(spread_c)
+    features = column_collect(after(spread_c, got_c))
 
     query, key_value = call(
         project_kernel,

time: 169 us -> 165 us (0.976)
  blocking collectives: 41.9 us -> 71.3 us
  waiting for transfers between devices: 49.9 us -> 29.4 us
  starting transfers between devices: 51.8 us -> 39.3 us
  local copies, waits for them, and re-layouts: 4.94 us -> 2.69 us
  Pallas kernels: 16.4 us -> 18.6 us
    all_to_all x1 -> x2, blocking collectives: 23.3 us -> 43.5 us  [column_collect(): lax.all_to_all(spread, 'ch', 0, 0, tiled=True, axis_index_groups=groups)]
    ppermute x3 -> x2, waiting for transfers between devices: 22.4 us -> 7.33 us  [crossed(): lax.ppermute(value, 'ch', [(k, (k + chs // 2) % chs) for k in range(chs)])]
    ppermute x3, waiting for transfers between devices: 23.7 us -> 12 us  [from_beside(): return lax.ppermute(value, ('ch', 'row'), pairs)]
    all_to_all x2 -> x3, blocking collectives: 18.6 us -> 27.8 us  [image_collect(): lax.all_to_all(spread, ('ch', 'row'), 0, 0, tiled=True, axis_index_groups...]
    all_to_all x2 -> x1, waiting for transfers between devices: 2.9 us -> 9.06 us  [column_collect(): lax.all_to_all(spread, 'ch', 0, 0, tiled=True, axis_index_groups=groups)]
    all_to_all x2 -> x1, starting transfers between devices: 12 us -> 6.82 us  [column_collect(): lax.all_to_all(spread, 'ch', 0, 0, tiled=True, axis_index_groups=groups)]
    all_to_all x1 -> x0, starting transfers between devices: 4.02 us -> none  [image_collect(): lax.all_to_all(spread, ('ch', 'row'), 0, 0, tiled=True, axis_index_groups...]
    slice x2 -> x0, local copies, waits for them, and re-layouts: 2.44 us -> none  [the longest x1 2.4 us: body(): high_b = from_beside(late_b[:cut])]
  transfers between devices with their start and end apart: 12 -> 9, of which waited for: 9 -> 6; matrix products, arithmetic and copies ran while one was open for 2% -> 1% of each run, Pallas kernels for 2% -> 7%
where the time goes in v6:
time: 165 us; the launch traced here: 164 us
  blocking collectives  71.3 us (43%)
  starting transfers between devices  39.3 us (24%)
  waiting for transfers between devices  29.4 us (18%)
  Pallas kernels  18.6 us (11%)
  local copies, waits for them, and re-layouts  2.69 us (2%)
  other arithmetic  1.67 us (1%)
    all_to_all x2, blocking collectives, column_collect(): lax.all_to_all(spread, 'ch', 0, 0, tiled=True, axis_index_groups=groups)  43.5 us
    all_to_all x3, blocking collectives, image_collect(): lax.all_to_all(spread, ('ch', 'row'), 0, 0, tiled=True, axis_index_groups...  27.8 us
    ppermute x2, starting transfers between devices, swapped(): return lax.ppermute(value, ('ch', 'row'), core_pairs())  12.2 us
    ppermute x3, waiting for transfers between devices, from_beside(): return lax.ppermute(value, ('ch', 'row'), pairs)  12 us
    ppermute x3, starting transfers between devices, from_beside(): return lax.ppermute(value, ('ch', 'row'), pairs)  12 us
    all_to_all x1, waiting for transfers between devices, column_collect(): lax.all_to_all(spread, 'ch', 0, 0, tiled=True, axis_index_groups=groups)  9.06 us
    pallas_call x2, Pallas kernels, conv(): call(functools.partial(conv_kernel, gots=len(gots)), [field, note], [VM]...  7.74 us
    ppermute x2, waiting for transfers between devices, crossed(): lax.ppermute(value, 'ch', [(k, (k + chs // 2) % chs) for k in range(chs)])  7.33 us
  transfers between devices with their start and end apart: 9, of which 6 were waited for; matrix products, arithmetic and copies ran while one was open for 1% of the time, Pallas kernels for 7%

profile of v6, /device:TPU:1, one launch (start us, length us, event | category | flops | bytes accessed | tf_op | source)
XLA Modules:
  0.0 164.0 jit_solution(9238062807380789358)
XLA Ops:
  0.0 3.2 %shard_map.118 = (f32[80,512]{1,0:T(8,128)}, f32[80,128]{1,0:T(8,128)}, bf16[720,640]{1,0:T(8,128)(2,1)}) custom-call(bf16[512,80]{1,0:T(8,128)(2,1)} %bitcast.14, bf16[720,1280]{1,0:T(8,128)(2,1)} %bitcast.12), custom_call_target="tpu_custom_call" | custom-call | tf_op jit(solution)/shard_map/pallas_call | solution.py:388
  3.2 5.3 %collective-permute-start.3 = (bf16[720,640]{1,0:T(8,128)(2,1)}, bf16[720,640]{1,0:T(8,128)(2,1)}, u32[]{:S(2)}, u32[]{:S(2)}) collective-permute-start(bf16[720,640]{1,0:T(8,128)(2,1)} %get-tuple-element.34), channel_id=1, source_target_pairs={{258,0},{259,1},{256,2},{257,3},{262,4},{263,5},{260,6},{261,7},{2... | collective-permute-start | bytes 2764808 | tf_op jit(solution)/shard_map/ppermute | solution.py:68
  8.6 5.5 %collective-permute-start = (f32[80,128]{1,0:T(8,128)}, f32[80,128]{1,0:T(8,128)S(1)}, u32[]{:S(2)}, u32[]{:S(2)}) collective-permute-start(f32[80,128]{1,0:T(8,128)} %get-tuple-element.28.own_ref), channel_id=1, source_target_pairs={{0,1},{1,0},{2,3},{3,2},{4,5},{5,4},{6,7},{7,6},{8,9},{9,8},{10,11... | collective-permute-start | bytes 122888 | tf_op jit(solution)/shard_map/ppermute | solution.py:49
  14.0 1.1 collective-permute-done.peer_ref
  15.1 0.9 copy-done.10
  16.0 0.8 copy-done.11
  16.8 1.1 shard_map.119
  17.9 4.3 %all-to-all-start = ((bf16[16,80,256]{2,1,0:T(8,128)(2,1)}), bf16[16,80,256]{2,1,0:T(8,128)(2,1)S(1)}, u32[]{:S(2)}, u32[]{:S(2)}) async-start(bf16[16,80,256]{2,1,0:T(8,128)(2,1)} %shard_map.119), calls=%async_computation | async-start | bytes 1310720 | tf_op jit(solution)/shard_map/all_to_all | solution.py:399
  22.2 3.1 %collective-permute-done.3.refs_0_ = bf16[720,640]{1,0:T(8,128)(2,1)} collective-permute-done((bf16[720,640]{1,0:T(8,128)(2,1)}, bf16[720,640]{1,0:T(8,128)(2,1)}, u32[]{:S(2)}, u32[]{:S(2)}) %collective-permute-start.3) | collective-permute-done | bytes 921632 | tf_op jit(solution)/shard_map/ppermute | solution.py:68
  25.4 6.8 %collective-permute-start.4 = (bf16[720,640]{1,0:T(8,128)(2,1)}, bf16[720,640]{1,0:T(8,128)(2,1)}, u32[]{:S(2)}, u32[]{:S(2)}) collective-permute-start(bf16[720,640]{1,0:T(8,128)(2,1)} %collective-permute-done.3.refs_0_), channel_id=1, source_target_pairs={{0,1},{1,0},{2,3},{3,2},{4,5},{5,4},{6,7},{7,6},{8,9},{9,8},{10,11... | collective-permute-start | bytes 2764808 | tf_op jit(solution)/shard_map/ppermute | solution.py:49
  32.2 4.6 %collective-permute-start.2 = (bf16[720,1280]{1,0:T(8,128)(2,1)}, bf16[720,1280]{1,0:T(8,128)(2,1)}, u32[]{:S(2)}, u32[]{:S(2)}) collective-permute-start(bf16[720,1280]{1,0:T(8,128)(2,1)} %bitcast.24), channel_id=1, source_target_pairs={{258,0},{259,1},{256,2},{257,3},{262,4},{263,5},{260,6},{261,7},{2... | collective-permute-start | bytes 5529608 | tf_op jit(solution)/shard_map/ppermute | solution.py:68
  38.5 1.9 %collective-permute-start.5 = (f32[80,384]{1,0:T(8,128)S(1)}, f32[80,384]{1,0:T(8,128)S(1)}, u32[]{:S(2)}, u32[]{:S(2)}) collective-permute-start(f32[80,384]{1,0:T(8,128)S(1)} %shard_map.120), channel_id=1, source_target_pairs={{0,256},{32,288},{64,320},{96,352},{128,384},{160,416},{192,448},{... | collective-permute-start | bytes 368648 | tf_op jit(solution)/shard_map/ppermute | solution.py:54
  40.4 4.7 %collective-permute-done.5.refs_3_.mail_ref.refs_2_ = f32[80,384]{1,0:T(8,128)S(1)} collective-permute-done((f32[80,384]{1,0:T(8,128)S(1)}, f32[80,384]{1,0:T(8,128)S(1)}, u32[]{:S(2)}, u32[]{:S(2)}) %collective-permute-start.5) | collective-permute-done | bytes 122912 | tf_op jit(solution)/shard_map/ppermute | solution.py:54
  45.1 3.2 %shard_map.121 = (f32[2,80,256]{2,1,0:T(8,128)S(1)}, bf16[4,176,128]{2,1,0:T(8,128)(2,1)S(1)}) custom-call(bf16[720,1280]{1,0:T(8,128)(2,1)S(1)} %bitcast.13, bf16[720,640]{1,0:T(8,128)(2,1)} %collective-permute-done.3.refs_0_, bf16[720,640]{1,0:T(8,128)(2,1)} %collective-permute-done.4.refs_1_, bf16[16,80,256]{2,1,0:T(8,128)(2,1)S(1)} %all-to-all-done.refs_2_, ...), custom_call_target="tpu_custom_call" | custom-call | tf_op jit(solution)/shard_map/pallas_call | solution.py:416
  48.3 8.4 %all_to_all.35.notes_ref = bf16[4,176,128]{2,1,0:T(8,128)(2,1)S(1)} all-to-all(bf16[4,176,128]{2,1,0:T(8,128)(2,1)S(1)} %get-tuple-element.39), channel_id=1, replica_groups={{0,256,257,1},{32,288,289,33},{64,320,321,65},{96,352,353,97},{128,384,..., dimensions={0} | all-to-all | bytes 360448 | tf_op jit(solution)/shard_map/all_to_all | solution.py:94
  56.7 2.0 %shard_map.122 = bf16[8,2,80,256]{3,2,1,0:T(8,128)(2,1)} custom-call(f32[2,80,256]{2,1,0:T(8,128)S(1)} %get-tuple-element.38.part_ref, bf16[4,176,128]{2,1,0:T(8,128)(2,1)S(1)} %all_to_all.35.notes_ref, f32[1,80]{1,0:T(1,128)S(1)} %bitcast.20, f32[80,384]{1,0:T(8,128)S(1)} %collective-permute-done.5.refs_3_.mail_ref.refs_2_), custom_call_target="tpu_custom_call" | custom-call | tf_op jit(solution)/shard_map/pallas_call | solution.py:425
  58.7 6.8 %all-to-all-start.2 = ((bf16[8,2,80,256]{3,2,1,0:T(8,128)(2,1)}), bf16[8,2,80,256]{3,2,1,0:T(8,128)(2,1)}, u32[]{:S(2)}, u32[]{:S(2)}) async-start(bf16[8,2,80,256]{3,2,1,0:T(8,128)(2,1)} %shard_map.122), calls=%async_computation.2 | async-start | bytes 1310720 | tf_op jit(solution)/shard_map/all_to_all | solution.py:84
  65.5 0.9 fusion.1
  66.4 2.0 %collective-permute-start.1 = (bf16[272,1280]{1,0:T(8,128)(2,1)}, bf16[272,1280]{1,0:T(8,128)(2,1)S(1)}, u32[]{:S(2)}, u32[]{:S(2)}) collective-permute-start(bf16[272,1280]{1,0:T(8,128)(2,1)} %fusion.1), channel_id=1, source_target_pairs={{258,0},{259,1},{256,2},{257,3},{262,4},{263,5},{260,6},{261,7},{2... | collective-permute-start | bytes 2088968 | tf_op jit(solution)/shard_map/ppermute | solution.py:68
  68.5 8.8 %collective-permute-done.2.refs_0_ = bf16[720,1280]{1,0:T(8,128)(2,1)} collective-permute-done((bf16[720,1280]{1,0:T(8,128)(2,1)}, bf16[720,1280]{1,0:T(8,128)(2,1)}, u32[]{:S(2)}, u32[]{:S(2)}) %collective-permute-start.2) | collective-permute-done | bytes 1843232 | tf_op jit(solution)/shard_map/ppermute | solution.py:68
  77.3 9.1 %all-to-all-done.2.refs_1_ = bf16[8,2,80,256]{3,2,1,0:T(8,128)(2,1)} async-done(((bf16[8,2,80,256]{3,2,1,0:T(8,128)(2,1)}), bf16[8,2,80,256]{3,2,1,0:T(8,128)(2,1)}, u32[]{:S(2)}, u32[]{:S(2)}) %all-to-all-start.2) | async-done | bytes 655392 | tf_op jit(solution)/shard_map/all_to_all | solution.py:84
  86.4 4.5 %shard_map.123 = (f32[2,80,256]{2,1,0:T(8,128)}, bf16[4,176,128]{2,1,0:T(8,128)(2,1)}) custom-call(bf16[720,1280]{1,0:T(8,128)(2,1)} %bitcast.25, bf16[720,1280]{1,0:T(8,128)(2,1)} %collective-permute-done.2.refs_0_, bf16[8,2,80,256]{3,2,1,0:T(8,128)(2,1)} %all-to-all-done.2.refs_1_, f32[80,384]{1,0:T(8,128)} %copy-done.1, bf16[512,80]{1,0:T(8,128)(2,1)} %bitcast.15), custom_call_target="tpu_custom_call" | custom-call | tf_op jit(solution)/shard_map/pallas_call | solution.py:416
  90.9 8.4 %all_to_all.36.notes_ref = bf16[4,176,128]{2,1,0:T(8,128)(2,1)S(1)} all-to-all(bf16[4,176,128]{2,1,0:T(8,128)(2,1)} %get-tuple-element.41), channel_id=1, replica_groups={{0,256,257,1},{32,288,289,33},{64,320,321,65},{96,352,353,97},{128,384,..., dimensions={0} | all-to-all | bytes 360448 | tf_op jit(solution)/shard_map/all_to_all | solution.py:94
  99.3 0.9 copy-done.9
  100.2 1.1 shard_map.124
  101.4 23.1 %all_to_all.37.full_ref = bf16[8,2,80,256]{3,2,1,0:T(8,128)(2,1)S(1)} all-to-all(bf16[8,2,80,256]{3,2,1,0:T(8,128)(2,1)S(1)} %get-tuple-element.43), channel_id=1, replica_groups={{0,32,64,96,128,160,192,224},{256,288,320,352,384,416,448,480},{1,33,65..., dimensions={0} | all-to-all | bytes 1310720 | tf_op jit(solution)/shard_map/all_to_all | solution.py:84
  124.9 11.1 %all_to_all.38.pairs_ref = bf16[4,2,128,256]{3,2,1,0:T(8,128)(2,1)S(1)} all-to-all(bf16[4,2,128,256]{3,2,1,0:T(8,128)(2,1)S(1)} %get-tuple-element.45), channel_id=1, replica_groups={{0,256,257,1},{32,288,289,33},{64,320,321,65},{96,352,353,97},{128,384,..., dimensions={0} | all-to-all | bytes 1048576 | tf_op jit(solution)/shard_map/all_to_all | solution.py:94
  136.0 1.8 %shard_map.126 = bf16[8,2,64,256]{3,2,1,0:T(8,128)(2,1)S(1)} custom-call(bf16[2,64,256]{2,1,0:T(8,128)(2,1)S(1)} %get-tuple-element.44.q_ref, bf16[4,2,128,256]{3,2,1,0:T(8,128)(2,1)S(1)} %all_to_all.38.pairs_ref), custom_call_target="tpu_custom_call" | custom-call | tf_op jit(solution)/shard_map/pallas_call | solution.py:444
  137.8 20.4 %all_to_all.39.full_ref = bf16[8,2,64,256]{3,2,1,0:T(8,128)(2,1)S(1)} all-to-all(bf16[8,2,64,256]{3,2,1,0:T(8,128)(2,1)S(1)} %shard_map.126), channel_id=1, replica_groups={{0,32,64,96,128,160,192,224},{256,288,320,352,384,416,448,480},{1,33,65..., dimensions={0} | all-to-all | bytes 1048576 | tf_op jit(solution)/shard_map/all_to_all | solution.py:84
  158.5 2.1 %collective-permute-start.6 = (bf16[80,256]{1,0:T(8,128)(2,1)S(1)}, bf16[80,256]{1,0:T(8,128)(2,1)S(1)}, u32[]{:S(2)}, u32[]{:S(2)}) collective-permute-start(bf16[80,256]{1,0:T(8,128)(2,1)S(1)} %get-tuple-element.48), channel_id=1, source_target_pairs={{0,256},{32,288},{64,320},{96,352},{128,384},{160,416},{192,448},{... | collective-permute-start | bytes 122888 | tf_op jit(solution)/shard_map/ppermute | solution.py:54
  160.6 2.7 %collective-permute-done.6.peer_ref = bf16[80,256]{1,0:T(8,128)(2,1)S(1)} collective-permute-done((bf16[80,256]{1,0:T(8,128)(2,1)S(1)}, bf16[80,256]{1,0:T(8,128)(2,1)S(1)}, u32[]{:S(2)}, u32[]{:S(2)}) %collective-permute-start.6) | collective-permute-done | bytes 40992 | tf_op jit(solution)/shard_map/ppermute | solution.py:54
  163.2 0.8 shard_map.128
  (40 shorter events, 1.8 us)
Async XLA Ops:
  0.0 15.1 %copy-start.14 = (f32[80]{0:T(128)S(1)}, f32[80]{0:T(128)}, u32[]{:S(2)}) copy-start(f32[80]{0:T(128)} %param.14) | copy-start | bytes 964
  0.0 36.8 %copy-start.15 = (s32[16]{0:T(128)S(1)}, s32[16]{0:T(128)}, u32[]{:S(2)}) copy-start(s32[16]{0:T(128)} %param.13) | copy-start | bytes 196
  0.0 38.2 %copy-start.12 = (f32[80]{0:T(128)S(1)}, f32[80]{0:T(128)}, u32[]{:S(2)}) copy-start(f32[80]{0:T(128)} %param.17) | copy-start | bytes 964
  0.0 38.2 %copy-start.13 = (f32[80]{0:T(128)S(1)}, f32[80]{0:T(128)}, u32[]{:S(2)}) copy-start(f32[80]{0:T(128)} %param.19) | copy-start | bytes 964
  3.2 35.0 %copy-start.3 = (bf16[16,32,80]{2,1,0:T(8,128)(2,1)S(1)}, bf16[16,32,80]{2,1,0:T(8,128)(2,1)}, u32[]{:S(2)}) copy-start(bf16[16,32,80]{2,1,0:T(8,128)(2,1)} %param.12) | copy-start | bytes 245764
  3.2 35.0 %copy-start.8 = (bf16[320,80]{0,1:T(8,128)(2,1)S(1)}, bf16[320,80]{0,1:T(8,128)(2,1)}, u32[]{:S(2)}) copy-start(bf16[320,80]{0,1:T(8,128)(2,1)} %param.16) | copy-start | bytes 153604
  3.2 41.9 %copy-start = (bf16[80,3,3,1280]{3,0,2,1:T(8,128)(2,1)S(1)}, bf16[80,3,3,1280]{3,0,2,1:T(8,128)(2,1)}, u32[]{:S(2)}) copy-start(bf16[80,3,3,1280]{3,0,2,1:T(8,128)(2,1)} %param.15) | copy-start | bytes 5529604
  3.2 22.2 %collective-permute-start.3 = (bf16[720,640]{1,0:T(8,128)(2,1)}, bf16[720,640]{1,0:T(8,128)(2,1)}, u32[]{:S(2)}, u32[]{:S(2)}) collective-permute-start(bf16[720,640]{1,0:T(8,128)(2,1)} %get-tuple-element.34), channel_id=1, source_target_pairs={{258,0},{259,1},{256,2},{257,3},{262,4},{263,5},{260,6},{261,7},{2... | collective-permute-start | bytes 2764808 | tf_op jit(solution)/shard_map/ppermute | solution.py:68
  8.6 6.5 %collective-permute-start = (f32[80,128]{1,0:T(8,128)}, f32[80,128]{1,0:T(8,128)S(1)}, u32[]{:S(2)}, u32[]{:S(2)}) collective-permute-start(f32[80,128]{1,0:T(8,128)} %get-tuple-element.28.own_ref), channel_id=1, source_target_pairs={{0,1},{1,0},{2,3},{3,2},{4,5},{5,4},{6,7},{7,6},{8,9},{9,8},{10,11... | collective-permute-start | bytes 122888 | tf_op jit(solution)/shard_map/ppermute | solution.py:49
  15.1 0.9 copy-start.10
  16.0 0.8 copy-start.11
  17.9 27.2 %all-to-all-start = ((bf16[16,80,256]{2,1,0:T(8,128)(2,1)}), bf16[16,80,256]{2,1,0:T(8,128)(2,1)S(1)}, u32[]{:S(2)}, u32[]{:S(2)}) async-start(bf16[16,80,256]{2,1,0:T(8,128)(2,1)} %shard_map.119), calls=%async_computation | async-start | bytes 1310720 | tf_op jit(solution)/shard_map/all_to_all | solution.py:399
  25.4 19.7 %collective-permute-start.4 = (bf16[720,640]{1,0:T(8,128)(2,1)}, bf16[720,640]{1,0:T(8,128)(2,1)}, u32[]{:S(2)}, u32[]{:S(2)}) collective-permute-start(bf16[720,640]{1,0:T(8,128)(2,1)} %collective-permute-done.3.refs_0_), channel_id=1, source_target_pairs={{0,1},{1,0},{2,3},{3,2},{4,5},{5,4},{6,7},{7,6},{8,9},{9,8},{10,11... | collective-permute-start | bytes 2764808 | tf_op jit(solution)/shard_map/ppermute | solution.py:49
  32.2 45.2 %collective-permute-start.2 = (bf16[720,1280]{1,0:T(8,128)(2,1)}, bf16[720,1280]{1,0:T(8,128)(2,1)}, u32[]{:S(2)}, u32[]{:S(2)}) collective-permute-start(bf16[720,1280]{1,0:T(8,128)(2,1)} %bitcast.24), channel_id=1, source_target_pairs={{258,0},{259,1},{256,2},{257,3},{262,4},{263,5},{260,6},{261,7},{2... | collective-permute-start | bytes 5529608 | tf_op jit(solution)/shard_map/ppermute | solution.py:68
  38.5 6.6 %collective-permute-start.5 = (f32[80,384]{1,0:T(8,128)S(1)}, f32[80,384]{1,0:T(8,128)S(1)}, u32[]{:S(2)}, u32[]{:S(2)}) collective-permute-start(f32[80,384]{1,0:T(8,128)S(1)} %shard_map.120), channel_id=1, source_target_pairs={{0,256},{32,288},{64,320},{96,352},{128,384},{160,416},{192,448},{... | collective-permute-start | bytes 368648 | tf_op jit(solution)/shard_map/ppermute | solution.py:54
  45.0 11.7 %copy-start.1 = (f32[80,384]{1,0:T(8,128)}, f32[80,384]{1,0:T(8,128)S(1)}, u32[]{:S(2)}) copy-start(f32[80,384]{1,0:T(8,128)S(1)} %collective-permute-done.5.refs_3_.mail_ref.refs_2_) | copy-start | bytes 368644
  48.3 17.2 %copy-start.4 = (bf16[64,1280]{1,0:T(8,128)(2,1)S(1)}, bf16[64,1280]{1,0:T(8,128)(2,1)}, u32[]{:S(2)}) copy-start(bf16[64,1280]{1,0:T(8,128)(2,1)} %value_ref.1) | copy-start | bytes 491524
  48.3 17.2 %copy-start.5 = (bf16[64,1280]{1,0:T(8,128)(2,1)S(1)}, bf16[64,1280]{1,0:T(8,128)(2,1)}, u32[]{:S(2)}) copy-start(bf16[64,1280]{1,0:T(8,128)(2,1)} %key_ref.1) | copy-start | bytes 491524
  48.3 17.2 %copy-start.6 = (bf16[64,1280]{1,0:T(8,128)(2,1)S(1)}, bf16[64,1280]{1,0:T(8,128)(2,1)}, u32[]{:S(2)}) copy-start(bf16[64,1280]{1,0:T(8,128)(2,1)} %query_ref.1) | copy-start | bytes 491524
  48.3 17.2 %copy-start.7 = (bf16[80,1024]{1,0:T(8,128)(2,1)S(1)}, bf16[80,1024]{1,0:T(8,128)(2,1)}, u32[]{:S(2)}) copy-start(bf16[80,1024]{1,0:T(8,128)(2,1)} %weight_ref.1) | copy-start | bytes 491524
  58.7 27.7 %all-to-all-start.2 = ((bf16[8,2,80,256]{3,2,1,0:T(8,128)(2,1)}), bf16[8,2,80,256]{3,2,1,0:T(8,128)(2,1)}, u32[]{:S(2)}, u32[]{:S(2)}) async-start(bf16[8,2,80,256]{3,2,1,0:T(8,128)(2,1)} %shard_map.122), calls=%async_computation.2 | async-start | bytes 1310720 | tf_op jit(solution)/shard_map/all_to_all | solution.py:84
  66.4 32.9 %copy-start.2 = (f32[80,384]{1,0:T(8,128)S(1)}, f32[80,384]{1,0:T(8,128)}, u32[]{:S(2)}) copy-start(f32[80,384]{1,0:T(8,128)} %copy-done.1) | copy-start | bytes 368644
  66.4 34.9 %collective-permute-start.1 = (bf16[272,1280]{1,0:T(8,128)(2,1)}, bf16[272,1280]{1,0:T(8,128)(2,1)S(1)}, u32[]{:S(2)}, u32[]{:S(2)}) collective-permute-start(bf16[272,1280]{1,0:T(8,128)(2,1)} %fusion.1), channel_id=1, source_target_pairs={{258,0},{259,1},{256,2},{257,3},{262,4},{263,5},{260,6},{261,7},{2... | collective-permute-start | bytes 2088968 | tf_op jit(solution)/shard_map/ppermute | solution.py:68
  99.3 0.9 copy-start.9
  158.5 4.7 %collective-permute-start.6 = (bf16[80,256]{1,0:T(8,128)(2,1)S(1)}, bf16[80,256]{1,0:T(8,128)(2,1)S(1)}, u32[]{:S(2)}, u32[]{:S(2)}) collective-permute-start(bf16[80,256]{1,0:T(8,128)(2,1)S(1)} %get-tuple-element.48), channel_id=1, source_target_pairs={{0,256},{32,288},{64,320},{96,352},{128,384},{160,416},{192,448},{... | collective-permute-start | bytes 122888 | tf_op jit(solution)/shard_map/ppermute | solution.py:54

commit v7 on v6

--- a/solution.py
+++ b/solution.py
@@ -25,14 +25,14 @@
 FAR = pl.BlockSpec(memory_space=pltpu.HBM)
 
 
-def call(kernel, outs, specs, scratch=(), limit=20 * 2**20):
+def call(kernel, outs, specs, scratch=()):
     return pl.pallas_call(
         kernel,
         out_shape=[jax.ShapeDtypeStruct(s, d) for s, d in outs],
         in_specs=specs,
         out_specs=[VM] * len(outs),
         scratch_shapes=list(scratch),
-        compiler_params=pltpu.CompilerParams(vmem_limit_bytes=limit),
+        compiler_params=pltpu.CompilerParams(vmem_limit_bytes=20 * 2**20),
     )
 
 
@@ -54,7 +54,7 @@
     return lax.ppermute(value, "ch", [(k, (k + chs // 2) % chs) for k in range(chs)])
 
 
-def from_beside(value):
+def from_beside(value, each_core=False):
     rows, chs = lax.axis_size("row"), lax.axis_size("ch")
     wide = 2 if rows % 4 == 0 else 1
     pairs = []
@@ -62,7 +62,8 @@
         for r in range(rows):
             core, high, rest = r % 2, r // 2 % wide, r // (2 * wide)
             side = k // (chs // 2)
-            x = (2 * high + side + (1 if side else -1)) % (2 * wide)
+            ahead = core == 0 if each_core else side == 1
+            x = (2 * high + side + (1 if ahead else -1)) % (2 * wide)
             source = device(x % 2 * (chs // 2) + k % (chs // 2), (rest * wide + x // 2) * 2 + core)
             pairs.append((source, device(k, r)))
     return lax.ppermute(value, ("ch", "row"), pairs)
@@ -390,10 +391,9 @@
         [((count, tokens), F32), ((count, 128), F32), ((9 * count, C // 2), BF16)],
         [VM, FAR],
         [pltpu.SemaphoreType.DMA],
-        limit=65_500_000,
     )(flat, own_a)
     peer = swapped(sums)
-    got_a = from_beside(half_a)
+    got_a = from_beside(half_a, each_core=True)
     (spread_a,) = call(first_kernel, [((chs, count, share), BF16)], [VM] * 4)(turned, sums, peer, gain_a)
 
     full = lax.all_to_all(spread_a, "ch", 0, 0, tiled=True)
@@ -407,18 +407,14 @@
     )
     mail = crossed(mail)
     got_b = from_beside(after(own_b, spread_a))
-    *late, late_out = [after(weight, spread_a) for weight in (w_query, w_key, w_value, w_out)]
-    late.append(jnp.pad(late_out, ((0, 0), (0, C - w_out.shape[1]))))
-    got_c = from_beside(jnp.concatenate(late, axis=0))
     other_a = swapped(after(got_a, spread_a))
 
-    def conv(limit, full, own, gots, *bases):
+    def conv(full, own, gots, *bases):
         return call(
             functools.partial(conv_kernel, gots=len(gots)),
             [field, note],
             [VM] * (3 + len(gots) + len(bases)),
             [whole],
-            limit=limit,
         )(own, *gots, full, mail, *bases)
 
     def finish(part, notes, gain, act, lane_of, outs):
@@ -426,10 +422,14 @@
             functools.partial(finish_kernel, act=act, lane_of=lane_of), outs, [VM] * 4
         )(part, notes, gain, mail)
 
-    part_a, note_a = conv(20 * 2**20, full, own_a, [got_a, other_a], time_weight.T, sinus)
+    part_a, note_a = conv(full, own_a, [got_a, other_a], time_weight.T, sinus)
     notes_a = image_collect(note_a)
     (spread_b,) = finish(part_a, notes_a, gain_b, True, 1, [active])
-    part_b, note_b = conv(65_000_000, column_collect(spread_b), own_b, [got_b], flat)
+    full_b = column_collect(spread_b)
+    *late, late_out = [after(weight, spread_b) for weight in (w_query, w_key, w_value, w_out)]
+    late.append(jnp.pad(late_out, ((0, 0), (0, C - w_out.shape[1]))))
+    got_c = from_beside(jnp.concatenate(late, axis=0))
+    part_b, note_b = conv(full_b, own_b, [got_b], flat)
     notes_b = image_collect(note_b)
     spread_c, hidden_b = finish(part_b, notes_b, gain_c, False, 2, [active, field])
     features = column_collect(after(spread_c, got_c))

time: 165 us -> 155 us (0.939)
  Pallas kernels: 18.6 us -> 15.2 us
  waiting for transfers between devices: 29.4 us -> 26.2 us
  starting transfers between devices: 39.3 us -> 36.5 us
    all_to_all x1, waiting for transfers between devices: 9.06 us -> 3.94 us  [column_collect(): lax.all_to_all(spread, 'ch', 0, 0, tiled=True, axis_index_groups=groups)]
    ppermute x3, starting transfers between devices: 12 us -> 8.71 us  [from_beside(): return lax.ppermute(value, ('ch', 'row'), pairs)]
    ppermute x2, starting transfers between devices: 12.2 us -> 15.4 us  [swapped(): return lax.ppermute(value, ('ch', 'row'), core_pairs())]
    all_to_all x1, starting transfers between devices: 6.82 us -> 4 us  [column_collect(): lax.all_to_all(spread, 'ch', 0, 0, tiled=True, axis_index_groups=groups)]
    pallas_call x1, Pallas kernels: 3.15 us -> 1.2 us  [body(): call(enter_kernel, [((count, tokens), F32), ((count, 128), F32), ((9 * co...]
    unnamed x32 -> x28, local copies, waits for them, and re-layouts: 2.68 us -> 3.99 us
  transfers between devices with their start and end apart: 9 -> 9, of which waited for: 6 -> 5; matrix products, arithmetic and copies ran while one was open for 1% -> 1% of each run, Pallas kernels for 7% -> 7%
where the time goes in v7:
time: 155 us; the launch traced here: 154 us
  blocking collectives  70 us (45%)
  starting transfers between devices  36.5 us (24%)
  waiting for transfers between devices  26.2 us (17%)
  Pallas kernels  15.2 us (10%)
  local copies, waits for them, and re-layouts  4 us (3%)
  other arithmetic  1.66 us (1%)
    all_to_all x2, blocking collectives, column_collect(): lax.all_to_all(spread, 'ch', 0, 0, tiled=True, axis_index_groups=groups)  43.5 us
    all_to_all x3, blocking collectives, image_collect(): lax.all_to_all(spread, ('ch', 'row'), 0, 0, tiled=True, axis_index_groups...  26.5 us
    ppermute x2, starting transfers between devices, swapped(): return lax.ppermute(value, ('ch', 'row'), core_pairs())  15.4 us
    ppermute x3, waiting for transfers between devices, from_beside(): return lax.ppermute(value, ('ch', 'row'), pairs)  13.2 us
    ppermute x3, starting transfers between devices, from_beside(): return lax.ppermute(value, ('ch', 'row'), pairs)  8.71 us
    ppermute x2, waiting for transfers between devices, crossed(): lax.ppermute(value, 'ch', [(k, (k + chs // 2) % chs) for k in range(chs)])  8.21 us
    pallas_call x2, Pallas kernels, conv(): call(functools.partial(conv_kernel, gots=len(gots)), [field, note], [VM]...  6.28 us
    all_to_all x1, starting transfers between devices, body(): full = lax.all_to_all(spread_a, 'ch', 0, 0, tiled=True)  4.33 us
  transfers between devices with their start and end apart: 9, of which 5 were waited for; matrix products, arithmetic and copies ran while one was open for 1% of the time, Pallas kernels for 7%

profile of v7, /device:TPU:1, one launch (start us, length us, event | category | flops | bytes accessed | tf_op | source)
XLA Modules:
  0.0 154.5 jit_solution(5187584509483634559)
XLA Ops:
  0.0 1.5 copy-done
  1.5 0.9 copy-done.3
  2.4 1.2 shard_map.118
  3.7 4.1 %collective-permute-start = (bf16[720,640]{1,0:T(8,128)(2,1)}, bf16[720,640]{1,0:T(8,128)(2,1)}, u32[]{:S(2)}, u32[]{:S(2)}) collective-permute-start(bf16[720,640]{1,0:T(8,128)(2,1)} %get-tuple-element.27), channel_id=1, source_target_pairs={{256,0},{259,1},{258,2},{257,3},{260,4},{263,5},{262,6},{261,7},{2... | collective-permute-start | bytes 2764808 | tf_op jit(solution)/shard_map/ppermute | solution.py:69
  7.8 6.7 %collective-permute-start.1 = (f32[80,128]{1,0:T(8,128)S(1)}, f32[80,128]{1,0:T(8,128)S(1)}, u32[]{:S(2)}, u32[]{:S(2)}) collective-permute-start(f32[80,128]{1,0:T(8,128)S(1)} %get-tuple-element.29.own_ref), channel_id=1, source_target_pairs={{0,1},{1,0},{2,3},{3,2},{4,5},{5,4},{6,7},{7,6},{8,9},{9,8},{10,11... | collective-permute-start | bytes 122888 | tf_op jit(solution)/shard_map/ppermute | solution.py:49
  14.5 0.8 collective-permute-done.1.peer_ref
  15.4 1.1 shard_map.119
  16.5 4.3 %all-to-all-start = ((bf16[16,80,256]{2,1,0:T(8,128)(2,1)}), bf16[16,80,256]{2,1,0:T(8,128)(2,1)S(1)}, u32[]{:S(2)}, u32[]{:S(2)}) async-start(bf16[16,80,256]{2,1,0:T(8,128)(2,1)} %shard_map.119), calls=%async_computation | async-start | bytes 1310720 | tf_op jit(solution)/shard_map/all_to_all | solution.py:399
  20.8 8.7 %collective-permute-start.2 = (bf16[720,640]{1,0:T(8,128)(2,1)}, bf16[720,640]{1,0:T(8,128)(2,1)}, u32[]{:S(2)}, u32[]{:S(2)}) collective-permute-start(bf16[720,640]{1,0:T(8,128)(2,1)} %collective-permute-done.refs_0_), channel_id=1, source_target_pairs={{0,1},{1,0},{2,3},{3,2},{4,5},{5,4},{6,7},{7,6},{8,9},{9,8},{10,11... | collective-permute-start | bytes 2764808 | tf_op jit(solution)/shard_map/ppermute | solution.py:49
  29.5 1.9 %collective-permute-start.5 = (bf16[720,1280]{1,0:T(8,128)(2,1)}, bf16[720,1280]{1,0:T(8,128)(2,1)}, u32[]{:S(2)}, u32[]{:S(2)}) collective-permute-start(bf16[720,1280]{1,0:T(8,128)(2,1)} %bitcast.14), channel_id=1, source_target_pairs={{258,0},{259,1},{256,2},{257,3},{262,4},{263,5},{260,6},{261,7},{2... | collective-permute-start | bytes 5529608 | tf_op jit(solution)/shard_map/ppermute | solution.py:69
  31.5 0.6 fusion.2
  33.2 1.9 %collective-permute-start.3 = (f32[80,384]{1,0:T(8,128)S(1)}, f32[80,384]{1,0:T(8,128)S(1)}, u32[]{:S(2)}, u32[]{:S(2)}) collective-permute-start(f32[80,384]{1,0:T(8,128)S(1)} %shard_map.120), channel_id=1, source_target_pairs={{0,256},{32,288},{64,320},{96,352},{128,384},{160,416},{192,448},{... | collective-permute-start | bytes 368648 | tf_op jit(solution)/shard_map/ppermute | solution.py:54
  35.1 5.5 %collective-permute-done.3.refs_3_.mail_ref.refs_2_ = f32[80,384]{1,0:T(8,128)S(1)} collective-permute-done((f32[80,384]{1,0:T(8,128)S(1)}, f32[80,384]{1,0:T(8,128)S(1)}, u32[]{:S(2)}, u32[]{:S(2)}) %collective-permute-start.3) | collective-permute-done | bytes 122912 | tf_op jit(solution)/shard_map/ppermute | solution.py:54
  40.7 3.2 %shard_map.121 = (f32[2,80,256]{2,1,0:T(8,128)S(1)}, bf16[4,176,128]{2,1,0:T(8,128)(2,1)S(1)}) custom-call(bf16[720,1280]{1,0:T(8,128)(2,1)S(1)} %bitcast.13, bf16[720,640]{1,0:T(8,128)(2,1)} %collective-permute-done.refs_0_, bf16[720,640]{1,0:T(8,128)(2,1)} %collective-permute-done.2.refs_1_, bf16[16,80,256]{2,1,0:T(8,128)(2,1)S(1)} %all-to-all-done.refs_2_, ...), custom_call_target="tpu_custom_call" | custom-call | tf_op jit(solution)/shard_map/pallas_call | solution.py:413
  43.9 8.0 %all_to_all.35.notes_ref = bf16[4,176,128]{2,1,0:T(8,128)(2,1)S(1)} all-to-all(bf16[4,176,128]{2,1,0:T(8,128)(2,1)S(1)} %get-tuple-element.34), channel_id=1, replica_groups={{0,256,257,1},{32,288,289,33},{64,320,321,65},{96,352,353,97},{128,384,..., dimensions={0} | all-to-all | bytes 360448 | tf_op jit(solution)/shard_map/all_to_all | solution.py:95
  51.9 1.9 %shard_map.122 = bf16[8,2,80,256]{3,2,1,0:T(8,128)(2,1)} custom-call(f32[2,80,256]{2,1,0:T(8,128)S(1)} %get-tuple-element.33.part_ref, bf16[4,176,128]{2,1,0:T(8,128)(2,1)S(1)} %all_to_all.35.notes_ref, f32[1,80]{1,0:T(1,128)S(1)} %bitcast.22, f32[80,384]{1,0:T(8,128)S(1)} %collective-permute-done.3.refs_3_.mail_ref.refs_2_), custom_call_target="tpu_custom_call" | custom-call | tf_op jit(solution)/shard_map/pallas_call | solution.py:421
  53.9 4.0 %all-to-all-start.2 = ((bf16[8,2,80,256]{3,2,1,0:T(8,128)(2,1)}), bf16[8,2,80,256]{3,2,1,0:T(8,128)(2,1)S(1)}, u32[]{:S(2)}, u32[]{:S(2)}) async-start(bf16[8,2,80,256]{3,2,1,0:T(8,128)(2,1)} %shard_map.122), calls=%async_computation.2 | async-start | bytes 1310720 | tf_op jit(solution)/shard_map/all_to_all | solution.py:85
  57.9 0.9 fusion.1
  58.8 2.7 %collective-permute-start.4 = (bf16[272,1280]{1,0:T(8,128)(2,1)}, bf16[272,1280]{1,0:T(8,128)(2,1)S(1)}, u32[]{:S(2)}, u32[]{:S(2)}) collective-permute-start(bf16[272,1280]{1,0:T(8,128)(2,1)} %fusion.1), channel_id=1, source_target_pairs={{258,0},{259,1},{256,2},{257,3},{262,4},{263,5},{260,6},{261,7},{2... | collective-permute-start | bytes 2088968 | tf_op jit(solution)/shard_map/ppermute | solution.py:69
  61.5 13.2 %collective-permute-done.5.refs_0_ = bf16[720,1280]{1,0:T(8,128)(2,1)} collective-permute-done((bf16[720,1280]{1,0:T(8,128)(2,1)}, bf16[720,1280]{1,0:T(8,128)(2,1)}, u32[]{:S(2)}, u32[]{:S(2)}) %collective-permute-start.5) | collective-permute-done | bytes 1843232 | tf_op jit(solution)/shard_map/ppermute | solution.py:69
  74.7 3.9 %all-to-all-done.2.refs_1_ = bf16[8,2,80,256]{3,2,1,0:T(8,128)(2,1)S(1)} async-done(((bf16[8,2,80,256]{3,2,1,0:T(8,128)(2,1)}), bf16[8,2,80,256]{3,2,1,0:T(8,128)(2,1)S(1)}, u32[]{:S(2)}, u32[]{:S(2)}) %all-to-all-start.2) | async-done | bytes 655392 | tf_op jit(solution)/shard_map/all_to_all | solution.py:85
  78.6 1.5 copy-done.2
  80.1 3.1 %shard_map.123 = (f32[2,80,256]{2,1,0:T(8,128)S(1)}, bf16[4,176,128]{2,1,0:T(8,128)(2,1)S(1)}) custom-call(bf16[720,1280]{1,0:T(8,128)(2,1)S(1)} %bitcast.15, bf16[720,1280]{1,0:T(8,128)(2,1)} %collective-permute-done.5.refs_0_, bf16[8,2,80,256]{3,2,1,0:T(8,128)(2,1)S(1)} %all-to-all-done.2.refs_1_, ...), custom_call_target="tpu_custom_call" | custom-call | tf_op jit(solution)/shard_map/pallas_call | solution.py:413
  83.3 7.4 %all_to_all.36.notes_ref = bf16[4,176,128]{2,1,0:T(8,128)(2,1)S(1)} all-to-all(bf16[4,176,128]{2,1,0:T(8,128)(2,1)S(1)} %get-tuple-element.41), channel_id=1, replica_groups={{0,256,257,1},{32,288,289,33},{64,320,321,65},{96,352,353,97},{128,384,..., dimensions={0} | all-to-all | bytes 360448 | tf_op jit(solution)/shard_map/all_to_all | solution.py:95
  90.7 1.1 shard_map.124
  91.9 23.1 %all_to_all.37.full_ref = bf16[8,2,80,256]{3,2,1,0:T(8,128)(2,1)S(1)} all-to-all(bf16[8,2,80,256]{3,2,1,0:T(8,128)(2,1)S(1)} %get-tuple-element.43), channel_id=1, replica_groups={{0,32,64,96,128,160,192,224},{256,288,320,352,384,416,448,480},{1,33,65..., dimensions={0} | all-to-all | bytes 1310720 | tf_op jit(solution)/shard_map/all_to_all | solution.py:85
  115.4 11.0 %all_to_all.38.pairs_ref = bf16[4,2,128,256]{3,2,1,0:T(8,128)(2,1)S(1)} all-to-all(bf16[4,2,128,256]{3,2,1,0:T(8,128)(2,1)S(1)} %get-tuple-element.45), channel_id=1, replica_groups={{0,256,257,1},{32,288,289,33},{64,320,321,65},{96,352,353,97},{128,384,..., dimensions={0} | all-to-all | bytes 1048576 | tf_op jit(solution)/shard_map/all_to_all | solution.py:95
  126.5 1.8 %shard_map.126 = bf16[8,2,64,256]{3,2,1,0:T(8,128)(2,1)S(1)} custom-call(bf16[2,64,256]{2,1,0:T(8,128)(2,1)S(1)} %get-tuple-element.44.q_ref, bf16[4,2,128,256]{3,2,1,0:T(8,128)(2,1)S(1)} %all_to_all.38.pairs_ref), custom_call_target="tpu_custom_call" | custom-call | tf_op jit(solution)/shard_map/pallas_call | solution.py:444
  128.3 20.4 %all_to_all.39.full_ref = bf16[8,2,64,256]{3,2,1,0:T(8,128)(2,1)S(1)} all-to-all(bf16[8,2,64,256]{3,2,1,0:T(8,128)(2,1)S(1)} %shard_map.126), channel_id=1, replica_groups={{0,32,64,96,128,160,192,224},{256,288,320,352,384,416,448,480},{1,33,65..., dimensions={0} | all-to-all | bytes 1048576 | tf_op jit(solution)/shard_map/all_to_all | solution.py:85
  148.9 2.1 %collective-permute-start.6 = (bf16[80,256]{1,0:T(8,128)(2,1)S(1)}, bf16[80,256]{1,0:T(8,128)(2,1)S(1)}, u32[]{:S(2)}, u32[]{:S(2)}) collective-permute-start(bf16[80,256]{1,0:T(8,128)(2,1)S(1)} %get-tuple-element.48), channel_id=1, source_target_pairs={{0,256},{32,288},{64,320},{96,352},{128,384},{160,416},{192,448},{... | collective-permute-start | bytes 122888 | tf_op jit(solution)/shard_map/ppermute | solution.py:54
  151.0 2.7 %collective-permute-done.6.peer_ref = bf16[80,256]{1,0:T(8,128)(2,1)S(1)} collective-permute-done((bf16[80,256]{1,0:T(8,128)(2,1)S(1)}, bf16[80,256]{1,0:T(8,128)(2,1)S(1)}, u32[]{:S(2)}, u32[]{:S(2)}) %collective-permute-start.6) | collective-permute-done | bytes 40992 | tf_op jit(solution)/shard_map/ppermute | solution.py:54
  153.7 0.8 shard_map.128
  (36 shorter events, 1.2 us)
Async XLA Ops:
  0.0 15.4 %copy-start.12 = (f32[80]{0:T(128)S(1)}, f32[80]{0:T(128)}, u32[]{:S(2)}) copy-start(f32[80]{0:T(128)} %param.14) | copy-start | bytes 964
  0.0 1.5 copy-start
  1.5 0.9 copy-start.3
  3.6 27.9 %copy-start.13 = (s32[16]{0:T(128)S(1)}, s32[16]{0:T(128)}, u32[]{:S(2)}) copy-start(s32[16]{0:T(128)} %param.13) | copy-start | bytes 196
  3.6 29.3 %copy-start.4 = (bf16[16,32,80]{2,1,0:T(8,128)(2,1)S(1)}, bf16[16,32,80]{2,1,0:T(8,128)(2,1)}, u32[]{:S(2)}) copy-start(bf16[16,32,80]{2,1,0:T(8,128)(2,1)} %param.12) | copy-start | bytes 245764
  3.7 29.3 %copy-start.9 = (bf16[320,80]{0,1:T(8,128)(2,1)S(1)}, bf16[320,80]{0,1:T(8,128)(2,1)}, u32[]{:S(2)}) copy-start(bf16[320,80]{0,1:T(8,128)(2,1)} %param.16) | copy-start | bytes 153604
  3.7 29.3 %copy-start.10 = (f32[80]{0:T(128)S(1)}, f32[80]{0:T(128)}, u32[]{:S(2)}) copy-start(f32[80]{0:T(128)} %param.17) | copy-start | bytes 964
  3.7 29.3 %copy-start.11 = (f32[80]{0:T(128)S(1)}, f32[80]{0:T(128)}, u32[]{:S(2)}) copy-start(f32[80]{0:T(128)} %param.19) | copy-start | bytes 964
  3.7 37.0 %copy-start.1 = (bf16[80,3,3,1280]{3,0,2,1:T(8,128)(2,1)S(1)}, bf16[80,3,3,1280]{3,0,2,1:T(8,128)(2,1)}, u32[]{:S(2)}) copy-start(bf16[80,3,3,1280]{3,0,2,1:T(8,128)(2,1)} %param.15) | copy-start | bytes 5529604
  3.7 17.1 %collective-permute-start = (bf16[720,640]{1,0:T(8,128)(2,1)}, bf16[720,640]{1,0:T(8,128)(2,1)}, u32[]{:S(2)}, u32[]{:S(2)}) collective-permute-start(bf16[720,640]{1,0:T(8,128)(2,1)} %get-tuple-element.27), channel_id=1, source_target_pairs={{256,0},{259,1},{258,2},{257,3},{260,4},{263,5},{262,6},{261,7},{2... | collective-permute-start | bytes 2764808 | tf_op jit(solution)/shard_map/ppermute | solution.py:69
  7.8 7.6 %collective-permute-start.1 = (f32[80,128]{1,0:T(8,128)S(1)}, f32[80,128]{1,0:T(8,128)S(1)}, u32[]{:S(2)}, u32[]{:S(2)}) collective-permute-start(f32[80,128]{1,0:T(8,128)S(1)} %get-tuple-element.29.own_ref), channel_id=1, source_target_pairs={{0,1},{1,0},{2,3},{3,2},{4,5},{5,4},{6,7},{7,6},{8,9},{9,8},{10,11... | collective-permute-start | bytes 122888 | tf_op jit(solution)/shard_map/ppermute | solution.py:49
  16.5 24.2 %all-to-all-start = ((bf16[16,80,256]{2,1,0:T(8,128)(2,1)}), bf16[16,80,256]{2,1,0:T(8,128)(2,1)S(1)}, u32[]{:S(2)}, u32[]{:S(2)}) async-start(bf16[16,80,256]{2,1,0:T(8,128)(2,1)} %shard_map.119), calls=%async_computation | async-start | bytes 1310720 | tf_op jit(solution)/shard_map/all_to_all | solution.py:399
  20.8 19.8 %collective-permute-start.2 = (bf16[720,640]{1,0:T(8,128)(2,1)}, bf16[720,640]{1,0:T(8,128)(2,1)}, u32[]{:S(2)}, u32[]{:S(2)}) collective-permute-start(bf16[720,640]{1,0:T(8,128)(2,1)} %collective-permute-done.refs_0_), channel_id=1, source_target_pairs={{0,1},{1,0},{2,3},{3,2},{4,5},{5,4},{6,7},{7,6},{8,9},{9,8},{10,11... | collective-permute-start | bytes 2764808 | tf_op jit(solution)/shard_map/ppermute | solution.py:49
  29.5 45.2 %collective-permute-start.5 = (bf16[720,1280]{1,0:T(8,128)(2,1)}, bf16[720,1280]{1,0:T(8,128)(2,1)}, u32[]{:S(2)}, u32[]{:S(2)}) collective-permute-start(bf16[720,1280]{1,0:T(8,128)(2,1)} %bitcast.14), channel_id=1, source_target_pairs={{258,0},{259,1},{256,2},{257,3},{262,4},{263,5},{260,6},{261,7},{2... | collective-permute-start | bytes 5529608 | tf_op jit(solution)/shard_map/ppermute | solution.py:69
  33.2 7.5 %collective-permute-start.3 = (f32[80,384]{1,0:T(8,128)S(1)}, f32[80,384]{1,0:T(8,128)S(1)}, u32[]{:S(2)}, u32[]{:S(2)}) collective-permute-start(f32[80,384]{1,0:T(8,128)S(1)} %shard_map.120), channel_id=1, source_target_pairs={{0,256},{32,288},{64,320},{96,352},{128,384},{160,416},{192,448},{... | collective-permute-start | bytes 368648 | tf_op jit(solution)/shard_map/ppermute | solution.py:54
  43.8 14.0 %copy-start.5 = (bf16[64,1280]{1,0:T(8,128)(2,1)S(1)}, bf16[64,1280]{1,0:T(8,128)(2,1)}, u32[]{:S(2)}) copy-start(bf16[64,1280]{1,0:T(8,128)(2,1)} %value_ref.1) | copy-start | bytes 491524
  43.9 14.0 %copy-start.6 = (bf16[64,1280]{1,0:T(8,128)(2,1)S(1)}, bf16[64,1280]{1,0:T(8,128)(2,1)}, u32[]{:S(2)}) copy-start(bf16[64,1280]{1,0:T(8,128)(2,1)} %key_ref.1) | copy-start | bytes 491524
  43.9 14.0 %copy-start.7 = (bf16[64,1280]{1,0:T(8,128)(2,1)S(1)}, bf16[64,1280]{1,0:T(8,128)(2,1)}, u32[]{:S(2)}) copy-start(bf16[64,1280]{1,0:T(8,128)(2,1)} %query_ref.1) | copy-start | bytes 491524
  43.9 14.0 %copy-start.8 = (bf16[80,1024]{1,0:T(8,128)(2,1)S(1)}, bf16[80,1024]{1,0:T(8,128)(2,1)}, u32[]{:S(2)}) copy-start(bf16[80,1024]{1,0:T(8,128)(2,1)} %weight_ref.1) | copy-start | bytes 491524
  53.9 24.8 %all-to-all-start.2 = ((bf16[8,2,80,256]{3,2,1,0:T(8,128)(2,1)}), bf16[8,2,80,256]{3,2,1,0:T(8,128)(2,1)S(1)}, u32[]{:S(2)}, u32[]{:S(2)}) async-start(bf16[8,2,80,256]{3,2,1,0:T(8,128)(2,1)} %shard_map.122), calls=%async_computation.2 | async-start | bytes 1310720 | tf_op jit(solution)/shard_map/all_to_all | solution.py:85
  58.8 33.0 %collective-permute-start.4 = (bf16[272,1280]{1,0:T(8,128)(2,1)}, bf16[272,1280]{1,0:T(8,128)(2,1)S(1)}, u32[]{:S(2)}, u32[]{:S(2)}) collective-permute-start(bf16[272,1280]{1,0:T(8,128)(2,1)} %fusion.1), channel_id=1, source_target_pairs={{258,0},{259,1},{256,2},{257,3},{262,4},{263,5},{260,6},{261,7},{2... | collective-permute-start | bytes 2088968 | tf_op jit(solution)/shard_map/ppermute | solution.py:69
  78.6 1.5 copy-start.2
  148.9 4.7 %collective-permute-start.6 = (bf16[80,256]{1,0:T(8,128)(2,1)S(1)}, bf16[80,256]{1,0:T(8,128)(2,1)S(1)}, u32[]{:S(2)}, u32[]{:S(2)}) collective-permute-start(bf16[80,256]{1,0:T(8,128)(2,1)S(1)} %get-tuple-element.48), channel_id=1, source_target_pairs={{0,256},{32,288},{64,320},{96,352},{128,384},{160,416},{192,448},{... | collective-permute-start | bytes 122888 | tf_op jit(solution)/shard_map/ppermute | solution.py:54

commit v8 on v7

--- a/solution.py
+++ b/solution.py
@@ -22,17 +22,19 @@
 BF16 = jnp.bfloat16
 
 VM = pl.BlockSpec(memory_space=pltpu.VMEM)
+ENTER_LIMIT = 56_000_000
+CONV_LIMIT = 54_300_000
 FAR = pl.BlockSpec(memory_space=pltpu.HBM)
 
 
-def call(kernel, outs, specs, scratch=()):
+def call(kernel, outs, specs, scratch=(), limit=20 * 2**20):
     return pl.pallas_call(
         kernel,
         out_shape=[jax.ShapeDtypeStruct(s, d) for s, d in outs],
         in_specs=specs,
         out_specs=[VM] * len(outs),
         scratch_shapes=list(scratch),
-        compiler_params=pltpu.CompilerParams(vmem_limit_bytes=20 * 2**20),
+        compiler_params=pltpu.CompilerParams(vmem_limit_bytes=limit),
     )
 
 
@@ -185,6 +187,11 @@
             whole_ref[at : at + count] = full_ref[peer, side]
 
 
+def arrived(ref, held_ref, sem):
+    pltpu.make_async_copy(ref, held_ref, sem).wait()
+    return held_ref[...]
+
+
 def both(own, gots, whole_ref):
     mine = jnp.dot(own, whole_ref[...], preferred_element_type=F32)
     depth = gots[0].shape[1]
@@ -197,9 +204,13 @@
     return mine, theirs + jnp.dot(gots[1], far, preferred_element_type=F32)
 
 
-def conv_kernel(own_ref, *refs, gots):
+def conv_kernel(own_ref, *refs, gots, copied):
     got_refs, refs = refs[:gots], refs[gots:]
-    full_ref, mail_ref, *base_refs, part_ref, note_ref, whole_ref = refs
+    full_ref, mail_ref, *base_refs, part_ref, note_ref, whole_ref = refs[: len(refs) - 3 * copied]
+    if copied:
+        weights = list(zip((own_ref, got_refs[0]), refs[-3:-1], (refs[-1].at[0], refs[-1].at[1])))
+        for ref, held_ref, sem in weights:
+            pltpu.make_async_copy(ref, held_ref, sem).start()
     _, count, tokens = part_ref.shape
     side, core, quarter = spot()
     token = lanes((count, tokens))
@@ -208,7 +219,10 @@
     begin = jnp.where(quarter > 0, W, 0)
     end = jnp.where(quarter < 3, tokens - W, tokens)
     gather_into(full_ref, whole_ref)
-    taps = both(own_ref[...], [ref[...] for ref in got_refs], whole_ref)
+    if copied:
+        taps = [jnp.dot(arrived(*each), whole_ref[...], preferred_element_type=F32) for each in weights]
+    else:
+        taps = both(own_ref[...], [ref[...] for ref in got_refs], whole_ref)
     if len(base_refs) == 2:
         bases = time_of(*base_refs), mail_ref[:, tokens : tokens + 1]
     else:
@@ -391,6 +405,7 @@
         [((count, tokens), F32), ((count, 128), F32), ((9 * count, C // 2), BF16)],
         [VM, FAR],
         [pltpu.SemaphoreType.DMA],
+        limit=ENTER_LIMIT,
     )(flat, own_a)
     peer = swapped(sums)
     got_a = from_beside(half_a, each_core=True)
@@ -409,12 +424,14 @@
     got_b = from_beside(after(own_b, spread_a))
     other_a = swapped(after(got_a, spread_a))
 
-    def conv(full, own, gots, *bases):
+    def conv(full, own, gots, *bases, copied=False):
+        held = [pltpu.VMEM(own.shape, BF16)] * 2 + [pltpu.SemaphoreType.DMA((2,))]
         return call(
-            functools.partial(conv_kernel, gots=len(gots)),
+            functools.partial(conv_kernel, gots=len(gots), copied=int(copied)),
             [field, note],
-            [VM] * (3 + len(gots) + len(bases)),
-            [whole],
+            [FAR if copied else VM] * (1 + len(gots)) + [VM] * (2 + len(bases)),
+            [whole] + held * copied,
+            limit=CONV_LIMIT if copied else 20 * 2**20,
         )(own, *gots, full, mail, *bases)
 
     def finish(part, notes, gain, act, lane_of, outs):
@@ -429,7 +446,7 @@
     *late, late_out = [after(weight, spread_b) for weight in (w_query, w_key, w_value, w_out)]
     late.append(jnp.pad(late_out, ((0, 0), (0, C - w_out.shape[1]))))
     got_c = from_beside(jnp.concatenate(late, axis=0))
-    part_b, note_b = conv(full_b, own_b, [got_b], flat)
+    part_b, note_b = conv(full_b, own_b, [got_b], flat, copied=True)
     notes_b = image_collect(note_b)
     spread_c, hidden_b = finish(part_b, notes_b, gain_c, False, 2, [active, field])
     features = column_collect(after(spread_c, got_c))

time: 155 us -> 154 us (level)
  local copies, waits for them, and re-layouts: 4 us -> 0.99 us
  Pallas kernels: 15.2 us -> 17.1 us
    unnamed x28 -> x24, local copies, waits for them, and re-layouts: 3.99 us -> 0.98 us
  transfers between devices with their start and end apart: 9 -> 9, of which waited for: 5 -> 5; matrix products, arithmetic and copies ran while one was open for 1% -> 1% of each run, Pallas kernels for 7% -> 8%
where the time goes in v8:
time: 154 us; the launch traced here: 153 us
  blocking collectives  70 us (45%)
  starting transfers between devices  36.5 us (24%)
  waiting for transfers between devices  27 us (18%)
  Pallas kernels  17.1 us (11%)
    all_to_all x2, blocking collectives, column_collect(): lax.all_to_all(spread, 'ch', 0, 0, tiled=True, axis_index_groups=groups)  43.5 us
    all_to_all x3, blocking collectives, image_collect(): lax.all_to_all(spread, ('ch', 'row'), 0, 0, tiled=True, axis_index_groups...  26.5 us
    ppermute x2, starting transfers between devices, swapped(): return lax.ppermute(value, ('ch', 'row'), core_pairs())  15.4 us
    ppermute x3, waiting for transfers between devices, from_beside(): return lax.ppermute(value, ('ch', 'row'), pairs)  14 us
    ppermute x3, starting transfers between devices, from_beside(): return lax.ppermute(value, ('ch', 'row'), pairs)  8.73 us
    ppermute x2, waiting for transfers between devices, crossed(): lax.ppermute(value, 'ch', [(k, (k + chs // 2) % chs) for k in range(chs)])  8.21 us
    pallas_call x2, Pallas kernels, conv(): call(functools.partial(conv_kernel, gots=len(gots), copied=int(copied)),...  7.18 us
    all_to_all x1, starting transfers between devices, body(): full = lax.all_to_all(spread_a, 'ch', 0, 0, tiled=True)  4.33 us
  transfers between devices with their start and end apart: 9, of which 5 were waited for; matrix products, arithmetic and copies ran while one was open for 1% of the time, Pallas kernels for 8%

profile of v8, /device:TPU:1, one launch (start us, length us, event | category | flops | bytes accessed | tf_op | source)
XLA Modules:
  0.0 153.4 jit_solution(4188622172921101030)
XLA Ops:
  0.0 0.9 copy-done.1
  0.9 2.2 %shard_map.118 = (f32[80,512]{1,0:T(8,128)S(1)}, f32[80,128]{1,0:T(8,128)S(1)}, bf16[720,640]{1,0:T(8,128)(2,1)}) custom-call(bf16[512,80]{1,0:T(8,128)(2,1)S(1)} %bitcast.14, bf16[720,1280]{1,0:T(8,128)(2,1)} %bitcast.12), custom_call_target="tpu_custom_call" | custom-call | tf_op jit(solution)/shard_map/pallas_call | solution.py:403
  3.2 4.1 %collective-permute-start = (bf16[720,640]{1,0:T(8,128)(2,1)}, bf16[720,640]{1,0:T(8,128)(2,1)}, u32[]{:S(2)}, u32[]{:S(2)}) collective-permute-start(bf16[720,640]{1,0:T(8,128)(2,1)} %get-tuple-element.27), channel_id=1, source_target_pairs={{256,0},{259,1},{258,2},{257,3},{260,4},{263,5},{262,6},{261,7},{2... | collective-permute-start | bytes 2764808 | tf_op jit(solution)/shard_map/ppermute | solution.py:71
  7.3 6.7 %collective-permute-start.1 = (f32[80,128]{1,0:T(8,128)S(1)}, f32[80,128]{1,0:T(8,128)S(1)}, u32[]{:S(2)}, u32[]{:S(2)}) collective-permute-start(f32[80,128]{1,0:T(8,128)S(1)} %get-tuple-element.29.own_ref), channel_id=1, source_target_pairs={{0,1},{1,0},{2,3},{3,2},{4,5},{5,4},{6,7},{7,6},{8,9},{9,8},{10,11... | collective-permute-start | bytes 122888 | tf_op jit(solution)/shard_map/ppermute | solution.py:51
  14.0 0.8 collective-permute-done.1.peer_ref
  14.9 1.1 shard_map.119
  16.0 4.3 %all-to-all-start = ((bf16[16,80,256]{2,1,0:T(8,128)(2,1)}), bf16[16,80,256]{2,1,0:T(8,128)(2,1)S(1)}, u32[]{:S(2)}, u32[]{:S(2)}) async-start(bf16[16,80,256]{2,1,0:T(8,128)(2,1)} %shard_map.119), calls=%async_computation | async-start | bytes 1310720 | tf_op jit(solution)/shard_map/all_to_all | solution.py:414
  20.4 8.7 %collective-permute-start.2 = (bf16[720,640]{1,0:T(8,128)(2,1)}, bf16[720,640]{1,0:T(8,128)(2,1)}, u32[]{:S(2)}, u32[]{:S(2)}) collective-permute-start(bf16[720,640]{1,0:T(8,128)(2,1)} %collective-permute-done.refs_0_), channel_id=1, source_target_pairs={{0,1},{1,0},{2,3},{3,2},{4,5},{5,4},{6,7},{7,6},{8,9},{9,8},{10,11... | collective-permute-start | bytes 2764808 | tf_op jit(solution)/shard_map/ppermute | solution.py:51
  29.1 1.9 %collective-permute-start.5 = (bf16[720,1280]{1,0:T(8,128)(2,1)}, bf16[720,1280]{1,0:T(8,128)(2,1)}, u32[]{:S(2)}, u32[]{:S(2)}) collective-permute-start(bf16[720,1280]{1,0:T(8,128)(2,1)} %bitcast.24), channel_id=1, source_target_pairs={{258,0},{259,1},{256,2},{257,3},{262,4},{263,5},{260,6},{261,7},{2... | collective-permute-start | bytes 5529608 | tf_op jit(solution)/shard_map/ppermute | solution.py:71
  31.0 0.6 fusion.2
  32.5 0.2 shard_map.120
  32.7 1.9 %collective-permute-start.3 = (f32[80,384]{1,0:T(8,128)S(1)}, f32[80,384]{1,0:T(8,128)S(1)}, u32[]{:S(2)}, u32[]{:S(2)}) collective-permute-start(f32[80,384]{1,0:T(8,128)S(1)} %shard_map.120), channel_id=1, source_target_pairs={{0,256},{32,288},{64,320},{96,352},{128,384},{160,416},{192,448},{... | collective-permute-start | bytes 368648 | tf_op jit(solution)/shard_map/ppermute | solution.py:56
  34.7 5.5 %collective-permute-done.3.refs_3_.mail_ref.refs_2_ = f32[80,384]{1,0:T(8,128)S(1)} collective-permute-done((f32[80,384]{1,0:T(8,128)S(1)}, f32[80,384]{1,0:T(8,128)S(1)}, u32[]{:S(2)}, u32[]{:S(2)}) %collective-permute-start.3) | collective-permute-done | bytes 122912 | tf_op jit(solution)/shard_map/ppermute | solution.py:56
  40.2 3.2 %shard_map.121 = (f32[2,80,256]{2,1,0:T(8,128)S(1)}, bf16[4,176,128]{2,1,0:T(8,128)(2,1)S(1)}) custom-call(bf16[720,1280]{1,0:T(8,128)(2,1)S(1)} %bitcast.13, bf16[720,640]{1,0:T(8,128)(2,1)} %collective-permute-done.refs_0_, bf16[720,640]{1,0:T(8,128)(2,1)} %collective-permute-done.2.refs_1_, bf16[16,80,256]{2,1,0:T(8,128)(2,1)S(1)} %all-to-all-done.refs_2_, ...), custom_call_target="tpu_custom_call" | custom-call | tf_op jit(solution)/shard_map/pallas_call | solution.py:429
  43.4 8.0 %all_to_all.35.notes_ref = bf16[4,176,128]{2,1,0:T(8,128)(2,1)S(1)} all-to-all(bf16[4,176,128]{2,1,0:T(8,128)(2,1)S(1)} %get-tuple-element.34), channel_id=1, replica_groups={{0,256,257,1},{32,288,289,33},{64,320,321,65},{96,352,353,97},{128,384,..., dimensions={0} | all-to-all | bytes 360448 | tf_op jit(solution)/shard_map/all_to_all | solution.py:97
  51.4 2.0 %shard_map.122 = bf16[8,2,80,256]{3,2,1,0:T(8,128)(2,1)} custom-call(f32[2,80,256]{2,1,0:T(8,128)S(1)} %get-tuple-element.33.part_ref, bf16[4,176,128]{2,1,0:T(8,128)(2,1)S(1)} %all_to_all.35.notes_ref, f32[1,80]{1,0:T(1,128)S(1)} %bitcast.20, f32[80,384]{1,0:T(8,128)S(1)} %collective-permute-done.3.refs_3_.mail_ref.refs_2_), custom_call_target="tpu_custom_call" | custom-call | tf_op jit(solution)/shard_map/pallas_call | solution.py:438
  53.4 4.0 %all-to-all-start.2 = ((bf16[8,2,80,256]{3,2,1,0:T(8,128)(2,1)}), bf16[8,2,80,256]{3,2,1,0:T(8,128)(2,1)S(1)}, u32[]{:S(2)}, u32[]{:S(2)}) async-start(bf16[8,2,80,256]{3,2,1,0:T(8,128)(2,1)} %shard_map.122), calls=%async_computation.2 | async-start | bytes 1310720 | tf_op jit(solution)/shard_map/all_to_all | solution.py:87
  57.5 2.7 %collective-permute-start.4 = (bf16[272,1280]{1,0:T(8,128)(2,1)S(1)}, bf16[272,1280]{1,0:T(8,128)(2,1)S(1)}, u32[]{:S(2)}, u32[]{:S(2)}) collective-permute-start(bf16[272,1280]{1,0:T(8,128)(2,1)S(1)} %fusion.1), channel_id=1, source_target_pairs={{258,0},{259,1},{256,2},{257,3},{262,4},{263,5},{260,6},{261,7},{2... | collective-permute-start | bytes 2088968 | tf_op jit(solution)/shard_map/ppermute | solution.py:71
  60.2 14.0 %collective-permute-done.5.refs_0_ = bf16[720,1280]{1,0:T(8,128)(2,1)} collective-permute-done((bf16[720,1280]{1,0:T(8,128)(2,1)}, bf16[720,1280]{1,0:T(8,128)(2,1)}, u32[]{:S(2)}, u32[]{:S(2)}) %collective-permute-start.5) | collective-permute-done | bytes 1843232 | tf_op jit(solution)/shard_map/ppermute | solution.py:71
  74.2 4.0 %all-to-all-done.2.refs_1_ = bf16[8,2,80,256]{3,2,1,0:T(8,128)(2,1)S(1)} async-done(((bf16[8,2,80,256]{3,2,1,0:T(8,128)(2,1)}), bf16[8,2,80,256]{3,2,1,0:T(8,128)(2,1)S(1)}, u32[]{:S(2)}, u32[]{:S(2)}) %all-to-all-start.2) | async-done | bytes 655392 | tf_op jit(solution)/shard_map/all_to_all | solution.py:87
  78.2 4.0 %shard_map.123 = (f32[2,80,256]{2,1,0:T(8,128)S(1)}, bf16[4,176,128]{2,1,0:T(8,128)(2,1)S(1)}) custom-call(bf16[720,1280]{1,0:T(8,128)(2,1)} %bitcast.25, bf16[720,1280]{1,0:T(8,128)(2,1)} %collective-permute-done.5.refs_0_, bf16[8,2,80,256]{3,2,1,0:T(8,128)(2,1)S(1)} %all-to-all-done.2.refs_1_, ...), custom_call_target="tpu_custom_call" | custom-call | tf_op jit(solution)/shard_map/pallas_call | solution.py:429
  82.2 7.4 %all_to_all.36.notes_ref = bf16[4,176,128]{2,1,0:T(8,128)(2,1)S(1)} all-to-all(bf16[4,176,128]{2,1,0:T(8,128)(2,1)S(1)} %get-tuple-element.41), channel_id=1, replica_groups={{0,256,257,1},{32,288,289,33},{64,320,321,65},{96,352,353,97},{128,384,..., dimensions={0} | all-to-all | bytes 360448 | tf_op jit(solution)/shard_map/all_to_all | solution.py:97
  89.6 1.1 shard_map.124
  90.8 23.1 %all_to_all.37.full_ref = bf16[8,2,80,256]{3,2,1,0:T(8,128)(2,1)S(1)} all-to-all(bf16[8,2,80,256]{3,2,1,0:T(8,128)(2,1)S(1)} %get-tuple-element.43), channel_id=1, replica_groups={{0,32,64,96,128,160,192,224},{256,288,320,352,384,416,448,480},{1,33,65..., dimensions={0} | all-to-all | bytes 1310720 | tf_op jit(solution)/shard_map/all_to_all | solution.py:87
  113.9 0.4 shard_map.125
  114.3 11.0 %all_to_all.38.pairs_ref = bf16[4,2,128,256]{3,2,1,0:T(8,128)(2,1)S(1)} all-to-all(bf16[4,2,128,256]{3,2,1,0:T(8,128)(2,1)S(1)} %get-tuple-element.45), channel_id=1, replica_groups={{0,256,257,1},{32,288,289,33},{64,320,321,65},{96,352,353,97},{128,384,..., dimensions={0} | all-to-all | bytes 1048576 | tf_op jit(solution)/shard_map/all_to_all | solution.py:97
  125.4 1.8 %shard_map.126 = bf16[8,2,64,256]{3,2,1,0:T(8,128)(2,1)S(1)} custom-call(bf16[2,64,256]{2,1,0:T(8,128)(2,1)S(1)} %get-tuple-element.44.q_ref, bf16[4,2,128,256]{3,2,1,0:T(8,128)(2,1)S(1)} %all_to_all.38.pairs_ref), custom_call_target="tpu_custom_call" | custom-call | tf_op jit(solution)/shard_map/pallas_call | solution.py:461
  127.2 20.4 %all_to_all.39.full_ref = bf16[8,2,64,256]{3,2,1,0:T(8,128)(2,1)S(1)} all-to-all(bf16[8,2,64,256]{3,2,1,0:T(8,128)(2,1)S(1)} %shard_map.126), channel_id=1, replica_groups={{0,32,64,96,128,160,192,224},{256,288,320,352,384,416,448,480},{1,33,65..., dimensions={0} | all-to-all | bytes 1048576 | tf_op jit(solution)/shard_map/all_to_all | solution.py:87
  147.6 0.3 shard_map.127
  147.9 2.1 %collective-permute-start.6 = (bf16[80,256]{1,0:T(8,128)(2,1)S(1)}, bf16[80,256]{1,0:T(8,128)(2,1)S(1)}, u32[]{:S(2)}, u32[]{:S(2)}) collective-permute-start(bf16[80,256]{1,0:T(8,128)(2,1)S(1)} %get-tuple-element.48), channel_id=1, source_target_pairs={{0,256},{32,288},{64,320},{96,352},{128,384},{160,416},{192,448},{... | collective-permute-start | bytes 122888 | tf_op jit(solution)/shard_map/ppermute | solution.py:56
  149.9 2.7 %collective-permute-done.6.peer_ref = bf16[80,256]{1,0:T(8,128)(2,1)S(1)} collective-permute-done((bf16[80,256]{1,0:T(8,128)(2,1)S(1)}, bf16[80,256]{1,0:T(8,128)(2,1)S(1)}, u32[]{:S(2)}, u32[]{:S(2)}) %collective-permute-start.6) | collective-permute-done | bytes 40992 | tf_op jit(solution)/shard_map/ppermute | solution.py:56
  152.6 0.8 shard_map.128
  (32 shorter events, 0.3 us)
Async XLA Ops:
  0.0 14.9 %copy-start.10 = (f32[80]{0:T(128)S(1)}, f32[80]{0:T(128)}, u32[]{:S(2)}) copy-start(f32[80]{0:T(128)} %param.14) | copy-start | bytes 964
  0.0 0.9 copy-start.1
  3.2 27.9 %copy-start.11 = (s32[16]{0:T(128)S(1)}, s32[16]{0:T(128)}, u32[]{:S(2)}) copy-start(s32[16]{0:T(128)} %param.13) | copy-start | bytes 196
  3.2 29.3 %copy-start.2 = (bf16[16,32,80]{2,1,0:T(8,128)(2,1)S(1)}, bf16[16,32,80]{2,1,0:T(8,128)(2,1)}, u32[]{:S(2)}) copy-start(bf16[16,32,80]{2,1,0:T(8,128)(2,1)} %param.12) | copy-start | bytes 245764
  3.2 29.3 %copy-start.7 = (bf16[320,80]{0,1:T(8,128)(2,1)S(1)}, bf16[320,80]{0,1:T(8,128)(2,1)}, u32[]{:S(2)}) copy-start(bf16[320,80]{0,1:T(8,128)(2,1)} %param.16) | copy-start | bytes 153604
  3.2 29.3 %copy-start.8 = (f32[80]{0:T(128)S(1)}, f32[80]{0:T(128)}, u32[]{:S(2)}) copy-start(f32[80]{0:T(128)} %param.17) | copy-start | bytes 964
  3.2 29.3 %copy-start.9 = (f32[80]{0:T(128)S(1)}, f32[80]{0:T(128)}, u32[]{:S(2)}) copy-start(f32[80]{0:T(128)} %param.19) | copy-start | bytes 964
  3.2 37.0 %copy-start = (bf16[80,3,3,1280]{3,0,2,1:T(8,128)(2,1)S(1)}, bf16[80,3,3,1280]{3,0,2,1:T(8,128)(2,1)}, u32[]{:S(2)}) copy-start(bf16[80,3,3,1280]{3,0,2,1:T(8,128)(2,1)} %param.15) | copy-start | bytes 5529604
  3.2 17.1 %collective-permute-start = (bf16[720,640]{1,0:T(8,128)(2,1)}, bf16[720,640]{1,0:T(8,128)(2,1)}, u32[]{:S(2)}, u32[]{:S(2)}) collective-permute-start(bf16[720,640]{1,0:T(8,128)(2,1)} %get-tuple-element.27), channel_id=1, source_target_pairs={{256,0},{259,1},{258,2},{257,3},{260,4},{263,5},{262,6},{261,7},{2... | collective-permute-start | bytes 2764808 | tf_op jit(solution)/shard_map/ppermute | solution.py:71
  7.3 7.6 %collective-permute-start.1 = (f32[80,128]{1,0:T(8,128)S(1)}, f32[80,128]{1,0:T(8,128)S(1)}, u32[]{:S(2)}, u32[]{:S(2)}) collective-permute-start(f32[80,128]{1,0:T(8,128)S(1)} %get-tuple-element.29.own_ref), channel_id=1, source_target_pairs={{0,1},{1,0},{2,3},{3,2},{4,5},{5,4},{6,7},{7,6},{8,9},{9,8},{10,11... | collective-permute-start | bytes 122888 | tf_op jit(solution)/shard_map/ppermute | solution.py:51
  16.0 24.2 %all-to-all-start = ((bf16[16,80,256]{2,1,0:T(8,128)(2,1)}), bf16[16,80,256]{2,1,0:T(8,128)(2,1)S(1)}, u32[]{:S(2)}, u32[]{:S(2)}) async-start(bf16[16,80,256]{2,1,0:T(8,128)(2,1)} %shard_map.119), calls=%async_computation | async-start | bytes 1310720 | tf_op jit(solution)/shard_map/all_to_all | solution.py:414
  20.4 19.8 %collective-permute-start.2 = (bf16[720,640]{1,0:T(8,128)(2,1)}, bf16[720,640]{1,0:T(8,128)(2,1)}, u32[]{:S(2)}, u32[]{:S(2)}) collective-permute-start(bf16[720,640]{1,0:T(8,128)(2,1)} %collective-permute-done.refs_0_), channel_id=1, source_target_pairs={{0,1},{1,0},{2,3},{3,2},{4,5},{5,4},{6,7},{7,6},{8,9},{9,8},{10,11... | collective-permute-start | bytes 2764808 | tf_op jit(solution)/shard_map/ppermute | solution.py:51
  29.1 45.2 %collective-permute-start.5 = (bf16[720,1280]{1,0:T(8,128)(2,1)}, bf16[720,1280]{1,0:T(8,128)(2,1)}, u32[]{:S(2)}, u32[]{:S(2)}) collective-permute-start(bf16[720,1280]{1,0:T(8,128)(2,1)} %bitcast.24), channel_id=1, source_target_pairs={{258,0},{259,1},{256,2},{257,3},{262,4},{263,5},{260,6},{261,7},{2... | collective-permute-start | bytes 5529608 | tf_op jit(solution)/shard_map/ppermute | solution.py:71
  32.7 7.5 %collective-permute-start.3 = (f32[80,384]{1,0:T(8,128)S(1)}, f32[80,384]{1,0:T(8,128)S(1)}, u32[]{:S(2)}, u32[]{:S(2)}) collective-permute-start(f32[80,384]{1,0:T(8,128)S(1)} %shard_map.120), channel_id=1, source_target_pairs={{0,256},{32,288},{64,320},{96,352},{128,384},{160,416},{192,448},{... | collective-permute-start | bytes 368648 | tf_op jit(solution)/shard_map/ppermute | solution.py:56
  43.4 14.0 %copy-start.3 = (bf16[64,1280]{1,0:T(8,128)(2,1)S(1)}, bf16[64,1280]{1,0:T(8,128)(2,1)}, u32[]{:S(2)}) copy-start(bf16[64,1280]{1,0:T(8,128)(2,1)} %value_ref.1) | copy-start | bytes 491524
  43.4 14.0 %copy-start.4 = (bf16[64,1280]{1,0:T(8,128)(2,1)S(1)}, bf16[64,1280]{1,0:T(8,128)(2,1)}, u32[]{:S(2)}) copy-start(bf16[64,1280]{1,0:T(8,128)(2,1)} %key_ref.1) | copy-start | bytes 491524
  43.4 14.0 %copy-start.5 = (bf16[64,1280]{1,0:T(8,128)(2,1)S(1)}, bf16[64,1280]{1,0:T(8,128)(2,1)}, u32[]{:S(2)}) copy-start(bf16[64,1280]{1,0:T(8,128)(2,1)} %query_ref.1) | copy-start | bytes 491524
  43.4 14.0 %copy-start.6 = (bf16[80,1024]{1,0:T(8,128)(2,1)S(1)}, bf16[80,1024]{1,0:T(8,128)(2,1)}, u32[]{:S(2)}) copy-start(bf16[80,1024]{1,0:T(8,128)(2,1)} %weight_ref.1) | copy-start | bytes 491524
  53.4 24.8 %all-to-all-start.2 = ((bf16[8,2,80,256]{3,2,1,0:T(8,128)(2,1)}), bf16[8,2,80,256]{3,2,1,0:T(8,128)(2,1)S(1)}, u32[]{:S(2)}, u32[]{:S(2)}) async-start(bf16[8,2,80,256]{3,2,1,0:T(8,128)(2,1)} %shard_map.122), calls=%async_computation.2 | async-start | bytes 1310720 | tf_op jit(solution)/shard_map/all_to_all | solution.py:87
  57.5 33.3 %collective-permute-start.4 = (bf16[272,1280]{1,0:T(8,128)(2,1)S(1)}, bf16[272,1280]{1,0:T(8,128)(2,1)S(1)}, u32[]{:S(2)}, u32[]{:S(2)}) collective-permute-start(bf16[272,1280]{1,0:T(8,128)(2,1)S(1)} %fusion.1), channel_id=1, source_target_pairs={{258,0},{259,1},{256,2},{257,3},{262,4},{263,5},{260,6},{261,7},{2... | collective-permute-start | bytes 2088968 | tf_op jit(solution)/shard_map/ppermute | solution.py:71
  147.9 4.7 %collective-permute-start.6 = (bf16[80,256]{1,0:T(8,128)(2,1)S(1)}, bf16[80,256]{1,0:T(8,128)(2,1)S(1)}, u32[]{:S(2)}, u32[]{:S(2)}) collective-permute-start(bf16[80,256]{1,0:T(8,128)(2,1)S(1)} %get-tuple-element.48), channel_id=1, source_target_pairs={{0,256},{32,288},{64,320},{96,352},{128,384},{160,416},{192,448},{... | collective-permute-start | bytes 122888 | tf_op jit(solution)/shard_map/ppermute | solution.py:56

commit v9 on v8

--- a/solution.py
+++ b/solution.py
@@ -192,25 +192,29 @@
     return held_ref[...]
 
 
-def both(own, gots, whole_ref):
-    mine = jnp.dot(own, whole_ref[...], preferred_element_type=F32)
-    depth = gots[0].shape[1]
-    if len(gots) == 1:
-        return mine, jnp.dot(gots[0], whole_ref[...], preferred_element_type=F32)
+def both(own_ref, halves, whole_ref):
+    mine = jnp.dot(own_ref[...], whole_ref[...], preferred_element_type=F32)
     _, core, _ = spot()
-    near = whole_ref[pl.ds(pl.multiple_of(core * depth, 128), depth), :]
-    far = whole_ref[pl.ds(pl.multiple_of((1 - core) * depth, 128), depth), :]
-    theirs = jnp.dot(gots[0], near, preferred_element_type=F32)
-    return mine, theirs + jnp.dot(gots[1], far, preferred_element_type=F32)
+    theirs = 0.0
+    for half, index in zip(halves, (core, 1 - core)):
+        got = arrived(*half)
+        depth = got.shape[1]
+        rows = pl.ds(pl.multiple_of(index * depth, 128), depth)
+        theirs = theirs + jnp.dot(got, whole_ref[rows, :], preferred_element_type=F32)
+    return mine, theirs
+
+
+def pair(own, got, whole_ref):
+    return [jnp.dot(weight, whole_ref[...], preferred_element_type=F32) for weight in (own, got)]
 
 
 def conv_kernel(own_ref, *refs, gots, copied):
     got_refs, refs = refs[:gots], refs[gots:]
-    full_ref, mail_ref, *base_refs, part_ref, note_ref, whole_ref = refs[: len(refs) - 3 * copied]
-    if copied:
-        weights = list(zip((own_ref, got_refs[0]), refs[-3:-1], (refs[-1].at[0], refs[-1].at[1])))
-        for ref, held_ref, sem in weights:
-            pltpu.make_async_copy(ref, held_ref, sem).start()
+    full_ref, mail_ref, *base_refs, part_ref, note_ref, whole_ref = refs[:-3]
+    fetched = ((own_ref,) if copied else ()) + tuple(got_refs)
+    weights = list(zip(fetched, refs[-3:-1], (refs[-1].at[0], refs[-1].at[1])))
+    for ref, held_ref, sem in weights:
+        pltpu.make_async_copy(ref, held_ref, sem).start()
     _, count, tokens = part_ref.shape
     side, core, quarter = spot()
     token = lanes((count, tokens))
@@ -222,7 +226,7 @@
     if copied:
         taps = [jnp.dot(arrived(*each), whole_ref[...], preferred_element_type=F32) for each in weights]
     else:
-        taps = both(own_ref[...], [ref[...] for ref in got_refs], whole_ref)
+        taps = both(own_ref, weights, whole_ref)
     if len(base_refs) == 2:
         bases = time_of(*base_refs), mail_ref[:, tokens : tokens + 1]
     else:
@@ -326,7 +330,7 @@
     for index, ref in enumerate((query_ref, key_ref, value_ref)):
         stack_ref[index * inner : (index + 1) * inner] = ref[...]
     gather_into(full_ref, whole_ref)
-    mixed = both(stack_ref[...], [got_ref[: 3 * inner]], whole_ref)
+    mixed = pair(stack_ref[...], got_ref[: 3 * inner], whole_ref)
     for which in range(2):
         here = side if which == 0 else 1 - side
         q_ref[here] = mixed[which][:inner].astype(BF16)
@@ -353,7 +357,7 @@
     count, depth = weight_ref.shape
     side, _, _ = spot()
     gather_into(full_ref, whole_ref)
-    mine, theirs = both(weight_ref[...], [got_ref[at : at + count, :depth]], whole_ref)
+    mine, theirs = pair(weight_ref[...], got_ref[at : at + count, :depth], whole_ref)
     keep_ref[...] = (hidden_ref[side] + mine).astype(BF16)
     send_ref[...] = (hidden_ref[1 - side] + theirs).astype(BF16)
 
@@ -422,15 +426,18 @@
     )
     mail = crossed(mail)
     got_b = from_beside(after(own_b, spread_a))
+    *late, late_out = [after(weight, spread_a) for weight in (w_query, w_key, w_value, w_out)]
+    late.append(jnp.pad(late_out, ((0, 0), (0, C - w_out.shape[1]))))
+    got_c = from_beside(jnp.concatenate(late, axis=0))
     other_a = swapped(after(got_a, spread_a))
 
     def conv(full, own, gots, *bases, copied=False):
-        held = [pltpu.VMEM(own.shape, BF16)] * 2 + [pltpu.SemaphoreType.DMA((2,))]
+        held = [pltpu.VMEM(gots[0].shape, BF16)] * 2 + [pltpu.SemaphoreType.DMA((2,))]
         return call(
-            functools.partial(conv_kernel, gots=len(gots), copied=int(copied)),
+            functools.partial(conv_kernel, gots=len(gots), copied=copied),
             [field, note],
-            [FAR if copied else VM] * (1 + len(gots)) + [VM] * (2 + len(bases)),
-            [whole] + held * copied,
+            [FAR if copied else VM] + [FAR] * len(gots) + [VM] * (2 + len(bases)),
+            [whole] + held,
             limit=CONV_LIMIT if copied else 20 * 2**20,
         )(own, *gots, full, mail, *bases)
 
@@ -443,10 +450,8 @@
     notes_a = image_collect(note_a)
     (spread_b,) = finish(part_a, notes_a, gain_b, True, 1, [active])
     full_b = column_collect(spread_b)
-    *late, late_out = [after(weight, spread_b) for weight in (w_query, w_key, w_value, w_out)]
-    late.append(jnp.pad(late_out, ((0, 0), (0, C - w_out.shape[1]))))
-    got_c = from_beside(jnp.concatenate(late, axis=0))
-    part_b, note_b = conv(full_b, own_b, [got_b], flat, copied=True)
+    (whole_b,) = call(gather_into, [((C, share), BF16)], [VM])(full_b)
+    part_b, note_b = conv(whole_b.reshape(chs, count, share), own_b, [got_b], flat, copied=True)
     notes_b = image_collect(note_b)
     spread_c, hidden_b = finish(part_b, notes_b, gain_c, False, 2, [active, field])
     features = column_collect(after(spread_c, got_c))

time: 154 us -> 155 us (level)
    all_to_all x1, waiting for transfers between devices: 3.95 us -> 17.9 us  [column_collect(): lax.all_to_all(spread, 'ch', 0, 0, tiled=True, axis_index_groups=groups)]
    ppermute x3, waiting for transfers between devices: 14 us -> 0.01 us  [from_beside(): return lax.ppermute(value, ('ch', 'row'), pairs)]
    pallas_call x2 -> x3, Pallas kernels: 7.18 us -> 7.96 us  [the longest x2 7.92 us: conv(): call(functools.partial(conv_kernel, gots=len(gots), copied=copied), [fiel...]
  transfers between devices with their start and end apart: 9 -> 9, of which waited for: 5 -> 4; matrix products, arithmetic and copies ran while one was open for 1% -> 1% of each run, Pallas kernels for 8% -> 8%
where the time goes in v9:
time: 155 us; the launch traced here: 154 us
  blocking collectives  70 us (45%)
  starting transfers between devices  36.5 us (24%)
  waiting for transfers between devices  27 us (17%)
  Pallas kernels  17.9 us (12%)
    all_to_all x2, blocking collectives, column_collect(): lax.all_to_all(spread, 'ch', 0, 0, tiled=True, axis_index_groups=groups)  43.5 us
    all_to_all x3, blocking collectives, image_collect(): lax.all_to_all(spread, ('ch', 'row'), 0, 0, tiled=True, axis_index_groups...  26.5 us
    all_to_all x1, waiting for transfers between devices, column_collect(): lax.all_to_all(spread, 'ch', 0, 0, tiled=True, axis_index_groups=groups)  17.9 us
    ppermute x2, starting transfers between devices, swapped(): return lax.ppermute(value, ('ch', 'row'), core_pairs())  15.4 us
    ppermute x3, starting transfers between devices, from_beside(): return lax.ppermute(value, ('ch', 'row'), pairs)  8.73 us
    ppermute x2, waiting for transfers between devices, crossed(): lax.ppermute(value, 'ch', [(k, (k + chs // 2) % chs) for k in range(chs)])  8.2 us
    pallas_call x2, Pallas kernels, conv(): call(functools.partial(conv_kernel, gots=len(gots), copied=copied), [fiel...  7.92 us
    all_to_all x1, starting transfers between devices, body(): full = lax.all_to_all(spread_a, 'ch', 0, 0, tiled=True)  4.33 us
  transfers between devices with their start and end apart: 9, of which 4 were waited for; matrix products, arithmetic and copies ran while one was open for 1% of the time, Pallas kernels for 8%

profile of v9, /device:TPU:1, one launch (start us, length us, event | category | flops | bytes accessed | tf_op | source)
XLA Modules:
  0.0 154.2 jit_solution(16415305810510765464)
XLA Ops:
  0.0 0.9 copy-done.1
  0.9 2.2 %shard_map.118 = (f32[80,512]{1,0:T(8,128)S(1)}, f32[80,128]{1,0:T(8,128)S(1)}, bf16[720,640]{1,0:T(8,128)(2,1)}) custom-call(bf16[512,80]{1,0:T(8,128)(2,1)S(1)} %bitcast.16, bf16[720,1280]{1,0:T(8,128)(2,1)} %bitcast.13), custom_call_target="tpu_custom_call" | custom-call | tf_op jit(solution)/shard_map/pallas_call | solution.py:407
  3.2 4.1 %collective-permute-start.3 = (bf16[720,640]{1,0:T(8,128)(2,1)}, bf16[720,640]{1,0:T(8,128)(2,1)}, u32[]{:S(2)}, u32[]{:S(2)}) collective-permute-start(bf16[720,640]{1,0:T(8,128)(2,1)} %get-tuple-element.34), channel_id=1, source_target_pairs={{256,0},{259,1},{258,2},{257,3},{260,4},{263,5},{262,6},{261,7},{2... | collective-permute-start | bytes 2764808 | tf_op jit(solution)/shard_map/ppermute | solution.py:71
  7.3 6.7 %collective-permute-start = (f32[80,128]{1,0:T(8,128)S(1)}, f32[80,128]{1,0:T(8,128)S(1)}, u32[]{:S(2)}, u32[]{:S(2)}) collective-permute-start(f32[80,128]{1,0:T(8,128)S(1)} %get-tuple-element.28.own_ref), channel_id=1, source_target_pairs={{0,1},{1,0},{2,3},{3,2},{4,5},{5,4},{6,7},{7,6},{8,9},{9,8},{10,11... | collective-permute-start | bytes 122888 | tf_op jit(solution)/shard_map/ppermute | solution.py:51
  14.0 0.8 collective-permute-done.peer_ref
  14.9 1.1 shard_map.119
  16.0 4.3 %all-to-all-start = ((bf16[16,80,256]{2,1,0:T(8,128)(2,1)}), bf16[16,80,256]{2,1,0:T(8,128)(2,1)S(1)}, u32[]{:S(2)}, u32[]{:S(2)}) async-start(bf16[16,80,256]{2,1,0:T(8,128)(2,1)} %shard_map.119), calls=%async_computation | async-start | bytes 1310720 | tf_op jit(solution)/shard_map/all_to_all | solution.py:418
  20.4 8.7 %collective-permute-start.4 = (bf16[720,640]{1,0:T(8,128)(2,1)}, bf16[720,640]{1,0:T(8,128)(2,1)}, u32[]{:S(2)}, u32[]{:S(2)}) collective-permute-start(bf16[720,640]{1,0:T(8,128)(2,1)} %collective-permute-done.3.refs_0_), channel_id=1, source_target_pairs={{0,1},{1,0},{2,3},{3,2},{4,5},{5,4},{6,7},{7,6},{8,9},{9,8},{10,11... | collective-permute-start | bytes 2764808 | tf_op jit(solution)/shard_map/ppermute | solution.py:51
  29.1 1.9 %collective-permute-start.2 = (bf16[720,1280]{1,0:T(8,128)(2,1)}, bf16[720,1280]{1,0:T(8,128)(2,1)}, u32[]{:S(2)}, u32[]{:S(2)}) collective-permute-start(bf16[720,1280]{1,0:T(8,128)(2,1)} %bitcast.26), channel_id=1, source_target_pairs={{258,0},{259,1},{256,2},{257,3},{262,4},{263,5},{260,6},{261,7},{2... | collective-permute-start | bytes 5529608 | tf_op jit(solution)/shard_map/ppermute | solution.py:71
  31.0 0.6 fusion.2
  32.4 0.1 pad_maximum_fusion.sinus_ref.refs_5_
  32.5 0.2 shard_map.120
  32.7 1.9 %collective-permute-start.5 = (f32[80,384]{1,0:T(8,128)S(1)}, f32[80,384]{1,0:T(8,128)S(1)}, u32[]{:S(2)}, u32[]{:S(2)}) collective-permute-start(f32[80,384]{1,0:T(8,128)S(1)} %shard_map.120), channel_id=1, source_target_pairs={{0,256},{32,288},{64,320},{96,352},{128,384},{160,416},{192,448},{... | collective-permute-start | bytes 368648 | tf_op jit(solution)/shard_map/ppermute | solution.py:56
  34.7 5.5 %collective-permute-done.5.refs_3_.mail_ref.refs_2_ = f32[80,384]{1,0:T(8,128)S(1)} collective-permute-done((f32[80,384]{1,0:T(8,128)S(1)}, f32[80,384]{1,0:T(8,128)S(1)}, u32[]{:S(2)}, u32[]{:S(2)}) %collective-permute-start.5) | collective-permute-done | bytes 122912 | tf_op jit(solution)/shard_map/ppermute | solution.py:56
  40.2 3.9 %shard_map.121 = (f32[2,80,256]{2,1,0:T(8,128)S(1)}, bf16[4,176,128]{2,1,0:T(8,128)(2,1)S(1)}) custom-call(bf16[720,1280]{1,0:T(8,128)(2,1)S(1)} %bitcast.14, bf16[720,640]{1,0:T(8,128)(2,1)} %collective-permute-done.3.refs_0_, bf16[720,640]{1,0:T(8,128)(2,1)} %collective-permute-done.4.refs_1_, bf16[16,80,256]{2,1,0:T(8,128)(2,1)S(1)} %all-to-all-done.refs_2_, ...), custom_call_target="tpu_custom_call" | custom-call | tf_op jit(solution)/shard_map/pallas_call | solution.py:436
  44.2 8.0 %all_to_all.35.notes_ref = bf16[4,176,128]{2,1,0:T(8,128)(2,1)S(1)} all-to-all(bf16[4,176,128]{2,1,0:T(8,128)(2,1)S(1)} %get-tuple-element.39), channel_id=1, replica_groups={{0,256,257,1},{32,288,289,33},{64,320,321,65},{96,352,353,97},{128,384,..., dimensions={0} | all-to-all | bytes 360448 | tf_op jit(solution)/shard_map/all_to_all | solution.py:97
  52.2 2.0 %shard_map.122 = bf16[8,2,80,256]{3,2,1,0:T(8,128)(2,1)} custom-call(f32[2,80,256]{2,1,0:T(8,128)S(1)} %get-tuple-element.38.part_ref, bf16[4,176,128]{2,1,0:T(8,128)(2,1)S(1)} %all_to_all.35.notes_ref, f32[1,80]{1,0:T(1,128)S(1)} %bitcast.22, f32[80,384]{1,0:T(8,128)S(1)} %collective-permute-done.5.refs_3_.mail_ref.refs_2_), custom_call_target="tpu_custom_call" | custom-call | tf_op jit(solution)/shard_map/pallas_call | solution.py:445
  54.1 4.0 %all-to-all-start.2 = ((bf16[8,2,80,256]{3,2,1,0:T(8,128)(2,1)}), bf16[8,2,80,256]{3,2,1,0:T(8,128)(2,1)S(1)}, u32[]{:S(2)}, u32[]{:S(2)}) async-start(bf16[8,2,80,256]{3,2,1,0:T(8,128)(2,1)} %shard_map.122), calls=%async_computation.2 | async-start | bytes 1310720 | tf_op jit(solution)/shard_map/all_to_all | solution.py:87
  58.2 2.7 %collective-permute-start.1 = (bf16[272,1280]{1,0:T(8,128)(2,1)S(1)}, bf16[272,1280]{1,0:T(8,128)(2,1)S(1)}, u32[]{:S(2)}, u32[]{:S(2)}) collective-permute-start(bf16[272,1280]{1,0:T(8,128)(2,1)S(1)} %fusion.1), channel_id=1, source_target_pairs={{258,0},{259,1},{256,2},{257,3},{262,4},{263,5},{260,6},{261,7},{2... | collective-permute-start | bytes 2088968 | tf_op jit(solution)/shard_map/ppermute | solution.py:71
  61.0 17.9 %all-to-all-done.2.full_ref = bf16[8,2,80,256]{3,2,1,0:T(8,128)(2,1)S(1)} async-done(((bf16[8,2,80,256]{3,2,1,0:T(8,128)(2,1)}), bf16[8,2,80,256]{3,2,1,0:T(8,128)(2,1)S(1)}, u32[]{:S(2)}, u32[]{:S(2)}) %all-to-all-start.2) | async-done | bytes 655392 | tf_op jit(solution)/shard_map/all_to_all | solution.py:87
  79.0 4.0 %shard_map.124 = (f32[2,80,256]{2,1,0:T(8,128)S(1)}, bf16[4,176,128]{2,1,0:T(8,128)(2,1)S(1)}) custom-call(bf16[720,1280]{1,0:T(8,128)(2,1)} %bitcast.27, bf16[720,1280]{1,0:T(8,128)(2,1)} %collective-permute-done.2.refs_0_, bf16[16,80,256]{2,1,0:T(8,128)(2,1)S(1)} %bitcast.15, f32[80,384]{1,0:T(8,128)S(1)} %collective-permute-done.5.refs_3_.mail_ref.refs_2_, ...), custom_call_target="tpu_custom_call" | custom-call | tf_op jit(solution)/shard_map/pallas_call | solution.py:436
  83.0 7.4 %all_to_all.36.notes_ref = bf16[4,176,128]{2,1,0:T(8,128)(2,1)S(1)} all-to-all(bf16[4,176,128]{2,1,0:T(8,128)(2,1)S(1)} %get-tuple-element.41), channel_id=1, replica_groups={{0,256,257,1},{32,288,289,33},{64,320,321,65},{96,352,353,97},{128,384,..., dimensions={0} | all-to-all | bytes 360448 | tf_op jit(solution)/shard_map/all_to_all | solution.py:97
  90.4 1.1 shard_map.125
  91.6 23.1 %all_to_all.37.full_ref = bf16[8,2,80,256]{3,2,1,0:T(8,128)(2,1)S(1)} all-to-all(bf16[8,2,80,256]{3,2,1,0:T(8,128)(2,1)S(1)} %get-tuple-element.43), channel_id=1, replica_groups={{0,32,64,96,128,160,192,224},{256,288,320,352,384,416,448,480},{1,33,65..., dimensions={0} | all-to-all | bytes 1310720 | tf_op jit(solution)/shard_map/all_to_all | solution.py:87
  114.7 0.4 shard_map.126
  115.2 11.0 %all_to_all.38.pairs_ref = bf16[4,2,128,256]{3,2,1,0:T(8,128)(2,1)S(1)} all-to-all(bf16[4,2,128,256]{3,2,1,0:T(8,128)(2,1)S(1)} %get-tuple-element.45), channel_id=1, replica_groups={{0,256,257,1},{32,288,289,33},{64,320,321,65},{96,352,353,97},{128,384,..., dimensions={0} | all-to-all | bytes 1048576 | tf_op jit(solution)/shard_map/all_to_all | solution.py:97
  126.2 1.8 %shard_map.127 = bf16[8,2,64,256]{3,2,1,0:T(8,128)(2,1)S(1)} custom-call(bf16[2,64,256]{2,1,0:T(8,128)(2,1)S(1)} %get-tuple-element.44.q_ref, bf16[4,2,128,256]{3,2,1,0:T(8,128)(2,1)S(1)} %all_to_all.38.pairs_ref), custom_call_target="tpu_custom_call" | custom-call | tf_op jit(solution)/shard_map/pallas_call | solution.py:466
  128.0 20.4 %all_to_all.39.full_ref = bf16[8,2,64,256]{3,2,1,0:T(8,128)(2,1)S(1)} all-to-all(bf16[8,2,64,256]{3,2,1,0:T(8,128)(2,1)S(1)} %shard_map.127), channel_id=1, replica_groups={{0,32,64,96,128,160,192,224},{256,288,320,352,384,416,448,480},{1,33,65..., dimensions={0} | all-to-all | bytes 1048576 | tf_op jit(solution)/shard_map/all_to_all | solution.py:87
  148.4 0.3 shard_map.128
  148.7 2.1 %collective-permute-start.6 = (bf16[80,256]{1,0:T(8,128)(2,1)S(1)}, bf16[80,256]{1,0:T(8,128)(2,1)S(1)}, u32[]{:S(2)}, u32[]{:S(2)}) collective-permute-start(bf16[80,256]{1,0:T(8,128)(2,1)S(1)} %get-tuple-element.48), channel_id=1, source_target_pairs={{0,256},{32,288},{64,320},{96,352},{128,384},{160,416},{192,448},{... | collective-permute-start | bytes 122888 | tf_op jit(solution)/shard_map/ppermute | solution.py:56
  150.7 2.7 %collective-permute-done.6.peer_ref = bf16[80,256]{1,0:T(8,128)(2,1)S(1)} collective-permute-done((bf16[80,256]{1,0:T(8,128)(2,1)S(1)}, bf16[80,256]{1,0:T(8,128)(2,1)S(1)}, u32[]{:S(2)}, u32[]{:S(2)}) %collective-permute-start.6) | collective-permute-done | bytes 40992 | tf_op jit(solution)/shard_map/ppermute | solution.py:56
  153.4 0.8 shard_map.129
  (33 shorter events, 0.2 us)
Async XLA Ops:
  0.0 14.9 %copy-start.10 = (f32[80]{0:T(128)S(1)}, f32[80]{0:T(128)}, u32[]{:S(2)}) copy-start(f32[80]{0:T(128)} %param.14) | copy-start | bytes 964
  0.0 0.9 copy-start.1
  3.2 27.9 %copy-start.11 = (s32[16]{0:T(128)S(1)}, s32[16]{0:T(128)}, u32[]{:S(2)}) copy-start(s32[16]{0:T(128)} %param.13) | copy-start | bytes 196
  3.2 29.3 %copy-start.2 = (bf16[16,32,80]{2,1,0:T(8,128)(2,1)S(1)}, bf16[16,32,80]{2,1,0:T(8,128)(2,1)}, u32[]{:S(2)}) copy-start(bf16[16,32,80]{2,1,0:T(8,128)(2,1)} %param.12) | copy-start | bytes 245764
  3.2 29.3 %copy-start.7 = (bf16[320,80]{0,1:T(8,128)(2,1)S(1)}, bf16[320,80]{0,1:T(8,128)(2,1)}, u32[]{:S(2)}) copy-start(bf16[320,80]{0,1:T(8,128)(2,1)} %param.16) | copy-start | bytes 153604
  3.2 29.3 %copy-start.8 = (f32[80]{0:T(128)S(1)}, f32[80]{0:T(128)}, u32[]{:S(2)}) copy-start(f32[80]{0:T(128)} %param.17) | copy-start | bytes 964
  3.2 29.3 %copy-start.9 = (f32[80]{0:T(128)S(1)}, f32[80]{0:T(128)}, u32[]{:S(2)}) copy-start(f32[80]{0:T(128)} %param.19) | copy-start | bytes 964
  3.2 37.0 %copy-start = (bf16[80,3,3,1280]{3,0,2,1:T(8,128)(2,1)S(1)}, bf16[80,3,3,1280]{3,0,2,1:T(8,128)(2,1)}, u32[]{:S(2)}) copy-start(bf16[80,3,3,1280]{3,0,2,1:T(8,128)(2,1)} %param.15) | copy-start | bytes 5529604
  3.2 17.1 %collective-permute-start.3 = (bf16[720,640]{1,0:T(8,128)(2,1)}, bf16[720,640]{1,0:T(8,128)(2,1)}, u32[]{:S(2)}, u32[]{:S(2)}) collective-permute-start(bf16[720,640]{1,0:T(8,128)(2,1)} %get-tuple-element.34), channel_id=1, source_target_pairs={{256,0},{259,1},{258,2},{257,3},{260,4},{263,5},{262,6},{261,7},{2... | collective-permute-start | bytes 2764808 | tf_op jit(solution)/shard_map/ppermute | solution.py:71
  7.3 7.6 %collective-permute-start = (f32[80,128]{1,0:T(8,128)S(1)}, f32[80,128]{1,0:T(8,128)S(1)}, u32[]{:S(2)}, u32[]{:S(2)}) collective-permute-start(f32[80,128]{1,0:T(8,128)S(1)} %get-tuple-element.28.own_ref), channel_id=1, source_target_pairs={{0,1},{1,0},{2,3},{3,2},{4,5},{5,4},{6,7},{7,6},{8,9},{9,8},{10,11... | collective-permute-start | bytes 122888 | tf_op jit(solution)/shard_map/ppermute | solution.py:51
  16.0 24.2 %all-to-all-start = ((bf16[16,80,256]{2,1,0:T(8,128)(2,1)}), bf16[16,80,256]{2,1,0:T(8,128)(2,1)S(1)}, u32[]{:S(2)}, u32[]{:S(2)}) async-start(bf16[16,80,256]{2,1,0:T(8,128)(2,1)} %shard_map.119), calls=%async_computation | async-start | bytes 1310720 | tf_op jit(solution)/shard_map/all_to_all | solution.py:418
  20.4 19.8 %collective-permute-start.4 = (bf16[720,640]{1,0:T(8,128)(2,1)}, bf16[720,640]{1,0:T(8,128)(2,1)}, u32[]{:S(2)}, u32[]{:S(2)}) collective-permute-start(bf16[720,640]{1,0:T(8,128)(2,1)} %collective-permute-done.3.refs_0_), channel_id=1, source_target_pairs={{0,1},{1,0},{2,3},{3,2},{4,5},{5,4},{6,7},{7,6},{8,9},{9,8},{10,11... | collective-permute-start | bytes 2764808 | tf_op jit(solution)/shard_map/ppermute | solution.py:51
  29.1 49.9 %collective-permute-start.2 = (bf16[720,1280]{1,0:T(8,128)(2,1)}, bf16[720,1280]{1,0:T(8,128)(2,1)}, u32[]{:S(2)}, u32[]{:S(2)}) collective-permute-start(bf16[720,1280]{1,0:T(8,128)(2,1)} %bitcast.26), channel_id=1, source_target_pairs={{258,0},{259,1},{256,2},{257,3},{262,4},{263,5},{260,6},{261,7},{2... | collective-permute-start | bytes 5529608 | tf_op jit(solution)/shard_map/ppermute | solution.py:71
  32.7 7.5 %collective-permute-start.5 = (f32[80,384]{1,0:T(8,128)S(1)}, f32[80,384]{1,0:T(8,128)S(1)}, u32[]{:S(2)}, u32[]{:S(2)}) collective-permute-start(f32[80,384]{1,0:T(8,128)S(1)} %shard_map.120), channel_id=1, source_target_pairs={{0,256},{32,288},{64,320},{96,352},{128,384},{160,416},{192,448},{... | collective-permute-start | bytes 368648 | tf_op jit(solution)/shard_map/ppermute | solution.py:56
  44.1 14.0 %copy-start.3 = (bf16[64,1280]{1,0:T(8,128)(2,1)S(1)}, bf16[64,1280]{1,0:T(8,128)(2,1)}, u32[]{:S(2)}) copy-start(bf16[64,1280]{1,0:T(8,128)(2,1)} %value_ref.1) | copy-start | bytes 491524
  44.1 14.0 %copy-start.4 = (bf16[64,1280]{1,0:T(8,128)(2,1)S(1)}, bf16[64,1280]{1,0:T(8,128)(2,1)}, u32[]{:S(2)}) copy-start(bf16[64,1280]{1,0:T(8,128)(2,1)} %key_ref.1) | copy-start | bytes 491524
  44.1 14.0 %copy-start.5 = (bf16[64,1280]{1,0:T(8,128)(2,1)S(1)}, bf16[64,1280]{1,0:T(8,128)(2,1)}, u32[]{:S(2)}) copy-start(bf16[64,1280]{1,0:T(8,128)(2,1)} %query_ref.1) | copy-start | bytes 491524
  44.2 14.0 %copy-start.6 = (bf16[80,1024]{1,0:T(8,128)(2,1)S(1)}, bf16[80,1024]{1,0:T(8,128)(2,1)}, u32[]{:S(2)}) copy-start(bf16[80,1024]{1,0:T(8,128)(2,1)} %weight_ref.1) | copy-start | bytes 491524
  54.1 24.8 %all-to-all-start.2 = ((bf16[8,2,80,256]{3,2,1,0:T(8,128)(2,1)}), bf16[8,2,80,256]{3,2,1,0:T(8,128)(2,1)S(1)}, u32[]{:S(2)}, u32[]{:S(2)}) async-start(bf16[8,2,80,256]{3,2,1,0:T(8,128)(2,1)} %shard_map.122), calls=%async_computation.2 | async-start | bytes 1310720 | tf_op jit(solution)/shard_map/all_to_all | solution.py:87
  58.2 33.3 %collective-permute-start.1 = (bf16[272,1280]{1,0:T(8,128)(2,1)S(1)}, bf16[272,1280]{1,0:T(8,128)(2,1)S(1)}, u32[]{:S(2)}, u32[]{:S(2)}) collective-permute-start(bf16[272,1280]{1,0:T(8,128)(2,1)S(1)} %fusion.1), channel_id=1, source_target_pairs={{258,0},{259,1},{256,2},{257,3},{262,4},{263,5},{260,6},{261,7},{2... | collective-permute-start | bytes 2088968 | tf_op jit(solution)/shard_map/ppermute | solution.py:71
  148.7 4.7 %collective-permute-start.6 = (bf16[80,256]{1,0:T(8,128)(2,1)S(1)}, bf16[80,256]{1,0:T(8,128)(2,1)S(1)}, u32[]{:S(2)}, u32[]{:S(2)}) collective-permute-start(bf16[80,256]{1,0:T(8,128)(2,1)S(1)} %get-tuple-element.48), channel_id=1, source_target_pairs={{0,256},{32,288},{64,320},{96,352},{128,384},{160,416},{192,448},{... | collective-permute-start | bytes 122888 | tf_op jit(solution)/shard_map/ppermute | solution.py:56
